TPU v7x, 32 devices: a whole 2x2x4 slice. The times are simulated.
32 devices in a mesh: dp: 8 (over z, y), mp: 4 (over x, core).
Axes of the slice: x: 2, y: 2, z: 4, core: 2. Of those that a mesh axis runs over, the one named last changes fastest.
Arguments:
- wide_state: bfloat16 [16, 2, 768, 1024], P('dp', None, 'mp'), may hold values from -6 to 6
- encoder: bfloat16 [16, 512, 768], P('dp', 'mp'), may hold values from -6 to 6
- segments: int32 [16, 1024], P('dp'), may hold values from 0 to 15, never falling along the last dimension, each value on 1 to 512 neighbouring positions
- key_valid: int32 [16, 1024], P('dp'), may hold values from 0 to 1, as said below
- self_qkv: bfloat16 [3, 768, 768], P(None, 'mp'), may hold values from -0.21875 to 0.21875
- self_out: bfloat16 [768, 768], P('mp'), may hold values from -0.875 to 0.875
- cross_qkv: bfloat16 [3, 768, 768], P(None, 'mp'), may hold values from -0.21875 to 0.21875
- cross_out: bfloat16 [768, 768], P('mp'), may hold values from -0.625 to 0.625
- ffn_in: bfloat16 [2, 768, 3072], P(None, None, 'mp'), may hold values from -0.21875 to 0.21875
- ffn_out: bfloat16 [3072, 768], P('mp'), may hold values from -0.109375 to 0.109375
- norm_gains: float32 [3, 768], replicated, may hold values from 0.5 to 1.5
- predict: float32 [2, 2], replicated, may hold values from 0.1 to 1.9
- correct: float32 [2], replicated, may hold values from 0.1 to 1.9
- cotangent: bfloat16 [16, 2, 768, 1024], P('dp', None, 'mp'), may hold values from -6 to 6
Outputs:
- new_state: bfloat16 [16, 2, 768, 1024], P('dp', None, 'mp')
- grad_state: float32 [16, 2, 768, 1024], P('dp', None, 'mp')
- grad_encoder: float32 [16, 512, 768], P('dp', 'mp')
- grad_self_qkv: float32 [3, 768, 768], P(None, 'mp', 'dp')
- grad_self_out: float32 [768, 768], P('mp', 'dp')
- grad_cross_qkv: float32 [3, 768, 768], P(None, 'mp', 'dp')
- grad_cross_out: float32 [768, 768], P('mp', 'dp')
- grad_ffn_in: float32 [2, 768, 3072], P(None, 'dp', 'mp')
- grad_ffn_out: float32 [3072, 768], P('mp', 'dp')
- grad_norm_gains: float32 [3, 768], replicated
- grad_predict: float32 [2, 2], replicated
- grad_correct: float32 [2], replicated
Inputs may be any that keep to these rules, and one draw needn't show every extreme that they name: `segments`: within a row the numbers never fall; a document spans 1 to 512 positions. `key_valid`: in each row the ones come first, followed by 1 to 256 zeros.
All inputs are finite; a program needn't handle non-finite values.
Results may differ from a plain program's by a relative error of at most 0.02.
Values may be sent and summed in bfloat16 or wider, within the bound.
A program may use at most 256 MiB of HBM per device.

v0:
```python
import jax
import jax.numpy as jnp
from jax import lax
from jax.sharding import PartitionSpec as P

HEADS = 12
HEAD = 64


EPSILON = 1e-06
MASKED_SCORE = -1e30


def rms_norm(values, norm_gain):
    mean_sq = jnp.mean(values * values, axis=-1, keepdims=True)
    return values * lax.rsqrt(mean_sq + EPSILON) * norm_gain


def rms_back(values, norm_gain, incoming):
    unused_out, pullback = jax.vjp(rms_norm, values, norm_gain)
    return pullback(incoming)


def gated_unit(gate_pre, up_pre):
    return jax.nn.gelu(gate_pre, approximate=True) * up_pre


def head_split(matrix):
    return matrix.reshape(matrix.shape[0], matrix.shape[1], HEADS, HEAD)


def head_join(tensor):
    return tensor.reshape(tensor.shape[0], tensor.shape[1], HEADS * HEAD)


def self_mask(segments, key_valid, query_start, query_len, key_len):
    seg_query = lax.dynamic_slice_in_dim(segments, query_start, query_len, 1)
    live_key = key_valid > 0
    query_pos = query_start + jnp.arange(query_len, dtype=jnp.int32)
    key_pos = jnp.arange(key_len, dtype=jnp.int32)
    earlier = key_pos[None, None, :] <= query_pos[None, :, None]
    itself = key_pos[None, None, :] == query_pos[None, :, None]
    same_doc = seg_query[:, :, None] == segments[:, None, :]
    return same_doc & earlier & live_key[:, None, :] | itself


def scores_of(queries, key_rows, allowed):
    scores = jnp.einsum(
        "rqhd,rkhd->rhqk",
        head_split(queries),
        head_split(key_rows),
        preferred_element_type=jnp.float32,
    ) * HEAD ** (-0.5)
    if allowed is None:
        return scores
    return jnp.where(allowed[:, None], scores, MASKED_SCORE)


def attend(queries, key_rows, value_rows, allowed):
    scores = scores_of(queries, key_rows, allowed)
    top_score = jnp.max(scores, axis=-1, keepdims=True)
    exponent = jnp.exp(scores - top_score)
    row_total = jnp.sum(exponent, axis=-1, keepdims=True)
    attn_probs = (exponent / row_total).astype(jnp.bfloat16)
    mixed_heads = jnp.einsum(
        "rhqk,rkhd->rqhd", attn_probs, head_split(value_rows), preferred_element_type=jnp.float32
    )
    return (head_join(mixed_heads).astype(jnp.bfloat16), top_score + jnp.log(row_total))


def query_side_grads(queries, key_rows, value_rows, allowed, log_total, grad_mix):
    scores = scores_of(queries, key_rows, allowed)
    attn_probs = jnp.exp(scores - log_total)
    grad_heads = head_split(grad_mix)
    grad_probs = jnp.einsum(
        "rqhd,rkhd->rhqk", grad_heads, head_split(value_rows), preferred_element_type=jnp.float32
    )
    row_dot = jnp.sum(grad_probs * attn_probs, axis=-1, keepdims=True)
    grad_scores = (attn_probs * (grad_probs - row_dot)).astype(jnp.bfloat16)
    grad_query = head_join(
        jnp.einsum(
            "rhqk,rkhd->rqhd", grad_scores, head_split(key_rows), preferred_element_type=jnp.float32
        )
    ) * HEAD ** (-0.5)
    grad_key = head_join(
        jnp.einsum(
            "rhqk,rqhd->rkhd", grad_scores, head_split(queries), preferred_element_type=jnp.float32
        )
    ) * HEAD ** (-0.5)
    grad_value = head_join(
        jnp.einsum(
            "rhqk,rqhd->rkhd",
            attn_probs.astype(jnp.bfloat16),
            grad_heads,
            preferred_element_type=jnp.float32,
        )
    )
    return (grad_query, jnp.stack([grad_key, grad_value]), row_dot)


def shards(
    wide_state,
    encoder,
    segments,
    key_valid,
    self_qkv,
    self_out,
    cross_qkv,
    cross_out,
    ffn_in,
    ffn_out,
    norm_gains,
    predict,
    correct,
    cotangent,
):
    length = segments.shape[1]
    local_len = length // lax.axis_size("mp")
    offset = lax.axis_index("mp") * local_len
    state_f = jnp.transpose(wide_state.astype(jnp.float32), (0, 3, 1, 2))
    block_a = state_f[:, :, 0]
    block_b = state_f[:, :, 1]
    guess_a = predict[0, 0] * block_a + predict[0, 1] * block_b
    guess_b = predict[1, 0] * block_a + predict[1, 1] * block_b
    w_self, w_self_out, w_cross, w_cross_out = (
        lax.all_gather(self_qkv, "mp", axis=1, tiled=True),
        lax.all_gather(self_out, "mp", axis=0, tiled=True),
        lax.all_gather(cross_qkv, "mp", axis=1, tiled=True),
        lax.all_gather(cross_out, "mp", axis=0, tiled=True),
    )
    active = lax.all_to_all(
        guess_a.astype(jnp.bfloat16), "mp", split_axis=1, concat_axis=2, tiled=True
    )
    cross_kv = jnp.einsum(
        "rsd,cde->crse", encoder, w_cross[1:], preferred_element_type=jnp.float32
    ).astype(jnp.bfloat16)
    resid_a = active.astype(jnp.float32)
    normed_a = rms_norm(resid_a, norm_gains[0]).astype(jnp.bfloat16)
    self_proj = jnp.einsum(
        "rtd,cde->crte", normed_a, w_self, preferred_element_type=jnp.float32
    ).astype(jnp.bfloat16)
    queries = self_proj[0]
    all_kv, all_ckv = (
        lax.all_gather(self_proj[1:], "mp", axis=2, tiled=True),
        lax.all_gather(cross_kv, "mp", axis=2, tiled=True),
    )
    allowed = self_mask(segments, key_valid, offset, local_len, length)
    self_mix, self_log = attend(queries, all_kv[0], all_kv[1], allowed)
    attn_out = jnp.einsum("rtd,de->rte", self_mix, w_self_out, preferred_element_type=jnp.float32)
    resid_b = resid_a + attn_out
    normed_b = rms_norm(resid_b, norm_gains[1]).astype(jnp.bfloat16)
    cross_q = jnp.einsum(
        "rtd,de->rte", normed_b, w_cross[0], preferred_element_type=jnp.float32
    ).astype(jnp.bfloat16)
    cross_mix, cross_log = attend(cross_q, all_ckv[0], all_ckv[1], None)
    cross_res = jnp.einsum(
        "rtd,de->rte", cross_mix, w_cross_out, preferred_element_type=jnp.float32
    )
    resid_c = resid_b + cross_res
    normed_c = rms_norm(resid_c, norm_gains[2]).astype(jnp.bfloat16)
    all_normed = lax.all_gather(normed_c, "mp", axis=1, tiled=True)
    gate_up = jnp.einsum("rtd,cdf->crtf", all_normed, ffn_in, preferred_element_type=jnp.float32)
    hidden = gated_unit(gate_up[0], gate_up[1]).astype(jnp.bfloat16)
    ffn_part = jnp.einsum("rtf,fd->rtd", hidden, ffn_out, preferred_element_type=jnp.float32)
    ffn_res = lax.psum_scatter(
        ffn_part.astype(jnp.bfloat16), "mp", scatter_dimension=2, tiled=True
    ).astype(jnp.float32)
    branch_rows = (attn_out + cross_res).astype(jnp.bfloat16)
    branch_cols = lax.all_to_all(branch_rows, "mp", split_axis=2, concat_axis=1, tiled=True)
    branch_sum = branch_cols.astype(jnp.float32) + ffn_res
    new_rows = jnp.stack(
        [guess_a + correct[0] * branch_sum, guess_b + correct[1] * branch_sum], axis=2
    )
    new_state = jnp.transpose(new_rows, (0, 2, 3, 1)).astype(jnp.bfloat16)
    cot_f = jnp.transpose(cotangent.astype(jnp.float32), (0, 3, 1, 2))
    cot_a = cot_f[:, :, 0]
    cot_b = cot_f[:, :, 1]
    grad_branch = (correct[0] * cot_a + correct[1] * cot_b).astype(jnp.bfloat16)
    grad_correct = jnp.stack([jnp.sum(cot_a * branch_sum), jnp.sum(cot_b * branch_sum)])
    all_grad = lax.all_gather(grad_branch, "mp", axis=2, tiled=True)
    grad_rows = lax.dynamic_slice_in_dim(all_grad, offset, local_len, 1).astype(jnp.float32)
    grad_hidden = jnp.einsum("rtd,fd->rtf", all_grad, ffn_out, preferred_element_type=jnp.float32)
    grad_ffn_out = jnp.einsum("rtf,rtd->fd", hidden, all_grad, preferred_element_type=jnp.float32)
    unused_hidden, gate_back = jax.vjp(gated_unit, gate_up[0], gate_up[1])
    grad_gate, grad_up = gate_back(grad_hidden)
    grad_gate_up = jnp.stack([grad_gate, grad_up]).astype(jnp.bfloat16)
    grad_ffn_in = jnp.einsum(
        "rtd,crtf->cdf", all_normed, grad_gate_up, preferred_element_type=jnp.float32
    )
    normed_part = jnp.einsum(
        "crtf,cdf->rtd", grad_gate_up, ffn_in, preferred_element_type=jnp.float32
    )
    grad_normed_c = lax.psum_scatter(normed_part, "mp", scatter_dimension=1, tiled=True)
    grad_resid_c, gain_grad_c = rms_back(resid_c, norm_gains[2], grad_normed_c)
    grad_cross_b = (grad_rows + grad_resid_c).astype(jnp.bfloat16)
    grad_cross_out = jnp.einsum(
        "rtd,rte->de", cross_mix, grad_cross_b, preferred_element_type=jnp.float32
    )
    grad_cross_mix = jnp.einsum(
        "rte,de->rtd", grad_cross_b, w_cross_out, preferred_element_type=jnp.float32
    ).astype(jnp.bfloat16)
    grad_cq, cross_key_part, cross_dot = query_side_grads(
        cross_q, all_ckv[0], all_ckv[1], None, cross_log, grad_cross_mix
    )
    grad_cq_b = grad_cq.astype(jnp.bfloat16)
    grad_cross_first = jnp.einsum(
        "rtd,rte->de", normed_b, grad_cq_b, preferred_element_type=jnp.float32
    )
    grad_normed_b = jnp.einsum(
        "rte,de->rtd", grad_cq_b, w_cross[0], preferred_element_type=jnp.float32
    )
    resid_b_part, gain_grad_b = rms_back(resid_b, norm_gains[1], grad_normed_b)
    grad_resid_b = grad_resid_c + resid_b_part
    grad_attn_b = (grad_rows + grad_resid_b).astype(jnp.bfloat16)
    grad_self_out = jnp.einsum(
        "rtd,rte->de", self_mix, grad_attn_b, preferred_element_type=jnp.float32
    )
    grad_self_mix = jnp.einsum(
        "rte,de->rtd", grad_attn_b, w_self_out, preferred_element_type=jnp.float32
    ).astype(jnp.bfloat16)
    grad_query, self_key_part, self_dot = query_side_grads(
        queries, all_kv[0], all_kv[1], allowed, self_log, grad_self_mix
    )
    own_kv, own_ckv = (
        lax.psum_scatter(
            self_key_part.astype(jnp.bfloat16), "mp", scatter_dimension=2, tiled=True
        ).astype(jnp.float32),
        lax.psum_scatter(
            cross_key_part.astype(jnp.bfloat16), "mp", scatter_dimension=2, tiled=True
        ).astype(jnp.float32),
    )
    own_kv_b = own_kv.astype(jnp.bfloat16)
    own_ckv_b = own_ckv.astype(jnp.bfloat16)
    grad_qkv_b = jnp.concatenate([grad_query.astype(jnp.bfloat16)[None], own_kv_b], axis=0)
    grad_self_qkv = jnp.einsum(
        "rtd,crte->cde", normed_a, grad_qkv_b, preferred_element_type=jnp.float32
    )
    grad_normed_a = jnp.einsum(
        "crte,cde->rtd", grad_qkv_b, w_self, preferred_element_type=jnp.float32
    )
    grad_cross_kv = jnp.einsum(
        "rsd,crse->cde", encoder, own_ckv_b, preferred_element_type=jnp.float32
    )
    grad_encoder = jnp.einsum(
        "crse,cde->rsd", own_ckv_b, w_cross[1:], preferred_element_type=jnp.float32
    )
    grad_cross_qkv = jnp.concatenate([grad_cross_first[None], grad_cross_kv], axis=0)
    resid_a_part, gain_grad_a = rms_back(resid_a, norm_gains[0], grad_normed_a)
    grad_active = (grad_resid_b + resid_a_part).astype(jnp.bfloat16)
    grad_cols = lax.all_to_all(grad_active, "mp", split_axis=2, concat_axis=1, tiled=True).astype(
        jnp.float32
    )
    grad_guess_a = cot_a + grad_cols
    grad_predict = jnp.stack(
        [
            jnp.stack([jnp.sum(grad_guess_a * block_a), jnp.sum(grad_guess_a * block_b)]),
            jnp.stack([jnp.sum(cot_b * block_a), jnp.sum(cot_b * block_b)]),
        ]
    )
    grad_rows_state = jnp.stack(
        [
            predict[0, 0] * grad_guess_a + predict[1, 0] * cot_b,
            predict[0, 1] * grad_guess_a + predict[1, 1] * cot_b,
        ],
        axis=2,
    )
    grad_state = jnp.transpose(grad_rows_state, (0, 2, 3, 1))
    gain_grads = jnp.stack([gain_grad_a, gain_grad_b, gain_grad_c])
    part_self_qkv, part_self_out, part_cross_qkv, part_cross_out, part_ffn_in, part_ffn_out = (
        lax.psum_scatter(
            grad_self_qkv.astype(jnp.bfloat16), "dp", scatter_dimension=2, tiled=True
        ).astype(jnp.float32),
        lax.psum_scatter(
            grad_self_out.astype(jnp.bfloat16), "dp", scatter_dimension=1, tiled=True
        ).astype(jnp.float32),
        lax.psum_scatter(
            grad_cross_qkv.astype(jnp.bfloat16), "dp", scatter_dimension=2, tiled=True
        ).astype(jnp.float32),
        lax.psum_scatter(
            grad_cross_out.astype(jnp.bfloat16), "dp", scatter_dimension=1, tiled=True
        ).astype(jnp.float32),
        lax.psum_scatter(
            grad_ffn_in.astype(jnp.bfloat16), "dp", scatter_dimension=1, tiled=True
        ).astype(jnp.float32),
        lax.psum_scatter(
            grad_ffn_out.astype(jnp.bfloat16), "dp", scatter_dimension=1, tiled=True
        ).astype(jnp.float32),
    )
    final_self_qkv, final_self_out, final_cross_qkv, final_cross_out = (
        lax.psum_scatter(
            part_self_qkv.astype(jnp.bfloat16), "mp", scatter_dimension=1, tiled=True
        ).astype(jnp.float32),
        lax.psum_scatter(
            part_self_out.astype(jnp.bfloat16), "mp", scatter_dimension=0, tiled=True
        ).astype(jnp.float32),
        lax.psum_scatter(
            part_cross_qkv.astype(jnp.bfloat16), "mp", scatter_dimension=1, tiled=True
        ).astype(jnp.float32),
        lax.psum_scatter(
            part_cross_out.astype(jnp.bfloat16), "mp", scatter_dimension=0, tiled=True
        ).astype(jnp.float32),
    )
    total_gains, total_predict, total_correct = lax.psum(
        (gain_grads, grad_predict, grad_correct), ("dp", "mp")
    )
    return (
        new_state,
        grad_state,
        grad_encoder,
        final_self_qkv,
        final_self_out,
        final_cross_qkv,
        final_cross_out,
        part_ffn_in,
        part_ffn_out,
        total_gains,
        total_predict,
        total_correct,
    )


def solution(mesh):
    in_specs = (
        P("dp", None, "mp", None),
        P("dp", "mp", None),
        P("dp", None),
        P("dp", None),
        P(None, "mp", None),
        P("mp", None),
        P(None, "mp", None),
        P("mp", None),
        P(None, None, "mp"),
        P("mp", None),
        P(),
        P(),
        P(),
        P("dp", None, "mp", None),
    )
    out_specs = (
        P("dp", None, "mp", None),
        P("dp", None, "mp", None),
        P("dp", "mp", None),
        P(None, "mp", "dp"),
        P("mp", "dp"),
        P(None, "mp", "dp"),
        P("mp", "dp"),
        P(None, "dp", "mp"),
        P("mp", "dp"),
        P(),
        P(),
        P(),
    )
    return jax.shard_map(shards, mesh=mesh, in_specs=in_specs, out_specs=out_specs, check_vma=False)
```

profile of v0, /device:TPU:0, one launch (start us, length us, event | category | flops | bytes accessed | tf_op | source)
XLA Modules:
  0.0 1167.1 jit_solution(17390512784717672318)
XLA Ops:
  8.7 34.3 %all-gather.15.cloned.1.call-done = bf16[3,768,768]{2,1,0:T(8,128)(2,1)} async-done(((bf16[3,192,768]{2,1,0:T(8,128)(2,1)}), bf16[3,768,768]{2,1,0:T(8,128)(2,1)}) %all-gather.15.cloned.1.call-update) | async-done | bytes 3538960 | tf_op jit(solution)/shard_map/all_gather | solution.py:128
  61.2 24.0 %all-to-all-done = bf16[2,1024,192]{2,0,1:T(2,128)(2,1)} async-done(((bf16[2,1024,192]{2,0,1:T(2,128)(2,1)}), bf16[2,1024,192]{2,0,1:T(2,128)(2,1)}, u32[]{:S(2)}, u32[]{:S(2)}) %all-to-all-start) | async-done | bytes 786464 | tf_op jit(solution)/shard_map/all_to_all | solution.py:131
  96.1 4.6 convert_bitcast_fusion.2
  110.3 5.5 all-gather.17.cloned.1.call-done
  119.6 44.1 %all-gather.11.cloned.1.call-done = bf16[2,2,1024,768]{3,2,0,1:T(8,128)(2,1)} async-done(((bf16[2,2,256,768]{3,2,0,1:T(8,128)(2,1)}), bf16[2,2,1024,768]{3,2,0,1:T(8,128)(2,1)}) %all-gather.11.cloned.1.call-update) | async-done | bytes 6291472 | tf_op jit(solution)/shard_map/all_gather | solution.py:144
  163.6 5.8 fusion.105
  169.5 4.7 copy.432
  174.2 4.7 copy.430
  178.9 15.2 %fusion.7 = (f32[2,12,256]{2,1,0:T(8,128)S(1)}, f32[2,12,256,1024]{3,2,1,0:T(8,128)}) fusion(pred[2,256,1024]{2,1,0:T(8,128)(4,1)S(1)} %and_or_fusion, bf16[2,256,12,64]{1,3,2,0:T(8,128)(2,1)} %bitcast.360, bf16[2,1024,12,64]{1,3,2,0:T(8,128)(2,1)} %bitcast.352), kind=kOutput, calls=%fused_computation.20 | convolution fusion | flops 824174592 | bytes 29646848 | tf_op jit(solution)/shard_map/rqhd,rkhd->rhqk/dot_general | solution.py:48
  194.0 11.9 %fusion = f32[2,12,256]{2,1,0:T(8,128)S(1)} fusion(f32[2,12,256]{2,1,0:T(8,128)S(1)} %get-tuple-element.156, f32[2,12,256,1024]{3,2,1,0:T(8,128)} %get-tuple-element.157, pred[2,256,1024]{2,1,0:T(8,128)(4,1)S(1)} %and_or_fusion), kind=kLoop, calls=%fused_computation.6 | loop fusion | flops 25159680 | bytes 25739264 | tf_op jit(solution)/shard_map/reduce_sum | solution.py:63
  206.0 12.9 %fusion.70 = bf16[2,12,64,256]{3,2,1,0:T(8,128)(2,1)} fusion(bf16[2,1024,12,64]{1,3,2,0:T(8,128)(2,1)S(1)} %bitcast.359, f32[2,12,256]{2,1,0:T(8,128)S(1)} %fusion, f32[2,12,256]{2,1,0:T(8,128)S(1)} %get-tuple-element.156, f32[2,12,256,1024]{3,2,1,0:T(8,128)} %get-tuple-element.157, pred[2,256,1024]{2,1,0:T(8,128)(4,1)S(1)} %and_or_fusion), kind=kOutput, calls=%fused_computation.144 | convolution fusion | flops 837156864 | bytes 29671424 | tf_op jit(solution)/shard_map/rhqk,rkhd->rqhd/dot_general | solution.py:65
  237.8 5.0 fusion.69
  255.4 22.6 %all-gather.21.cloned.1.call-done = bf16[2,1024,768]{2,1,0:T(8,128)(2,1)} async-done(((bf16[2,256,768]{2,1,0:T(8,128)(2,1)}), bf16[2,1024,768]{2,1,0:T(8,128)(2,1)}) %all-gather.21.cloned.1.call-update) | async-done | bytes 3145744 | tf_op jit(solution)/shard_map/all_gather | solution.py:161
  278.0 10.0 convolution_bitcast_fusion
  288.1 20.1 %all-gather.23.cloned.1.call-done = bf16[2,1024,768]{1,0,2:T(2,128)(2,1)} async-done(((bf16[2,1024,192]{1,0,2:T(2,128)(2,1)}), bf16[2,1024,768]{1,0,2:T(2,128)(2,1)}) %all-gather.23.cloned.1.call-update) | async-done | bytes 3145744 | tf_op jit(solution)/shard_map/all_gather | solution.py:180
  308.1 13.1 %fusion.31 = (bf16[1,2,1024,768]{3,2,1,0:T(8,128)(2,1)S(1)}, bf16[1,2,1024,768]{3,2,1,0:T(8,128)(2,1)S(1)}, bf16[2,1024,768]{2,1,0:T(8,128)(2,1)}) fusion(f32[2,2,1024,768]{3,2,0,1:T(8,128)} %convolution_bitcast_fusion, bf16[768,768]{1,0:T(8,128)(2,1)} %param.23, bf16[2,1024,768]{1,0,2:T(2,128)(2,1)} %all-gather.23.cloned.1.call-done), kind=kOutput, calls=%fused_computation.61 | convolution fusion | flops 2456813568 | bytes 26345472 | tf_op jit(solution)/shard_map/rtd,fd->rtf/dot_general | solution.py:182
  323.8 6.9 fusion.36
  335.7 54.0 %reduce-scatter.23.cloned.1.call-done = f32[2,256,768]{2,1,0:T(8,128)} async-done(((f32[2,1024,768]{2,1,0:T(8,128)}), f32[2,256,768]{2,1,0:T(8,128)}) %reduce-scatter.23.cloned.1.call-update) | async-done | bytes 1572880 | tf_op jit(solution)/shard_map/reduce_scatter | solution.py:193
  399.8 11.8 %multiply_reduce_fusion.1 = (f32[2,12,256]{2,1,0:T(8,128)S(1)}, f32[2,12,256,512]{3,2,1,0:T(8,128)}) fusion(f32[2,12,256,512]{3,2,1,0:T(8,128)} %copy-done.2, f32[2,12,256]{2,1,0:T(8,128)S(1)} %log_add_fusion.1, bf16[2,256,12,64]{1,3,2,0:T(8,128)(2,1)S(1)} %bitcast.364, bf16[2,512,12,64]{1,3,2,0:T(8,128)(2,1)} %bitcast.372), kind=kOutput, calls=%fused_computation.11 | convolution fusion | flops 415229952 | bytes 27574272 | tf_op jit(solution)/shard_map/rqhd,rkhd->rhqk/dot_general | solution.py:75
  412.9 6.7 multiply_convert_fusion.1
  432.9 6.3 fusion.52
  441.1 8.8 copy.505
  450.0 8.1 reshape.292
  462.6 13.0 %fusion.41 = bf16[2,12,64,1024]{3,2,1,0:T(8,128)(2,1)} fusion(bf16[2,256,12,64]{1,3,2,0:T(8,128)(2,1)S(1)} %bitcast.385, f32[2,12,256]{2,1,0:T(8,128)S(1)} %log_add_fusion, f32[2,12,256,1024]{3,2,1,0:T(8,128)} %get-tuple-element.157, pred[2,256,1024]{2,1,0:T(8,128)(4,1)S(1)} %and_or_fusion), kind=kOutput, calls=%fused_computation.81 | convolution fusion | flops 832045056 | bytes 29646848 | tf_op jit(solution)/shard_map/rhqk,rqhd->rkhd/dot_general | solution.py:91
  475.5 4.6 copy.453
  480.2 19.3 %multiply_reduce_fusion = (f32[2,12,256]{2,1,0:T(8,128)S(1)}, f32[2,12,256,1024]{3,2,1,0:T(8,128)}) fusion(f32[2,12,256]{2,1,0:T(8,128)S(1)} %log_add_fusion, f32[2,12,256,1024]{3,2,1,0:T(8,128)} %get-tuple-element.157, pred[2,256,1024]{2,1,0:T(8,128)(4,1)S(1)} %and_or_fusion, bf16[2,256,12,64]{1,3,2,0:T(8,128)(2,1)S(1)} %bitcast.386, ...), kind=kOutput, calls=%fused_computation.1 | convolution fusion | flops 836757504 | bytes 54837248 | tf_op jit(solution)/shard_map/rqhd,rkhd->rhqk/dot_general | solution.py:75
  499.5 17.0 %multiply_convert_fusion = bf16[2,12,256,1024]{3,2,1,0:T(8,128)(2,1)S(1)} fusion(f32[2,12,256,1024]{3,2,1,0:T(8,128)} %get-tuple-element.165, f32[2,12,256]{2,1,0:T(8,128)S(1)} %get-tuple-element.164, f32[2,12,256]{2,1,0:T(8,128)S(1)} %log_add_fusion, f32[2,12,256,1024]{3,2,1,0:T(8,128)} %get-tuple-element.157, pred[2,256,1024]{2,1,0:T(8,128)(4,1)S(1)} %and_or_fusion), kind=kLoop, calls=%fused_computation | loop fusion | flops 37748736 | bytes 63488000 | tf_op jit(solution)/shard_map/convert_element_type | solution.py:79
  522.1 4.7 copy.452
  526.8 6.1 pad_maximum_fusion.1
  534.2 5.0 convolution_convert_fusion
  539.1 5.0 copy.443
  544.2 8.3 fusion.38
  552.5 4.6 copy.471
  557.2 6.7 bitcast_convert_fusion.3
  580.3 11.7 multiply_convert_fusion.6
  592.3 39.3 %reduce-scatter.25.cloned.1.call-done = bf16[2,2,256,768]{3,2,0,1:T(8,128)(2,1)} async-done(((bf16[2,2,1024,768]{3,2,0,1:T(8,128)(2,1)}), bf16[2,2,256,768]{3,2,0,1:T(8,128)(2,1)}) %reduce-scatter.25.cloned.1.call-update) | async-done | bytes 1572880 | tf_op jit(solution)/shard_map/reduce_scatter | solution.py:225
  631.6 5.3 fusion.23
  645.8 17.9 %all-to-all-done.1 = bf16[2,256,768]{1,0,2:T(2,128)(2,1)S(1)} async-done(((bf16[2,256,768]{1,0,2:T(2,128)(2,1)}), bf16[2,256,768]{1,0,2:T(2,128)(2,1)S(1)}, u32[]{:S(2)}, u32[]{:S(2)}) %all-to-all-start.1) | async-done | bytes 786464 | tf_op jit(solution)/shard_map/all_to_all | solution.py:169
  675.3 36.9 %all-reduce.6.cloned.1.call-done = bf16[2,1024,768]{1,0,2:T(2,128)(2,1)} async-done(((bf16[2,1024,768]{1,0,2:T(2,128)(2,1)}), bf16[2,1024,768]{1,0,2:T(2,128)(2,1)}) %all-reduce.6.cloned.1.call-update) | async-done | bytes 3145744
  713.9 110.4 %all-reduce.8.cloned.1.call-done = bf16[2,768,768]{2,0,1:T(2,128)(2,1)} async-done(((bf16[2,768,768]{2,0,1:T(2,128)(2,1)}), bf16[2,768,768]{2,0,1:T(2,128)(2,1)}) %all-reduce.8.cloned.1.call-update) | async-done | bytes 2359312
  826.3 65.1 %reduce-scatter.35.cloned.1.call-done = bf16[768,96]{0,1:T(8,128)(2,1)} async-done(((bf16[768,768]{0,1:T(8,128)(2,1)}), bf16[768,96]{0,1:T(8,128)(2,1)}) %reduce-scatter.35.cloned.1.call-update) | async-done | bytes 147472 | tf_op jit(solution)/shard_map/reduce_scatter | solution.py:285
  893.0 20.1 %reduce-scatter.45.cloned.1.call-done = bf16[192,96]{1,0:T(8,128)(2,1)} async-done(((bf16[768,96]{1,0:T(8,128)(2,1)}), bf16[192,96]{1,0:T(8,128)(2,1)}) %reduce-scatter.45.cloned.1.call-update) | async-done | bytes 36880
  914.8 21.1 %reduce-scatter.41.cloned.1.call-done = bf16[192,96]{1,0:T(8,128)(2,1)} async-done(((bf16[768,96]{1,0:T(8,128)(2,1)}), bf16[192,96]{1,0:T(8,128)(2,1)}) %reduce-scatter.41.cloned.1.call-update) | async-done | bytes 36880
  941.9 77.1 %reduce-scatter.31.cloned.1.call-done = bf16[3,768,96]{1,2,0:T(8,128)(2,1)} async-done(((bf16[3,768,768]{1,2,0:T(8,128)(2,1)}), bf16[3,768,96]{1,2,0:T(8,128)(2,1)}) %reduce-scatter.31.cloned.1.call-update) | async-done | bytes 442384 | tf_op jit(solution)/shard_map/reduce_scatter | solution.py:276
  1025.3 6.0 fusion.66
  1035.8 65.7 %reduce-scatter.27.cloned.1.call-done = bf16[3,768,96]{1,2,0:T(8,128)(2,1)} async-done(((bf16[3,768,768]{1,2,0:T(8,128)(2,1)}), bf16[3,768,96]{1,2,0:T(8,128)(2,1)}) %reduce-scatter.27.cloned.1.call-update) | async-done | bytes 442384 | tf_op jit(solution)/shard_map/reduce_scatter | solution.py:270
  1104.2 4.9 multiply_add_fusion.1
  1115.4 40.3 %all-reduce.2 = (f32[3,768]{1,0:T(4,128)}, f32[2,2]{1,0:T(2,128)}, f32[2]{0:T(128)}) all-reduce(f32[3,768]{1,0:T(4,128)S(1)} %pad_maximum_fusion.13, f32[2,2]{1,0:T(2,128)S(1)} %pad_maximum_fusion.14, f32[2]{0:T(128)S(1)} %pad_maximum_fusion.15), channel_id=1, replica_groups=mesh['dp'=8,'mp'=4] {'dp','mp'}, use_global_device_ids=true, to_apply=%region_30.31 | all-reduce | flops 2310 | bytes 18480 | tf_op jit(solution)/shard_map/psum | solution.py:303
  (284 shorter events, 192.6 us)
Async XLA Ops:
  7.2 270.9 %copy-start = (bf16[2,768,768]{2,1,0:T(8,128)(2,1)S(1)}, bf16[2,768,768]{2,1,0:T(8,128)(2,1)}, u32[]{:S(2)}) copy-start(bf16[2,768,768]{2,1,0:T(8,128)(2,1)} %param.22) | copy-start | bytes 7077892
  7.2 35.9 %all-gather.15.cloned.1.call-start = ((), (), s32[]{:S(2)}) async-start(), calls=%async_computation.18 | async-start | bytes 4423680 | tf_op jit(solution)/shard_map/all_gather | solution.py:128
  7.9 88.1 %all-gather.9.cloned.1.call-start = ((), (), s32[]{:S(2)}) async-start(), calls=%async_computation.15 | async-start | bytes 4423680 | tf_op jit(solution)/shard_map/all_gather | solution.py:126
  8.7 37.8 %copy-start.46 = (f32[2,2]{1,0:T(2,128)S(1)}, f32[2,2]{1,0:T(2,128)}, u32[]{:S(2)}) copy-start(f32[2,2]{1,0:T(2,128)} %param.25) | copy-start | bytes 52
  8.7 107.2 %all-gather.17.cloned.1.call-start = ((), (), s32[]{:S(2)}) async-start(), calls=%async_computation.19 | async-start | bytes 3932160 | tf_op jit(solution)/shard_map/all_gather | solution.py:145
  56.8 28.4 %all-to-all-start = ((bf16[2,1024,192]{2,0,1:T(2,128)(2,1)}), bf16[2,1024,192]{2,0,1:T(2,128)(2,1)}, u32[]{:S(2)}, u32[]{:S(2)}) async-start(bf16[2,1024,192]{2,0,1:T(2,128)(2,1)} %copy.424), calls=%async_computation | async-start | bytes 2097152 | tf_op jit(solution)/shard_map/all_to_all | solution.py:131
  61.0 102.6 %all-gather.11.cloned.1.call-start = ((), (), s32[]{:S(2)}) async-start(), calls=%async_computation.16 | async-start | bytes 7864320 | tf_op jit(solution)/shard_map/all_gather | solution.py:144
  61.1 34.9 %copy-start.39 = (f32[768]{0:T(1024)}, f32[768]{0:T(1024)S(1)}, u32[]{:S(2)}) copy-start(f32[768]{0:T(1024)S(1)} %get-tuple-element.125) | copy-start | bytes 9220
  103.4 115.5 %all-gather.13.cloned.1.call-start = ((), (), s32[]{:S(2)}) async-start(), calls=%async_computation.17 | async-start | bytes 1474560 | tf_op jit(solution)/shard_map/all_gather | solution.py:127
  104.0 138.8 %all-gather.19.cloned.1.call-start = ((), (), s32[]{:S(2)}) async-start(), calls=%async_computation.20 | async-start | bytes 1474560 | tf_op jit(solution)/shard_map/all_gather | solution.py:129
  104.6 173.5 %all-gather.21.cloned.1.call-start = ((), (), s32[]{:S(2)}) async-start(), calls=%async_computation.21 | async-start | bytes 3932160 | tf_op jit(solution)/shard_map/all_gather | solution.py:161
  194.0 11.9 %copy-start.20 = (bf16[1,2,1024,768]{2,3,1,0:T(8,128)(2,1)S(1)}, bf16[1,2,1024,768]{2,3,1,0:T(8,128)(2,1)}, u32[]{:S(2)}) copy-start(bf16[1,2,1024,768]{2,3,1,0:T(8,128)(2,1)} %copy.430) | copy-start | bytes 9437188
  249.3 58.8 %all-gather.23.cloned.1.call-start = ((), (), s32[]{:S(2)}) async-start(), calls=%async_computation.22 | async-start | bytes 3932160 | tf_op jit(solution)/shard_map/all_gather | solution.py:180
  255.4 134.4 %reduce-scatter.23.cloned.1.call-start = ((), (), s32[]{:S(2)}) async-start(), calls=%async_computation.23 | async-start | bytes 7864320 | tf_op jit(solution)/shard_map/reduce_scatter | solution.py:193
  330.8 59.0 %copy-start.7 = (f32[2,256,768]{2,1,0:T(8,128)S(1)}, f32[2,256,768]{2,1,0:T(8,128)}, u32[]{:S(2)}) copy-start(f32[2,256,768]{2,1,0:T(8,128)} %copy-done.6) | copy-start | bytes 4718596
  330.8 233.3 %reduce-scatter.33.cloned.1.call-start = ((), (), s32[]{:S(2)}) async-start(), calls=%async_computation.28 | async-start | bytes 1327104 | tf_op jit(solution)/shard_map/reduce_scatter | solution.py:279
  335.7 56.5 %copy-start.23 = (bf16[2,256,768]{2,1,0:T(8,128)(2,1)}, bf16[2,256,768]{2,1,0:T(8,128)(2,1)S(1)}, u32[]{:S(2)}) copy-start(bf16[2,256,768]{2,1,0:T(8,128)(2,1)S(1)} %copy.518) | copy-start | bytes 2359300
  399.7 169.7 %reduce-scatter.29.cloned.1.call-start = ((), (), s32[]{:S(2)}) async-start(), calls=%async_computation.26 | async-start | bytes 1327104 | tf_op jit(solution)/shard_map/reduce_scatter | solution.py:273
  399.8 11.8 %slice-start = ((s8[12582912]{0:T(1024)(128)(4,1)}), s8[4194304]{0:T(1024)(128)(4,1)S(1)}, s32[]{:S(2)}) async-start(s8[12582912]{0:T(1024)(128)(4,1)} %bitcast.350), calls=%async_computation.37 | async-start | bytes 8388608
  399.8 11.8 %slice-start.1 = ((s8[12582912]{0:T(1024)(128)(4,1)}), s8[4194304]{0:T(1024)(128)(4,1)S(1)}, s32[]{:S(2)}) async-start(s8[12582912]{0:T(1024)(128)(4,1)} %bitcast.350), calls=%async_computation.38 | async-start | bytes 8388608
  399.8 13.1 %slice-start.2 = ((s8[12582912]{0:T(1024)(128)(4,1)}), s8[4194304]{0:T(1024)(128)(4,1)S(1)}, s32[]{:S(2)}) async-start(s8[12582912]{0:T(1024)(128)(4,1)} %bitcast.350), calls=%async_computation.39 | async-start | bytes 8388608
  412.9 6.7 copy-start.14
  428.8 142.5 %reduce-scatter.37.cloned.1.call-start = ((), (), s32[]{:S(2)}) async-start(), calls=%async_computation.30 | async-start | bytes 3932160
  450.0 8.1 copy-start.16
  450.0 8.1 copy-start.25
  462.5 169.1 %reduce-scatter.25.cloned.1.call-start = ((), (), s32[]{:S(2)}) async-start(), calls=%async_computation.24 | async-start | bytes 7864320 | tf_op jit(solution)/shard_map/reduce_scatter | solution.py:225
  499.5 17.0 %copy-start.21 = (bf16[1,2,256,768]{2,3,1,0:T(8,128)(2,1)S(1)}, bf16[1,2,256,768]{2,3,1,0:T(8,128)(2,1)}, u32[]{:S(2)}) copy-start(bf16[1,2,256,768]{2,3,1,0:T(8,128)(2,1)} %copy.431) | copy-start | bytes 2359300
  532.9 179.3 %all-reduce.6.cloned.1.call-start = ((), (), s32[]{:S(2)}) async-start(), calls=%async_computation.35 | async-start | bytes 6291456
  544.2 280.2 %all-reduce.8.cloned.1.call-start = ((), (), s32[]{:S(2)}) async-start(), calls=%async_computation.36 | async-start | bytes 4718592
  557.1 8.7 copy-start.12
  557.1 8.7 copy-start.31
  557.2 334.2 %reduce-scatter.35.cloned.1.call-start = ((), (), s32[]{:S(2)}) async-start(), calls=%async_computation.29 | async-start | bytes 1327104 | tf_op jit(solution)/shard_map/reduce_scatter | solution.py:285
  564.0 349.2 %reduce-scatter.45.cloned.1.call-start = ((), (), s32[]{:S(2)}) async-start(), calls=%async_computation.34 | async-start | bytes 245760
  565.8 370.0 %reduce-scatter.41.cloned.1.call-start = ((), (), s32[]{:S(2)}) async-start(), calls=%async_computation.32 | async-start | bytes 245760
  571.2 447.8 %reduce-scatter.31.cloned.1.call-start = ((), (), s32[]{:S(2)}) async-start(), calls=%async_computation.27 | async-start | bytes 3981312 | tf_op jit(solution)/shard_map/reduce_scatter | solution.py:276
  580.3 51.3 %copy-start.13 = (f32[2,256,768]{2,1,0:T(8,128)S(1)}, f32[2,256,768]{2,1,0:T(8,128)}, u32[]{:S(2)}) copy-start(f32[2,256,768]{2,1,0:T(8,128)} %copy.429) | copy-start | bytes 4718596
  580.3 51.3 %copy-start.40 = (f32[768]{0:T(1024)S(1)}, f32[768]{0:T(1024)}, u32[]{:S(2)}) copy-start(f32[768]{0:T(1024)} %copy-done.39) | copy-start | bytes 9220
  580.3 51.3 %copy-start.43 = (f32[2,256]{1,0:T(2,128)S(1)}, f32[2,256]{1,0:T(2,128)}, u32[]{:S(2)}) copy-start(f32[2,256]{1,0:T(2,128)} %copy-done.42) | copy-start | bytes 6148
  580.3 521.2 %reduce-scatter.27.cloned.1.call-start = ((), (), s32[]{:S(2)}) async-start(), calls=%async_computation.25 | async-start | bytes 3981312 | tf_op jit(solution)/shard_map/reduce_scatter | solution.py:270
  636.9 6.4 copy-start.52
  636.9 7.0 copy-start.51
  639.8 23.9 %all-to-all-start.1 = ((bf16[2,256,768]{1,0,2:T(2,128)(2,1)}), bf16[2,256,768]{1,0,2:T(2,128)(2,1)S(1)}, u32[]{:S(2)}, u32[]{:S(2)}) async-start(bf16[2,256,768]{1,0,2:T(2,128)(2,1)} %copy.438), calls=%async_computation.1 | async-start | bytes 1572864 | tf_op jit(solution)/shard_map/all_to_all | solution.py:169
  671.5 269.4 %all-to-all-start.2 = ((bf16[2,256,768]{1,0,2:T(2,128)(2,1)}), bf16[2,256,768]{1,0,2:T(2,128)(2,1)S(1)}, u32[]{:S(2)}, u32[]{:S(2)}) async-start(bf16[2,256,768]{1,0,2:T(2,128)(2,1)} %copy.457), calls=%async_computation.4 | async-start | bytes 1572864 | tf_op jit(solution)/shard_map/all_to_all | solution.py:250
  675.0 262.5 %copy-start.29 = (bf16[2,2,128,768]{2,3,1,0:T(8,128)(2,1)S(1)}, bf16[2,2,128,768]{2,3,1,0:T(8,128)(2,1)}, u32[]{:S(2)}) copy-start(bf16[2,2,128,768]{2,3,1,0:T(8,128)(2,1)} %copy.506) | copy-start | bytes 2359300
  675.0 480.7 %reduce-scatter.43.cloned.1.call-start = ((), (), s32[]{:S(2)}) async-start(), calls=%async_computation.33 | async-start | bytes 737280
  1021.7 136.0 %reduce-scatter.39.cloned.1.call-start = ((), (), s32[]{:S(2)}) async-start(), calls=%async_computation.31 | async-start | bytes 737280
  1035.8 68.4 %copy-start.27 = (f32[2,1024,1,192]{1,3,0,2:T(8,128)S(1)}, f32[2,1024,1,192]{1,3,0,2:T(8,128)}, u32[]{:S(2)}) copy-start(f32[2,1024,1,192]{1,3,0,2:T(8,128)} %reshape.264) | copy-start | bytes 4718596
  1109.5 50.3 %copy-start.1 = (bf16[2,768,768]{2,1,0:T(8,128)(2,1)S(1)}, bf16[2,768,768]{2,1,0:T(8,128)(2,1)}, u32[]{:S(2)}) copy-start(bf16[2,768,768]{2,1,0:T(8,128)(2,1)} %param.22) | copy-start | bytes 7077892
  (35 other events, 92.0 us)
Sparse Core Ops, SparseCore 0:
  9.6 33.4 all-gather.14
  44.6 40.4 all-gather.8
  86.6 29.1 all-gather.16
  117.3 46.3 all-gather.10
  165.1 17.4 all-gather.12
  183.9 17.4 all-gather.18
  249.5 28.5 all-gather.20
  279.6 28.4 all-gather.22
  330.9 58.8 reduce-scatter.22
  399.8 64.7 reduce-scatter.32
  468.0 63.6 reduce-scatter.28
  534.1 36.8 reduce-scatter.36
  573.6 57.9 reduce-scatter.24
  633.8 78.3 all-reduce.5
  715.6 108.6 all-reduce.7
  827.6 63.7 reduce-scatter.34
  894.2 18.8 reduce-scatter.44
  916.0 19.7 reduce-scatter.40
  939.5 79.4 reduce-scatter.30
  1022.4 79.0 reduce-scatter.26
  1104.0 22.1 reduce-scatter.42
  1128.7 21.8 reduce-scatter.38
where the time goes:
time: 1170 us
  waiting for transfers between devices  661 us (56%)
  matrix products  206 us (18%)
  local copies, waits for them, and re-layouts  146 us (12%)
  other arithmetic  84.3 us (7%)
  blocking collectives  40.3 us (3%)
  between operations  17.1 us (1%)
  starting transfers between devices  12.6 us (1%)
    unnamed x29, waiting for transfers between devices  191 us
    reduce_scatter x1, waiting for transfers between devices, shards(): lax.psum_scatter(grad_cross_qkv.astype(jnp.bfloat16), 'dp', scatter_dimen...  77.1 us
    unnamed x144, local copies, waits for them, and re-layouts  67.8 us
    reduce_scatter x1, waiting for transfers between devices, shards(): lax.psum_scatter(grad_self_qkv.astype(jnp.bfloat16), 'dp', scatter_dimens...  65.7 us
    reduce_scatter x1, waiting for transfers between devices, shards(): lax.psum_scatter(grad_ffn_out.astype(jnp.bfloat16), 'dp', scatter_dimensi...  65.1 us
    reduce_scatter x1, waiting for transfers between devices, shards(): lax.psum_scatter(normed_part, 'mp', scatter_dimension=1, tiled=True)  54 us
    all_gather x1, waiting for transfers between devices, shards(): lax.all_gather(self_proj[1:], 'mp', axis=2, tiled=True)  44.1 us
    psum x1, blocking collectives, shards(): lax.psum((gain_grads, grad_predict, grad_correct), ('dp', 'mp'))  40.3 us
  transfers between devices with their start and end apart: 25, of which 16 were waited for; matrix products, arithmetic and copies ran while one was open for 32% of the time, Pallas kernels for 0%

commit v1 on v0

--- a/solution.py
+++ b/solution.py
@@ -1,6 +1,10 @@
+import functools
+
 import jax
 import jax.numpy as jnp
 from jax import lax
+from jax.experimental import pallas as pl
+from jax.experimental.pallas import tpu as pltpu
 from jax.sharding import PartitionSpec as P
 
 HEADS = 12
@@ -17,7 +21,7 @@
 
 
 def rms_back(values, norm_gain, incoming):
-    unused_out, pullback = jax.vjp(rms_norm, values, norm_gain)
+    _, pullback = jax.vjp(rms_norm, values, norm_gain)
     return pullback(incoming)
 
 
@@ -181,7 +185,7 @@
     grad_rows = lax.dynamic_slice_in_dim(all_grad, offset, local_len, 1).astype(jnp.float32)
     grad_hidden = jnp.einsum("rtd,fd->rtf", all_grad, ffn_out, preferred_element_type=jnp.float32)
     grad_ffn_out = jnp.einsum("rtf,rtd->fd", hidden, all_grad, preferred_element_type=jnp.float32)
-    unused_hidden, gate_back = jax.vjp(gated_unit, gate_up[0], gate_up[1])
+    _, gate_back = jax.vjp(gated_unit, gate_up[0], gate_up[1])
     grad_gate, grad_up = gate_back(grad_hidden)
     grad_gate_up = jnp.stack([grad_gate, grad_up]).astype(jnp.bfloat16)
     grad_ffn_in = jnp.einsum(
@@ -199,7 +203,7 @@
     grad_cross_mix = jnp.einsum(
         "rte,de->rtd", grad_cross_b, w_cross_out, preferred_element_type=jnp.float32
     ).astype(jnp.bfloat16)
-    grad_cq, cross_key_part, cross_dot = query_side_grads(
+    grad_cq, cross_key_part, _ = query_side_grads(
         cross_q, all_ckv[0], all_ckv[1], None, cross_log, grad_cross_mix
     )
     grad_cq_b = grad_cq.astype(jnp.bfloat16)
@@ -218,7 +222,7 @@
     grad_self_mix = jnp.einsum(
         "rte,de->rtd", grad_attn_b, w_self_out, preferred_element_type=jnp.float32
     ).astype(jnp.bfloat16)
-    grad_query, self_key_part, self_dot = query_side_grads(
+    grad_query, self_key_part, _ = query_side_grads(
         queries, all_kv[0], all_kv[1], allowed, self_log, grad_self_mix
     )
     own_kv, own_ckv = (
@@ -319,6 +323,795 @@
     )
 
 
+def dot_tn(left, right):
+    return lax.dot_general(
+        left, right, (((0,), (0,)), ((), ())), preferred_element_type=jnp.float32
+    )
+
+
+def dot_nn(left, right):
+    return lax.dot_general(
+        left, right, (((1,), (0,)), ((), ())), preferred_element_type=jnp.float32
+    )
+
+
+def dot_nt(left, right):
+    return lax.dot_general(
+        left, right, (((1,), (1,)), ((), ())), preferred_element_type=jnp.float32
+    )
+
+
+def block_scores(keys_t, query, seg_ref, code_ref, block, size, high):
+    scores = dot_nn(keys_t[:high], query)
+    if seg_ref is None:
+        return scores
+    seg_query = seg_ref[:, block * size : (block + 1) * size]
+    codes = jnp.concatenate([code_ref[:high, :]] * (size // 128), axis=1)
+    same = codes == seg_query
+    low = block * size
+    key = lax.broadcasted_iota(jnp.int32, (size, size), 0)
+    query_pos = lax.broadcasted_iota(jnp.int32, (size, size), 1)
+    near = (same[low:] & (key <= query_pos)) | (key == query_pos)
+    lower = jnp.where(near, scores[low:], MASKED_SCORE)
+    if low == 0:
+        return lower
+    return jnp.concatenate([jnp.where(same[:low], scores[:low], MASKED_SCORE), lower], axis=0)
+
+
+def attend_kernel(masked, size, *refs):
+    if masked:
+        q_ref, k_ref, v_ref, seg_ref, code_ref, mix_ref, log_ref = refs
+    else:
+        q_ref, k_ref, v_ref, mix_ref, log_ref = refs
+        seg_ref = code_ref = None
+    key_len, query_len = k_ref.shape[1], q_ref.shape[1]
+    keys_t = k_ref[...].T
+    values = v_ref[...]
+    for block in range(query_len // size):
+        cols = slice(block * size, (block + 1) * size)
+        high = (block + 1) * size if masked else key_len
+        query = q_ref[:, cols] * jnp.bfloat16(HEAD ** (-0.5))
+        scores = block_scores(keys_t, query, seg_ref, code_ref, block, size, high)
+        top = jnp.max(scores, axis=0, keepdims=True)
+        exponent = jnp.exp(scores - top)
+        total = jnp.sum(exponent, axis=0, keepdims=True)
+        mixed = dot_nn(values[:, :high], exponent.astype(jnp.bfloat16))
+        mix_ref[:, cols] = (mixed / total).astype(jnp.bfloat16)
+        log_ref[0, :, cols] = top + jnp.log(total)
+
+
+def attend_back_kernel(masked, size, *refs):
+    if masked:
+        q_ref, k_ref, v_ref, seg_ref, code_ref = refs[:5]
+        refs = refs[5:]
+    else:
+        q_ref, k_ref, v_ref = refs[:3]
+        seg_ref = code_ref = None
+        refs = refs[3:]
+    log_ref, mix_ref, grad_ref, dq_ref, dk_ref, dv_ref, dk_sum, dv_sum = refs
+    key_len, query_len = k_ref.shape[1], q_ref.shape[1]
+    keys = k_ref[...]
+    keys_t = keys.T
+    values_t = v_ref[...].T
+    last = query_len // size - 1
+    for block in range(last, -1, -1):
+        cols = slice(block * size, (block + 1) * size)
+        high = (block + 1) * size if masked else key_len
+        query = q_ref[:, cols] * jnp.bfloat16(HEAD ** (-0.5))
+        grad = grad_ref[:, cols]
+        scores = block_scores(keys_t, query, seg_ref, code_ref, block, size, high)
+        probs = jnp.exp(scores - log_ref[0, :, cols])
+        grad_probs = dot_nn(values_t[:high], grad)
+        row_dot = jnp.sum(
+            grad.astype(jnp.float32) * mix_ref[:, cols].astype(jnp.float32), axis=0, keepdims=True
+        )
+        grad_scores = (probs * (grad_probs - row_dot)).astype(jnp.bfloat16)
+        dq_ref[:, cols] = (dot_nn(keys[:, :high], grad_scores) * HEAD ** (-0.5)).astype(
+            jnp.bfloat16
+        )
+        dk = dot_nt(query, grad_scores)
+        dv = dot_nt(grad, probs.astype(jnp.bfloat16))
+        if block == last:
+            dk_sum[:, :high] = dk
+            dv_sum[:, :high] = dv
+        else:
+            dk_sum[:, :high] += dk
+            dv_sum[:, :high] += dv
+    dk_ref[...] = dk_sum[...].astype(jnp.bfloat16)
+    dv_ref[...] = dv_sum[...].astype(jnp.bfloat16)
+
+
+def head_rows(first, length):
+    return pl.BlockSpec((HEAD, length), lambda head: (first + head, 0))
+
+
+def attention_call(queries, keys, values, heads, mask, back, size):
+    (q_arr, q_at), (k_arr, k_at), (v_arr, v_at) = queries, keys, values
+    q_len, k_len = q_arr.shape[1], k_arr.shape[1]
+    operands = [q_arr, k_arr, v_arr]
+    specs = [head_rows(q_at, q_len), head_rows(k_at, k_len), head_rows(v_at, k_len)]
+    if mask is not None:
+        operands += list(mask)
+        specs += [
+            pl.BlockSpec((1, q_len), lambda head: (0, 0)),
+            pl.BlockSpec((k_len, 128), lambda head: (0, 0)),
+        ]
+    log_spec = pl.BlockSpec((1, 1, q_len), lambda head: (head, 0, 0))
+    q_out = jax.ShapeDtypeStruct((heads * HEAD, q_len), jnp.bfloat16)
+    k_out = jax.ShapeDtypeStruct((heads * HEAD, k_len), jnp.bfloat16)
+    pairs = heads * q_len * k_len * (0.6 if mask is not None else 1.0)
+    if back is None:
+        kernel, dots, scratch = attend_kernel, 2, []
+        out_shape = [q_out, jax.ShapeDtypeStruct((heads, 1, q_len), jnp.float32)]
+        out_specs = [head_rows(0, q_len), log_spec]
+    else:
+        kernel, dots = attend_back_kernel, 5
+        operands += list(back)
+        specs += [log_spec, head_rows(0, q_len), head_rows(0, q_len)]
+        out_shape = [q_out, k_out, k_out]
+        out_specs = [head_rows(0, q_len), head_rows(0, k_len), head_rows(0, k_len)]
+        scratch = [pltpu.VMEM((HEAD, k_len), jnp.float32)] * 2
+    return pl.pallas_call(
+        functools.partial(kernel, mask is not None, size),
+        grid=(heads,),
+        in_specs=specs,
+        out_specs=out_specs,
+        out_shape=out_shape,
+        scratch_shapes=scratch,
+        compiler_params=pltpu.CompilerParams(vmem_limit_bytes=32 << 20),
+        cost_estimate=pl.CostEstimate(
+            flops=int(8 * HEAD * dots * pairs),
+            bytes_accessed=4 * heads * HEAD * (q_len + k_len) * dots // 2,
+            transcendentals=int(pairs),
+        ),
+        name="attend" if back is None else "attend_back",
+    )(*operands)
+
+
+MESH = pl.DeviceIdType.MESH
+
+
+def after(value, *earlier):
+    return lax.optimization_barrier((value, *earlier))[0]
+
+
+def rms_scale(values):
+    return lax.rsqrt(jnp.mean(values * values, axis=0, keepdims=True) + EPSILON)
+
+
+def pick(array, index, axis=0):
+    return lax.dynamic_index_in_dim(array, index, axis, keepdims=False)
+
+
+def all_sum_kernel(dp_size, mp_size, part_ref, out_ref, mp_slots, row_sum, dp_slots, *sems):
+    mp_send, mp_recv, dp_send, dp_recv = sems
+    dp, mp = lax.axis_index("dp"), lax.axis_index("mp")
+    mp_peers = [lax.rem(mp + s, mp_size) for s in range(1, mp_size)]
+    dp_peers = [lax.rem(dp + s, dp_size) for s in range(1, dp_size)]
+    barrier = pltpu.get_barrier_semaphore()
+    for peer in mp_peers:
+        pl.semaphore_signal(barrier, inc=1, device_id=(dp, peer), device_id_type=MESH)
+    for peer in dp_peers:
+        pl.semaphore_signal(barrier, inc=1, device_id=(peer, mp), device_id_type=MESH)
+    pl.semaphore_wait(barrier, mp_size + dp_size - 2)
+
+    def exchange(source, slots, send, recv, targets):
+        copies = []
+        for step, target in enumerate(targets):
+            copies.append(
+                pltpu.make_async_remote_copy(
+                    src_ref=source,
+                    dst_ref=slots.at[step],
+                    send_sem=send.at[step],
+                    recv_sem=recv.at[step],
+                    device_id=target,
+                    device_id_type=MESH,
+                )
+            )
+            copies[-1].start()
+        for copy in copies:
+            copy.wait()
+
+    exchange(part_ref, mp_slots, mp_send, mp_recv, [(dp, p) for p in mp_peers])
+    row_sum[...] = ordered_sum(part_ref, mp_slots, mp, mp_size)
+    exchange(row_sum, dp_slots, dp_send, dp_recv, [(p, mp) for p in dp_peers])
+    out_ref[...] = ordered_sum(row_sum, dp_slots, dp, dp_size)
+
+
+def ordered_sum(own_ref, slots, place, size):
+    total = jnp.zeros_like(own_ref)
+    for device in range(size):
+        term = own_ref[...]
+        for step in range(size - 1):
+            from_here = lax.rem(place + size - step - 1, size) == device
+            term = jnp.where(from_here, slots[step], term)
+        total += term
+    return total
+
+
+def all_sum(part, dp_size, mp_size):
+    return pl.pallas_call(
+        functools.partial(all_sum_kernel, dp_size, mp_size),
+        out_shape=jax.ShapeDtypeStruct(part.shape, part.dtype),
+        in_specs=[pl.BlockSpec(memory_space=pltpu.VMEM)],
+        out_specs=pl.BlockSpec(memory_space=pltpu.VMEM),
+        scratch_shapes=[
+            pltpu.VMEM((mp_size - 1, *part.shape), part.dtype),
+            pltpu.VMEM(part.shape, part.dtype),
+            pltpu.VMEM((dp_size - 1, *part.shape), part.dtype),
+            pltpu.SemaphoreType.DMA((mp_size - 1,)),
+            pltpu.SemaphoreType.DMA((mp_size - 1,)),
+            pltpu.SemaphoreType.DMA((dp_size - 1,)),
+            pltpu.SemaphoreType.DMA((dp_size - 1,)),
+        ],
+        compiler_params=pltpu.CompilerParams(collective_id=0, has_side_effects=True),
+        name="all_sum",
+    )(part)
+
+
+def row_scatter_kernel(dp_size, keep_ref, send_ref, side_ref, out_ref, side_out_ref, *scratch):
+    landed, mine, step_send, step_land, far_send, far_land = scratch[:6]
+    cross_sems, step_sems, far_sems = scratch[6:8], scratch[8:10], scratch[10:12]
+    bf16, f32 = jnp.bfloat16, jnp.float32
+    dp, mp = lax.axis_index("dp"), lax.axis_index("mp")
+    chip, core = mp // 2, lax.rem(mp, 2)
+    outer, inner = dp // 2, lax.rem(dp, 2)
+    count = dp_size // 2
+    peer = ((dp, (1 - chip) * 2 + core))
+    mate = (outer * 2 + 1 - inner, mp)
+    offsets = [(count // 2 + i) % count for i in range(count)]
+    offsets = [o for o in offsets if o] + [0]
+    places = [lax.rem(outer + o, count) for o in offsets]
+    targets = [(place * 2 + inner, mp) for place in places]
+    last = count - 1
+
+    barrier = pltpu.get_barrier_semaphore()
+    for device in [peer, mate] + targets[:last]:
+        pl.semaphore_signal(barrier, inc=1, device_id=device, device_id_type=MESH)
+    pl.semaphore_wait(barrier, count + 1)
+
+    def remote(source, target, sems, index, device):
+        return pltpu.make_async_remote_copy(
+            src_ref=source,
+            dst_ref=target,
+            send_sem=sems[0].at[index],
+            recv_sem=sems[1].at[index],
+            device_id=device,
+            device_id_type=MESH,
+        )
+
+    def half_block(dp_index):
+        return lax.rem(dp_index // count + core, 2), lax.rem(dp_index, count)
+
+    crossing = []
+    for k, place in enumerate(places):
+        for own in range(2):
+            part, block = half_block(place * 2 + (inner if own else 1 - inner))
+            copy = remote(
+                send_ref.at[part, :, block], landed.at[2 * k + own], cross_sems, 2 * k + own, peer
+            )
+            copy.start()
+            crossing.append(copy)
+    stepping = {}
+    for k, place in enumerate(places):
+        stepping[0, k] = remote(
+            side_ref.at[:, place * 2 + 1 - inner], step_land.at[0, k], step_sems, k, mate
+        )
+        stepping[0, k].start()
+    going = []
+
+    def pass_on(group, k, value, final_ref):
+        stepping[group, k].wait()
+        total = value.astype(f32) + step_land[group, k].astype(f32)
+        if k == last:
+            final_ref[...] = total
+            return
+        far_send[group, k] = total.astype(bf16)
+        copy = remote(
+            far_send.at[group, k], far_land.at[group, k], far_sems, group * last + k, targets[k]
+        )
+        copy.start()
+        going.append((copy, final_ref, group, k))
+
+    for k, place in enumerate(places):
+        pass_on(0, k, side_ref[:, place * 2 + inner], side_out_ref)
+    for k, place in enumerate(places):
+        for own in range(2):
+            part, block = half_block(place * 2 + (inner if own else 1 - inner))
+            crossing[2 * k + own].wait()
+            total = keep_ref[part, :, block].astype(f32) + landed[2 * k + own].astype(f32)
+            if own:
+                mine[k] = total.astype(bf16)
+            else:
+                step_send[k] = total.astype(bf16)
+                stepping[1, k] = remote(
+                    step_send.at[k], step_land.at[1, k], step_sems, count + k, mate
+                )
+                stepping[1, k].start()
+        if k:
+            pass_on(1, k - 1, mine[k - 1], out_ref)
+    pass_on(1, last, mine[last], out_ref)
+    for copy, final_ref, group, k in going:
+        copy.wait()
+        final_ref[...] += far_land[group, k].astype(f32)
+
+
+def row_scatter(keep, send, side, dp_size):
+    _, mats, _, rows, columns = keep.shape
+    block = (mats, rows, columns)
+    count = dp_size // 2
+    whole = pl.BlockSpec(memory_space=pltpu.VMEM)
+    shape = jax.ShapeDtypeStruct(block, jnp.float32)
+    dma = pltpu.SemaphoreType.DMA
+    return pl.pallas_call(
+        functools.partial(row_scatter_kernel, dp_size),
+        out_shape=[shape, shape],
+        in_specs=[whole] * 3,
+        out_specs=[whole] * 2,
+        scratch_shapes=[
+            pltpu.VMEM((dp_size, *block), jnp.bfloat16),
+            pltpu.VMEM((count, *block), jnp.bfloat16),
+            pltpu.VMEM((count, *block), jnp.bfloat16),
+            pltpu.VMEM((2, count, *block), jnp.bfloat16),
+            pltpu.VMEM((2, count - 1, *block), jnp.bfloat16),
+            pltpu.VMEM((2, count - 1, *block), jnp.bfloat16),
+            dma((dp_size,)),
+            dma((dp_size,)),
+            dma((2 * count,)),
+            dma((2 * count,)),
+            dma((2 * (count - 1),)),
+            dma((2 * (count - 1),)),
+        ],
+        compiler_params=pltpu.CompilerParams(
+            collective_id=1, has_side_effects=True, vmem_limit_bytes=40 << 20
+        ),
+        name="row_scatter",
+    )(keep, send, side)
+
+
+def join_norm_kernel(place_ref, gain_ref, *refs):
+    pieces, (active_ref, normed_ref, scale_ref) = refs[:4], refs[4:]
+    depth = pieces[0].shape[0]
+    squares = sum(
+        jnp.sum(jnp.square(p[...].astype(jnp.float32)), axis=0, keepdims=True) for p in pieces
+    )
+    scale = lax.rsqrt(squares * (1.0 / (4 * depth)) + EPSILON)
+    scale_ref[...] = scale
+    for i, piece in enumerate(pieces):
+        quarter = place_ref[i]
+        value = piece[...]
+        active_ref[quarter] = value
+        normed = value.astype(jnp.float32) * scale * gain_ref[quarter]
+        normed_ref[i] = normed.astype(jnp.bfloat16)
+
+
+def join_norm(places, gain, pieces):
+    depth, length = pieces[0].shape
+    whole = pl.BlockSpec(memory_space=pltpu.VMEM)
+    full = jax.ShapeDtypeStruct((4, depth, length), jnp.bfloat16)
+    return pl.pallas_call(
+        join_norm_kernel,
+        out_shape=[full, full, jax.ShapeDtypeStruct((1, length), jnp.float32)],
+        in_specs=[pl.BlockSpec(memory_space=pltpu.SMEM)] + [whole] * 5,
+        out_specs=[whole] * 3,
+        cost_estimate=pl.CostEstimate(
+            flops=40 * depth * length, bytes_accessed=24 * depth * length, transcendentals=length
+        ),
+        name="join_norm",
+    )(places, gain, *pieces)
+
+
+def dot_tt(left, right):
+    return lax.dot_general(
+        left, right, (((0,), (1,)), ((), ())), preferred_element_type=jnp.float32
+    )
+
+
+def outer_kernel(sizes, *refs):
+    keep_ref, send_ref = refs[-2:]
+    at, row = 0, 0
+    for size in sizes:
+        near, far = refs[at][...], refs[at + 1][...]
+        for ref in refs[at + 2 : at + 2 + size]:
+            for low in range(0, ref.shape[0], 384):
+                block = ref[low : low + 384, :]
+                rows = slice(row, row + block.shape[0])
+                keep_ref[rows, :] = dot_nt(block, near).astype(jnp.bfloat16)
+                send_ref[rows, :] = dot_nt(block, far).astype(jnp.bfloat16)
+                row += block.shape[0]
+        at += 2 + size
+
+
+def outer_products(groups):
+    operands, sizes, rows, flops = [], [], 0, 0
+    for outer, inner in groups:
+        operands += [*inner, *outer]
+        sizes.append(len(outer))
+        rows += sum(o.shape[0] for o in outer)
+        flops += sum(4 * o.size * inner[0].shape[0] for o in outer)
+    columns = operands[0].shape[0]
+    whole = pl.BlockSpec(memory_space=pltpu.VMEM)
+    shape = jax.ShapeDtypeStruct((rows, columns), jnp.bfloat16)
+    return pl.pallas_call(
+        functools.partial(outer_kernel, tuple(sizes)),
+        out_shape=[shape, shape],
+        in_specs=[whole] * len(operands),
+        out_specs=[whole] * 2,
+        compiler_params=pltpu.CompilerParams(vmem_limit_bytes=32 << 20),
+        cost_estimate=pl.CostEstimate(
+            flops=flops,
+            bytes_accessed=sum(2 * o.size for o in operands) + 4 * rows * columns,
+            transcendentals=0,
+        ),
+        name="outer_products",
+    )(*operands)
+
+
+def self_products_kernel(core_ref, *refs):
+    grads, (norm_ref, near_own, near_mate, far_own, far_mate) = refs[:6], refs[6:11]
+    attn_ref, mix_near, mix_far, keep_ref, send_ref, into_ref = refs[11:]
+    core = core_ref[0]
+    for i, ref in enumerate(grads):
+        side, mat = i // 3, i % 3
+        grad = ref[...]
+        send_ref[side, mat] = dot_nt(grad, norm_ref[1]).astype(jnp.bfloat16)
+        keep_ref[side, mat] = dot_nt(grad, norm_ref[0]).astype(jnp.bfloat16)
+    for side in range(2):
+        place = core if side == 0 else 1 - core
+        grad = attn_ref[place]
+        send_ref[side, 3] = dot_nt(grad, mix_far[...]).astype(jnp.bfloat16)
+        keep_ref[side, 3] = dot_nt(grad, mix_near[...]).astype(jnp.bfloat16)
+    for mat in range(3):
+        joined = jnp.concatenate([grads[mat][...], grads[3 + mat][...]], axis=0)
+        for out, (own, mate) in enumerate(((near_own, near_mate), (far_own, far_mate))):
+            term = dot_nn(jnp.concatenate([own[mat], mate[mat]], axis=1), joined)
+            if mat == 0:
+                into_ref[out] = term
+            else:
+                into_ref[out] += term
+
+
+def self_products(grads, normed, weights, grad_attn, mixes, core):
+    half, length = grads[0].shape
+    depth = normed.shape[1]
+    whole = pl.BlockSpec(memory_space=pltpu.VMEM)
+    shape = jax.ShapeDtypeStruct((2, 4, half, depth), jnp.bfloat16)
+    operands = [*grads, normed, *weights, grad_attn, *mixes]
+    return pl.pallas_call(
+        self_products_kernel,
+        out_shape=[shape, shape, jax.ShapeDtypeStruct((2, depth, length), jnp.float32)],
+        in_specs=[pl.BlockSpec(memory_space=pltpu.SMEM)] + [whole] * len(operands),
+        out_specs=[whole] * 3,
+        compiler_params=pltpu.CompilerParams(vmem_limit_bytes=40 << 20),
+        cost_estimate=pl.CostEstimate(
+            flops=2 * 28 * half * length * depth,
+            bytes_accessed=sum(2 * o.size for o in operands) + 8 * depth * length,
+            transcendentals=0,
+        ),
+        name="self_products",
+    )(core, *operands)
+
+
+def paired_shards(
+    dp_size,
+    wide_state,
+    encoder,
+    segments,
+    key_valid,
+    self_qkv,
+    self_out,
+    cross_qkv,
+    cross_out,
+    ffn_in,
+    ffn_out,
+    norm_gains,
+    predict,
+    correct,
+    cotangent,
+):
+    bf16, f32 = jnp.bfloat16, jnp.float32
+    me = lax.axis_index("mp")
+    chip, core = me // 2, me % 2
+    far = me ^ 2
+    mates = [(i, i ^ 1) for i in range(4)]
+    peers = [(i, i ^ 2) for i in range(4)]
+
+    def to_mate(array):
+        return lax.ppermute(array, "mp", mates)
+
+    def to_peer(array):
+        return lax.ppermute(array, "mp", peers)
+
+    def quarters(own, across, axis=0):
+        pieces = [own, across, to_mate(own), to_mate(across)]
+        stacked = jnp.stack(pieces)
+        order = [pick(stacked, ((j % 2) ^ core) * 2 + ((j // 2) ^ chip)) for j in range(4)]
+        return jnp.concatenate(order, axis=axis)
+
+    def halves(own, axis=0):
+        other = to_mate(own)
+        return jnp.where(
+            core == 0,
+            jnp.concatenate([own, other], axis=axis),
+            jnp.concatenate([other, own], axis=axis),
+        )
+
+    def by_row(own, other):
+        return jnp.where(chip == 0, jnp.stack([own, other]), jnp.stack([other, own]))
+
+    def project(weights, values):
+        return dot_tn(weights, values)
+
+    length = wide_state.shape[3]
+    width = self_qkv.shape[2]
+    depth = self_qkv.shape[1]
+    half = width // 2
+    heads = half // HEAD
+    gains = norm_gains[:, :, None]
+
+    block_a = wide_state[:, 0].astype(f32)
+    block_b = wide_state[:, 1].astype(f32)
+    guess_a = predict[0, 0] * block_a + predict[0, 1] * block_b
+    guess_b = predict[1, 0] * block_a + predict[1, 1] * block_b
+    active_rows = guess_a.astype(bf16)
+    act_own = pick(active_rows, chip)
+    act_far = to_peer(pick(active_rows, 1 - chip))
+    qkv_far = to_peer(self_qkv)
+    act_pieces = [act_own, act_far, to_mate(act_own), to_mate(act_far)]
+    places = jnp.stack([me, far, me ^ 1, me ^ 3]).astype(jnp.int32)
+    active, normed_pieces, scale_a = join_norm(
+        places, norm_gains[0].reshape(4, depth, 1), act_pieces
+    )
+    active = active.reshape(width, length)
+    normed_a = normed_pieces.reshape(width, length)
+    self_out = after(self_out, qkv_far, act_far)
+    self_out_far = to_peer(self_out)
+    enc_far = to_peer(after(pick(encoder, 1 - chip), qkv_far, act_far))
+    cross_qkv_far = to_peer(after(cross_qkv, qkv_far, act_far))
+    cross_out_far = to_peer(after(cross_out, qkv_far, act_far))
+    cot_a = cotangent[:, 0].astype(f32)
+    cot_b = cotangent[:, 1].astype(f32)
+    grad_branch = (correct[0] * cot_a + correct[1] * cot_b).astype(bf16)
+    grad_far = to_peer(after(grad_branch, qkv_far, act_far))
+
+    def columns(array, which):
+        return lax.dynamic_slice_in_dim(array, which * half, half, array.ndim - 1)
+
+    own_near, own_far = columns(self_qkv, core), columns(qkv_far, core)
+    mate_near, mate_far = columns(self_qkv, 1 - core), columns(qkv_far, 1 - core)
+    w_qkv = jnp.concatenate([own_near, own_far, to_mate(mate_near), to_mate(mate_far)], axis=1)
+    w_self_out = quarters(self_out, self_out_far)
+    enc = quarters(pick(encoder, chip), enc_far)
+    w_cross = quarters(cross_qkv, cross_qkv_far, axis=1)
+    w_cross_out = quarters(cross_out, cross_out_far)
+    all_grad = quarters(grad_branch, grad_far, axis=1)
+    grad_own = pick(all_grad, chip)
+    grad_other = pick(all_grad, 1 - chip)
+
+    resid_a = active.astype(f32)
+    qkv = jnp.concatenate([project(w_qkv[i], normed_a).astype(bf16) for i in range(3)], axis=0)
+    seg_row = pick(segments, chip)
+    code = jnp.where(pick(key_valid, chip) > 0, seg_row, -1)
+    mask = (seg_row[None], jnp.broadcast_to(code[:, None], (length, 128)))
+    self_args = ((qkv, 0), (qkv, heads), (qkv, 2 * heads), heads, mask)
+    mix_own, self_log = attention_call(*self_args, None, 512)
+    self_mix = halves(mix_own)
+    attn_out = project(w_self_out, self_mix)
+
+    resid_b = resid_a + attn_out
+    scale_b = rms_scale(resid_b)
+    normed_b = (resid_b * scale_b * gains[1]).astype(bf16)
+    w_cross_own = columns(w_cross, core)
+    cross_q = project(w_cross_own[0], normed_b).astype(bf16)
+    cross_kv = jnp.concatenate(
+        [
+            lax.dot_general(
+                w_cross_own[i], enc, (((0,), (1,)), ((), ())), preferred_element_type=f32
+            ).astype(bf16)
+            for i in (1, 2)
+        ],
+        axis=0,
+    )
+    cross_args = ((cross_q, 0), (cross_kv, 0), (cross_kv, heads), heads, None)
+    cmix_own, cross_log = attention_call(*cross_args, None, 512)
+    cross_mix = halves(cmix_own)
+    cross_res = project(w_cross_out, cross_mix)
+    resid_c = resid_b + cross_res
+    scale_c = rms_scale(resid_c)
+    normed_own = (resid_c * scale_c * gains[2]).astype(bf16)
+    branch = (attn_out + cross_res).astype(bf16)
+
+    normed_half = lax.dynamic_slice_in_dim(normed_own, core * half, half, 0)
+    normed_other = halves(to_peer(normed_half))
+
+    def forward(normed):
+        gate_pre = project(ffn_in[0], normed)
+        up_pre = project(ffn_in[1], normed)
+        hidden = gated_unit(gate_pre, up_pre).astype(bf16)
+        return gate_pre, up_pre, hidden, project(ffn_out, hidden)
+
+    def backward(gate_pre, up_pre, grad_rows):
+        grad_hidden = dot_nn(ffn_out, grad_rows)
+        _, gate_back = jax.vjp(gated_unit, gate_pre, up_pre)
+        grad_gate, grad_up = (g.astype(bf16) for g in gate_back(grad_hidden))
+        back = dot_nn(ffn_in[0], grad_gate) + dot_nn(ffn_in[1], grad_up)
+        return grad_gate, grad_up, back
+
+    def my_half(part):
+        split = part.reshape(2, 2, depth, length)
+        got = to_mate(pick(split, 1 - core, 1).astype(bf16))
+        return pick(split, core, 1) + got.astype(f32)
+
+    gate_o, up_o, hid_o, res_o = forward(normed_own)
+    gg_o, gu_o, back_o = backward(gate_o, up_o, grad_own)
+    normed_other = after(normed_other, gg_o, gu_o, back_o)
+    gate_t, up_t, hid_t, res_t = forward(normed_other)
+    gg_t, gu_t, back_t = backward(gate_t, up_t, grad_other)
+
+    block = width // dp_size
+
+    def joined(mats):
+        return jnp.concatenate([m.reshape(dp_size, block, m.shape[1]) for m in mats], axis=1)
+
+    def scatter(rows):
+        out = lax.psum_scatter(rows, "dp", scatter_dimension=0, tiled=True)
+        return out.reshape(-1, block, out.shape[2]).astype(f32)
+
+    grad_in = [
+        (dot_nt(normed_own, own) + dot_nt(normed_other, other)).astype(bf16)
+        for own, other in ((gg_o, gg_t), (gu_o, gu_t))
+    ]
+    grad_out = (dot_nt(grad_own, hid_o) + dot_nt(grad_other, hid_t)).astype(bf16)
+    ffn_joined = joined(grad_in + [grad_out])
+    back_sent = my_half(back_t).astype(bf16)
+    back_far = to_peer(back_sent)
+    sum_o = my_half(res_o) + pick(branch.reshape(2, 2, depth, length), core, 1).astype(f32)
+    sum_t = my_half(res_t)
+    sum_sent = jnp.stack([pick(sum_o, 1 - chip), pick(sum_t, 1 - chip)]).astype(bf16)
+    back_far, ffn_joined, sum_sent = lax.optimization_barrier(
+        (back_far, ffn_joined, sum_sent)
+    )
+    back_half = my_half(back_o) + back_far.astype(f32)
+    back_mate = to_mate(back_half.astype(bf16)).astype(f32)
+    back_both = jnp.stack([back_half, back_mate])
+    grad_normed_c = jnp.stack([pick(back_both, core), pick(back_both, 1 - core)], axis=1).reshape(
+        width, length
+    )
+
+    ffn_parts = scatter(ffn_joined)
+
+    sum_far = to_peer(sum_sent)
+    branch_sum = by_row(
+        pick(sum_o, chip) + sum_far[1].astype(f32), pick(sum_t, chip) + sum_far[0].astype(f32)
+    )
+    new_state = jnp.stack(
+        [guess_a + correct[0] * branch_sum, guess_b + correct[1] * branch_sum], axis=1
+    ).astype(bf16)
+    grad_correct = jnp.stack([jnp.sum(cot_a * branch_sum), jnp.sum(cot_b * branch_sum)])
+
+
+    def rms_back(values, scale, gain, incoming):
+        inner = jnp.mean(gain * incoming * values, axis=0, keepdims=True)
+        return (
+            scale * gain * incoming - values * (scale * scale * scale) * inner,
+            jnp.sum(incoming * values * scale, axis=1),
+        )
+
+    def near_far(inner):
+        split = inner.reshape(4, depth, inner.shape[1])
+        return pick(split, me), pick(split, far)
+
+    grad_rows = grad_own.astype(f32)
+    grad_resid_c, gain_grad_c = rms_back(resid_c, scale_c, gains[2], grad_normed_c)
+    grad_cross_b = (grad_rows + grad_resid_c).astype(bf16)
+    cross_out_rows = lax.dynamic_slice_in_dim(w_cross_out, core * half, half, 0)
+    grad_cmix = dot_nn(cross_out_rows, grad_cross_b).astype(bf16)
+    gcq, gck, gcv = attention_call(*cross_args, (cross_log, cmix_own, grad_cmix), 512)
+    gcq_all, gck_all, gcv_all = halves(gcq), halves(gck), halves(gcv)
+    grad_normed_b = dot_nn(w_cross[0], gcq_all)
+    side_keep, side_send = outer_products(
+        (
+            ((gcq_all,), near_far(normed_b)),
+            ((gck_all, gcv_all), near_far(enc.T)),
+            ((grad_cross_b,), near_far(cross_mix)),
+        )
+    )
+    side_sum = (side_keep.astype(f32) + to_peer(side_send).astype(f32)).astype(bf16)
+    enc_rows = encoder.shape[1]
+
+    def encoder_grad(which):
+        keys = lax.dynamic_slice_in_dim(gck_all, which * enc_rows, enc_rows, 1)
+        values = lax.dynamic_slice_in_dim(gcv_all, which * enc_rows, enc_rows, 1)
+        return dot_tt(keys, w_cross[1]) + dot_tt(values, w_cross[2])
+
+    enc_got = to_peer(encoder_grad(far).astype(bf16)).astype(f32)
+    grad_encoder = by_row(encoder_grad(me), enc_got)
+
+    resid_b_part, gain_grad_b = rms_back(resid_b, scale_b, gains[1], grad_normed_b)
+    grad_resid_b = grad_resid_c + resid_b_part
+    grad_attn_b = (grad_rows + grad_resid_b).astype(bf16)
+    self_out_rows = lax.dynamic_slice_in_dim(w_self_out, core * half, half, 0)
+    grad_mix = dot_nn(self_out_rows, grad_attn_b).astype(bf16)
+    g_own = attention_call(*self_args, (self_log, mix_own, grad_mix), 256)
+    g_mate = [to_mate(g) for g in g_own]
+    keep, send, both_in = self_products(
+        (*g_own, *g_mate),
+        normed_pieces,
+        (own_near, mate_near, own_far, mate_far),
+        grad_attn_b.reshape(2, half, length),
+        near_far(self_mix),
+        core.astype(jnp.int32).reshape(1),
+    )
+    blocks = (2, 4, dp_size // 2, half // (dp_size // 2), depth)
+    self_parts, side_parts = row_scatter(
+        keep.reshape(blocks),
+        send.reshape(blocks),
+        side_sum.reshape(4, dp_size, block, depth),
+        dp_size,
+    )
+    both_act = jnp.stack([act_own, act_far]).astype(f32)
+    gain_a = norm_gains[0].reshape(4, depth)
+    both_gain = jnp.stack([pick(gain_a, me), pick(gain_a, far)])[:, :, None]
+    inner = jnp.sum(both_gain * both_in * both_act, axis=(0, 1))[None]
+    inner = (inner + to_mate(inner)) / width
+    split_b = grad_resid_b.reshape(4, depth, length)
+    both_b = jnp.stack([pick(split_b, me), pick(split_b, far)])
+    both_back = scale_a * both_gain * both_in - both_act * (scale_a * scale_a * scale_a) * inner
+    grad_active = (both_b + both_back).astype(bf16)
+    gain_sums = jnp.sum(both_in * both_act * scale_a, axis=2)
+    slot = jnp.arange(4, dtype=jnp.int32)[:, None]
+    gain_grad_a = (
+        jnp.where(slot == me, gain_sums[0][None], 0.0)
+        + jnp.where(slot == far, gain_sums[1][None], 0.0)
+    ).reshape(width)
+
+    grad_cols = by_row(grad_active[0], to_peer(grad_active[1])).astype(f32)
+    grad_guess_a = cot_a + grad_cols
+    grad_predict = jnp.stack(
+        [
+            jnp.sum(grad_guess_a * block_a),
+            jnp.sum(grad_guess_a * block_b),
+            jnp.sum(cot_b * block_a),
+            jnp.sum(cot_b * block_b),
+        ]
+    )
+    grad_state = jnp.stack(
+        [
+            predict[0, 0] * grad_guess_a + predict[1, 0] * cot_b,
+            predict[0, 1] * grad_guess_a + predict[1, 1] * cot_b,
+        ],
+        axis=1,
+    )
+    scalars = jnp.concatenate([grad_predict, grad_correct, jnp.zeros((width - 6,), f32)])
+    total = all_sum(
+        jnp.stack([gain_grad_a, 0.5 * gain_grad_b, 0.5 * gain_grad_c, scalars]), dp_size, 4
+    )
+
+    def columns_out(part):
+        return jnp.swapaxes(part, -1, -2)
+
+    return (
+        new_state,
+        grad_state,
+        grad_encoder,
+        columns_out(self_parts[:3]),
+        columns_out(self_parts[3]),
+        columns_out(side_parts[:3]),
+        columns_out(side_parts[3]),
+        ffn_parts[:2],
+        columns_out(ffn_parts[2]),
+        total[:3],
+        total[3, :4].reshape(2, 2),
+        total[3, 4:6],
+    )
+
+
+def choose(paired, dp_size, wide_state, *rest):
+    if paired and wide_state.shape[0] == 2:
+        return paired_shards(dp_size, wide_state, *rest)
+    return shards(wide_state, *rest)
+
+
 def solution(mesh):
     in_specs = (
         P("dp", None, "mp", None),
@@ -350,4 +1143,8 @@
         P(),
         P(),
     )
-    return jax.shard_map(shards, mesh=mesh, in_specs=in_specs, out_specs=out_specs, check_vma=False)
+    paired = mesh.shape["mp"] == 4
+    body = functools.partial(choose, paired, mesh.shape["dp"])
+    return jax.shard_map(
+        body, mesh=mesh, in_specs=in_specs, out_specs=out_specs, check_vma=False
+    )

time: 1170 us -> 395 us (0.34)
  waiting for transfers between devices: 661 us -> 66.9 us
  matrix products: 206 us -> 44.6 us
  Pallas kernels: 0 us -> 110 us
  local copies, waits for them, and re-layouts: 146 us -> 63.4 us
  blocking collectives: 40.3 us -> 0 us
  other arithmetic: 84.3 us -> 68.8 us
    reduce_scatter x7 -> x1, waiting for transfers between devices: 301 us -> 0.01 us  [scatter(): out = lax.psum_scatter(rows, 'dp', scatter_dimension=0, tiled=True)]
    unnamed x29 -> x1, waiting for transfers between devices: 191 us -> 0.02 us
    dot_general x33, matrix products: 206 us -> 44.6 us  [the longest x12 18.4 us: dot_tn(): lax.dot_general(left, right, (((0,), (0,)), ((), ())), preferred_element_...]
    all_gather x8 -> x0, waiting for transfers between devices: 127 us -> none  [the longest x1 44.1 us: shards(): lax.all_gather(self_proj[1:], 'mp', axis=2, tiled=True)]
    pallas_call x0 -> x9, Pallas kernels: none -> 110 us  [the longest x1 44.9 us: row_scatter(): pl.pallas_call(functools.partial(row_scatter_kernel, dp_size), out_shape=...]
    ppermute x0 -> x42, waiting for transfers between devices: none -> 66.9 us  [the longest x13 65.1 us: to_peer(): return lax.ppermute(array, 'mp', peers)]
    all_to_all x3 -> x0, waiting for transfers between devices: 41.9 us -> none  [the longest x1 24 us: shards(): lax.all_to_all(guess_a.astype(jnp.bfloat16), 'mp', split_axis=1, concat_a...]
    psum x1 -> x0, blocking collectives: 40.3 us -> none  [shards(): lax.psum((gain_grads, grad_predict, grad_correct), ('dp', 'mp'))]
  transfers between devices with their start and end apart: 25 -> 43, of which waited for: 16 -> 10; matrix products, arithmetic and copies ran while one was open for 32% -> 34% of each run, Pallas kernels for 0% -> 26%
where the time goes in v1:
time: 395 us; the launch traced here: 389 us
  Pallas kernels  110 us (28%)
  other arithmetic  68.8 us (17%)
  waiting for transfers between devices  66.9 us (17%)
  local copies, waits for them, and re-layouts  63.4 us (16%)
  matrix products  44.6 us (11%)
  starting transfers between devices  19 us (5%)
  between operations  16.3 us (4%)
    ppermute x13, waiting for transfers between devices, to_peer(): return lax.ppermute(array, 'mp', peers)  65.1 us
    pallas_call x1, Pallas kernels, row_scatter(): pl.pallas_call(functools.partial(row_scatter_kernel, dp_size), out_shape=...  44.9 us
    pallas_call x4, Pallas kernels, attention_call(): pl.pallas_call(functools.partial(kernel, mask is not None, size), grid=(h...  40.1 us
    unnamed x225, local copies, waits for them, and re-layouts  31.6 us
    dot_general x12, matrix products, dot_tn(): lax.dot_general(left, right, (((0,), (0,)), ((), ())), preferred_element_...  18.4 us
    dot_general x9, matrix products, dot_nn(): lax.dot_general(left, right, (((1,), (0,)), ((), ())), preferred_element_...  14.6 us
    ppermute x13, starting transfers between devices, to_peer(): return lax.ppermute(array, 'mp', peers)  12.3 us
    pallas_call x1, Pallas kernels, all_sum(): pl.pallas_call(functools.partial(all_sum_kernel, dp_size, mp_size), out_s...  10.4 us
  transfers between devices with their start and end apart: 43, of which 10 were waited for; matrix products, arithmetic and copies ran while one was open for 34% of the time, Pallas kernels for 26%

profile of v1, /device:TPU:0, one launch (start us, length us, event | category | flops | bytes accessed | tf_op | source)
XLA Modules:
  0.0 388.8 jit_solution(4219718607935514202)
XLA Ops:
  7.3 1.5 fusion.145
  8.7 3.0 fusion.41
  11.8 3.0 collective-permute-start
  17.4 3.9 %fusion.51 = bf16[2,192,1024]{2,1,0:T(8,128)(2,1)} fusion(f32[]{:T(128)} %bitcast.64, f32[]{:T(128)} %bitcast.2, bf16[2,2,192,1024]{3,2,1,0:T(8,128)(2,1)} %param.27), kind=kLoop, calls=%fused_computation.114 | loop fusion | flops 2359296 | bytes 2359304 | tf_op jit(solution)/shard_map/convert_element_type | solution.py:874
  22.0 3.9 %fusion.110 = bf16[1,2,192,1024]{3,2,1,0:T(8,128)(2,1)} fusion(f32[]{:T(128)} %bitcast.64, f32[]{:T(128)} %bitcast.2, bf16[2,2,192,1024]{3,2,1,0:T(8,128)(2,1)} %param.27), kind=kLoop, calls=%fused_computation.208 | loop fusion | flops 2359296 | bytes 2359304 | tf_op jit(solution)/shard_map/convert_element_type | solution.py:874
  28.4 14.6 %collective-permute-done.3 = bf16[3,192,768]{2,1,0:T(8,128)(2,1)} collective-permute-done((bf16[3,192,768]{2,1,0:T(8,128)(2,1)}, bf16[3,192,768]{2,1,0:T(8,128)(2,1)}, u32[]{:S(2)}, u32[]{:S(2)}) %collective-permute-start.3) | collective-permute-done | bytes 884768 | tf_op jit(solution)/shard_map/ppermute | solution.py:823
  43.0 1.7 collective-permute-start.16
  47.2 3.6 join_norm.1
  52.9 1.7 collective-permute-start.13
  56.1 4.9 %collective-permute-done.4 = bf16[192,768]{1,0:T(8,128)(2,1)S(1)} collective-permute-done((bf16[192,768]{1,0:T(8,128)(2,1)}, bf16[192,768]{1,0:T(8,128)(2,1)S(1)}, u32[]{:S(2)}, u32[]{:S(2)}) %collective-permute-start.4) | collective-permute-done | bytes 294944 | tf_op jit(solution)/shard_map/ppermute | solution.py:823
  65.8 8.9 %attend.2 = (bf16[384,1024]{1,0:T(8,128)(2,1)S(1)}, f32[6,1,1024]{2,1,0:T(1,128)S(1)}) custom-call(bf16[1152,1024]{1,0:T(8,128)(2,1)S(1)} %pad_maximum_fusion.7.refs_0_.refs_1_.refs_2_, bf16[1152,1024]{1,0:T(8,128)(2,1)S(1)} %pad_maximum_fusion.7.refs_0_.refs_1_.refs_2_, bf16[1152,1024]{1,0:T(8,128)(2,1)S(1)} %pad_maximum_fusion.7.refs_0_.refs_1_.refs_2_, ...), custom_call_target="tpu_custom_call" | custom-call | flops 3865470464 | bytes 3145728 | tf_op jit(solution)/shard_map/attend/pallas_call | solution.py:454
  75.4 11.0 %collective-permute-done.10 = bf16[192,768]{1,0:T(8,128)(2,1)} collective-permute-done((bf16[192,768]{1,0:T(8,128)(2,1)}, bf16[192,768]{1,0:T(8,128)(2,1)}, u32[]{:S(2)}, u32[]{:S(2)}) %collective-permute-start.10) | collective-permute-done | bytes 294944 | tf_op jit(solution)/shard_map/ppermute | solution.py:823
  93.2 9.0 %collective-permute-done.21 = bf16[2,192,1024]{2,1,0:T(8,128)(2,1)} collective-permute-done((bf16[2,192,1024]{2,1,0:T(8,128)(2,1)}, bf16[2,192,1024]{2,1,0:T(8,128)(2,1)}, u32[]{:S(2)}, u32[]{:S(2)}) %collective-permute-start.21) | collective-permute-done | bytes 786464 | tf_op jit(solution)/shard_map/ppermute | solution.py:823
  102.7 2.0 maximum_select_fusion
  104.9 1.7 multiply_reduce_fusion.3
  108.3 1.6 pad_maximum_fusion.3
  109.9 1.5 pad_maximum_fusion
  115.1 7.3 %attend.3 = (bf16[384,1024]{1,0:T(8,128)(2,1)S(1)}, f32[6,1,1024]{2,1,0:T(1,128)S(1)}) custom-call(bf16[384,1024]{1,0:T(8,128)(2,1)S(1)} %convolution_convert_fusion.2.refs_0_, bf16[768,512]{1,0:T(8,128)(2,1)S(1)} %pad_maximum_fusion.16.refs_1_.refs_2_, bf16[768,512]{1,0:T(8,128)(2,1)S(1)} %pad_maximum_fusion.16.refs_1_.refs_2_), custom_call_target="tpu_custom_call" | custom-call | flops 3221225472 | bytes 2359296 | tf_op jit(solution)/shard_map/attend/pallas_call | solution.py:454
  125.6 1.8 multiply_reduce_fusion.2
  133.6 4.2 %fusion.24 = (bf16[768,1024]{0,1:T(8,128)(2,1)S(1)}, bf16[768,1024]{0,1:T(8,128)(2,1)S(1)}, bf16[768,1024]{0,1:T(8,128)(2,1)S(1)}) fusion(f32[1024,768]{1,0:T(8,128)S(1)} %fusion.99, f32[1024,768]{1,0:T(8,128)S(1)} %fusion.91, bf16[768,768]{1,0:T(8,128)(2,1)S(1)} %copy-done, bf16[2,768,1024]{2,1,0:T(8,128)(2,1)S(1)} %pad_maximum_fusion.4, s32[]{:T(128)S(6)} %select_n.245), kind=kOutput, calls=%fused_computation.51 | convolution fusion | flops 1228406784 | bytes 13762564 | tf_op jit(solution)/shard_map/dot_general | solution.py:333
  146.8 6.4 %collective-permute-done.24 = bf16[384,1024]{1,0:T(8,128)(2,1)S(1)} collective-permute-done((bf16[384,1024]{1,0:T(8,128)(2,1)S(1)}, bf16[384,1024]{1,0:T(8,128)(2,1)S(1)}, u32[]{:S(2)}, u32[]{:S(2)}) %collective-permute-start.24) | collective-permute-done | bytes 786464 | tf_op jit(solution)/shard_map/ppermute | solution.py:823
  159.2 4.4 %fusion.23 = (bf16[768,1024]{0,1:T(8,128)(2,1)S(1)}, bf16[768,1024]{0,1:T(8,128)(2,1)S(1)}, bf16[768,1024]{0,1:T(8,128)(2,1)S(1)}) fusion(f32[1024,768]{1,0:T(8,128)S(1)} %fusion.95, f32[1024,768]{1,0:T(8,128)S(1)} %fusion.79, bf16[768,1024]{1,0:T(8,128)(2,1)S(1)} %maximum_select_fusion.2, bf16[2,768,768]{2,1,0:T(8,128)(2,1)S(1)} %copy-done.107), kind=kOutput, calls=%fused_computation.48 | convolution fusion | flops 1228406784 | bytes 13762560 | tf_op jit(solution)/shard_map/dot_general | solution.py:327
  175.4 2.1 pad_maximum_fusion.2
  177.6 2.0 bitcast_add_fusion.1
  181.8 12.2 %collective-permute-done.27 = bf16[2,192,1024]{2,1,0:T(8,128)(2,1)} collective-permute-done((bf16[2,192,1024]{2,1,0:T(8,128)(2,1)}, bf16[2,192,1024]{2,1,0:T(8,128)(2,1)}, u32[]{:S(2)}, u32[]{:S(2)}) %collective-permute-start.27) | collective-permute-done | bytes 786464 | tf_op jit(solution)/shard_map/ppermute | solution.py:823
  194.0 3.2 fusion.121
  212.9 10.2 %attend_back.2 = (bf16[384,1024]{1,0:T(8,128)(2,1)S(1)}, bf16[384,512]{1,0:T(8,128)(2,1)S(1)}, bf16[384,512]{1,0:T(8,128)(2,1)S(1)}) custom-call(bf16[384,1024]{1,0:T(8,128)(2,1)S(1)} %copy-done.33, bf16[768,512]{1,0:T(8,128)(2,1)S(1)} %pad_maximum_fusion.16.refs_1_.refs_2_, bf16[768,512]{1,0:T(8,128)(2,1)S(1)} %pad_maximum_fusion.16.refs_1_.refs_2_, ...), custom_call_target="tpu_custom_call" | custom-call | flops 8053063680 | bytes 5898240 | tf_op jit(solution)/shard_map/attend_back/pallas_call | solution.py:454
  224.5 4.5 %fusion.45 = (bf16[2,1,192,1024]{3,2,0,1:T(8,128)(2,1)S(1)}, bf16[2,1,192,1024]{3,2,0,1:T(8,128)(2,1)S(1)}) fusion(f32[1,1,192,1024]{3,2,0,1:T(8,128)S(1)} %bitcast.511, f32[1,1,192,1024]{3,2,0,1:T(8,128)S(1)} %bitcast.510, f32[]{:T(128)} %bitcast.2, f32[]{:T(128)} %bitcast.1, f32[]{:T(128)} %bitcast, pred[]{:T(512)S(6)} %eq.37, ...), kind=kLoop, calls=%fused_computation.108 | loop fusion | flops 6684672 | bytes 4718617 | tf_op jit(solution)/shard_map/convert.8
  234.2 1.8 collective-permute-start.40
  238.9 1.8 multiply_reduce_fusion
  240.7 3.4 fusion.1
  246.7 13.8 %attend_back.3 = (bf16[384,1024]{1,0:T(8,128)(2,1)}, bf16[384,1024]{1,0:T(8,128)(2,1)}, bf16[384,1024]{1,0:T(8,128)(2,1)}) custom-call(bf16[1152,1024]{1,0:T(8,128)(2,1)S(1)} %copy-done.3, bf16[1152,1024]{1,0:T(8,128)(2,1)S(1)} %copy-done.3, bf16[1152,1024]{1,0:T(8,128)(2,1)S(1)} %copy-done.3, s32[1,1024]{1,0:T(1,128)S(1)} %copy-done.29, ...), custom_call_target="tpu_custom_call" | custom-call | flops 9663676416 | bytes 7864320 | tf_op jit(solution)/shard_map/attend_back/pallas_call | solution.py:454
  262.1 2.6 outer_products.1
  265.9 1.5 copy.82
  267.9 2.8 constant_dynamic-slice_fusion.3
  272.2 8.2 %self_products.1 = (bf16[2,4,384,192]{3,2,1,0:T(8,128)(2,1)S(1)}, bf16[2,4,384,192]{3,2,1,0:T(8,128)(2,1)S(1)}, f32[2,192,1024]{2,1,0:T(8,128)S(1)}) custom-call(s32[1]{0:T(128)} %bitcast.111.core_ref, bf16[384,1024]{1,0:T(8,128)(2,1)} %get-tuple-element.57.refs_0_, bf16[384,1024]{1,0:T(8,128)(2,1)} %get-tuple-element.58.refs_1_, ...), custom_call_target="tpu_custom_call" | custom-call | flops 4227858432 | bytes 11993088 | tf_op jit(solution)/shard_map/self_products/pallas_call | solution.py:780
  282.8 1.6 fusion.61
  285.7 1.6 fusion.58
  288.5 1.7 collective-permute-start.37
  290.2 6.5 %collective-permute-done.41 = bf16[3072,192]{0,1:T(8,128)(2,1)} collective-permute-done((bf16[3072,192]{0,1:T(8,128)(2,1)}, bf16[3072,192]{0,1:T(8,128)(2,1)}, u32[]{:S(2)}, u32[]{:S(2)}) %collective-permute-start.41) | collective-permute-done | bytes 1179680 | tf_op jit(solution)/shard_map/ppermute | solution.py:823
  296.6 2.8 copy.83
  299.4 2.0 add_convert_fusion
  301.8 44.9 %row_scatter.1 = (f32[4,96,192]{2,1,0:T(8,128)S(1)}, f32[4,96,192]{2,1,0:T(8,128)S(1)}) custom-call(bf16[2,4,4,96,192]{4,3,2,1,0:T(8,128)(2,1)S(1)} %bitcast.504, bf16[2,4,4,96,192]{4,3,2,1,0:T(8,128)(2,1)S(1)} %bitcast.505, bf16[4,8,96,192]{3,2,1,0:T(8,128)(2,1)S(1)} %bitcast.503), custom_call_target="tpu_custom_call" | custom-call | tf_op jit(solution)/shard_map/row_scatter/pallas_call | solution.py:646
  350.0 4.2 %fusion.65 = (f32[2,1,192,1024]{3,2,0,1:T(8,128)S(1)}, f32[2,1,192,1024]{3,2,0,1:T(8,128)S(1)}) fusion(f32[]{:T(128)} %bitcast.97, f32[]{:T(128)} %bitcast, bf16[2,2,192,1024]{3,2,1,0:T(8,128)(2,1)S(1)} %copy-done.38, bf16[1,1,192,1024]{3,2,0,1:T(8,128)(2,1)S(1)} %copy-done.74, bf16[1,1,192,1024]{3,2,0,1:T(8,128)(2,1)} %bitcast.122, pred[]{:T(512)S(6)} %eq.37, ...), kind=kLoop, calls=%fused_computation.128 | loop fusion | flops 5111808 | bytes 5505041 | tf_op jit(solution)/shard_map/add | solution.py:1080
  354.7 1.9 copy.85
  357.7 2.8 fusion.64
  360.5 3.9 %concatenate.125 = f32[768]{0:T(1024)S(1)} concatenate(f32[1]{0:T(128)} %bitcast.153, f32[1]{0:T(128)} %bitcast.154, f32[1]{0:T(128)} %bitcast.155, f32[1]{0:T(128)} %bitcast.156, f32[1]{0:T(128)} %bitcast.157, f32[1]{0:T(128)} %bitcast.158, f32[762]{0:T(1024)S(1)} %broadcast_in_dim.73), dimensions={0} | concatenate | bytes 6144 | tf_op jit(solution)/shard_map/concatenate | solution.py:1085
  365.0 10.4 %all_sum.1 = f32[4,768]{1,0:T(4,128)} custom-call(f32[4,768]{1,0:T(4,128)} %pad_maximum_fusion.19.part_ref), custom_call_target="tpu_custom_call" | custom-call | tf_op jit(solution)/shard_map/all_sum/pallas_call | solution.py:533
  (414 shorter events, 116.5 us)
Async XLA Ops:
  7.2 116.2 %copy-start = (bf16[768,768]{1,0:T(8,128)(2,1)S(1)}, bf16[768,768]{1,0:T(8,128)(2,1)}, u32[]{:S(2)}) copy-start(bf16[768,768]{1,0:T(8,128)(2,1)} %param.23) | copy-start | bytes 3538948
  7.2 370.9 %reduce-scatter.2.cloned.1.call-start = ((), (), s32[]{:S(2)}) async-start(), calls=%async_computation.1 | async-start | bytes 3981312 | tf_op jit(solution)/shard_map/reduce_scatter | solution.py:957
  11.8 14.1 %collective-permute-start = (bf16[192,1024]{1,0:T(8,128)(2,1)S(1)}, bf16[192,1024]{1,0:T(8,128)(2,1)}, u32[]{:S(2)}, u32[]{:S(2)}) collective-permute-start(bf16[192,1024]{1,0:T(8,128)(2,1)S(1)} %get-tuple-element.201), channel_id=1, source_target_pairs={{0,2},{1,3},{2,0},{3,1},{4,6},{5,7},{6,4},{7,5},{8,10},{9,11},{10,... | collective-permute-start | bytes 1179656 | tf_op jit(solution)/shard_map/ppermute | solution.py:823
  14.8 31.8 %collective-permute-start.1 = (bf16[192,1024]{1,0:T(8,128)(2,1)S(1)}, bf16[192,1024]{1,0:T(8,128)(2,1)}, u32[]{:S(2)}, u32[]{:S(2)}) collective-permute-start(bf16[192,1024]{1,0:T(8,128)(2,1)S(1)} %bitcast.513), channel_id=1, source_target_pairs={{0,1},{1,0},{2,3},{3,2},{4,5},{5,4},{6,7},{7,6},{8,9},{9,8},{10,11... | collective-permute-start | bytes 1179656 | tf_op jit(solution)/shard_map/ppermute | solution.py:820
  14.9 28.2 %collective-permute-start.3 = (bf16[3,192,768]{2,1,0:T(8,128)(2,1)}, bf16[3,192,768]{2,1,0:T(8,128)(2,1)}, u32[]{:S(2)}, u32[]{:S(2)}) collective-permute-start(bf16[3,192,768]{2,1,0:T(8,128)(2,1)} %param.18), channel_id=1, source_target_pairs={{0,2},{1,3},{2,0},{3,1},{4,6},{5,7},{6,4},{7,5},{8,10},{9,11},{10,... | collective-permute-start | bytes 2654216 | tf_op jit(solution)/shard_map/ppermute | solution.py:823
  16.3 45.0 %copy-start.4 = (bf16[3,192,384]{2,1,0:T(8,128)(2,1)}, bf16[3,192,384]{2,1,0:T(8,128)(2,1)S(1)}, u32[]{:S(2)}) copy-start(bf16[3,192,384]{2,1,0:T(8,128)(2,1)S(1)} %get-tuple-element.186.refs_7_) | copy-start | bytes 1327108
  16.3 39.4 %collective-permute-start.7 = (bf16[3,192,384]{2,1,0:T(8,128)(2,1)S(1)}, bf16[3,192,384]{2,1,0:T(8,128)(2,1)}, u32[]{:S(2)}, u32[]{:S(2)}) collective-permute-start(bf16[3,192,384]{2,1,0:T(8,128)(2,1)S(1)} %get-tuple-element.187.refs_8_), channel_id=1, source_target_pairs={{0,1},{1,0},{2,3},{3,2},{4,5},{5,4},{6,7},{7,6},{8,9},{9,8},{10,11... | collective-permute-start | bytes 1327112 | tf_op jit(solution)/shard_map/ppermute | solution.py:820
  22.0 43.7 %copy-start.28 = (s32[1,1024]{1,0:T(1,128)}, s32[1,1024]{1,0:T(1,128)S(1)}, u32[]{:S(2)}) copy-start(s32[1,1024]{1,0:T(1,128)S(1)} %get-tuple-element.142.refs_3_) | copy-start | bytes 12292
  25.9 21.3 %collective-permute-start.2 = (bf16[192,1024]{1,0:T(8,128)(2,1)}, bf16[192,1024]{1,0:T(8,128)(2,1)}, u32[]{:S(2)}, u32[]{:S(2)}) collective-permute-start(bf16[192,1024]{1,0:T(8,128)(2,1)} %collective-permute-done.refs_1_), channel_id=1, source_target_pairs={{0,1},{1,0},{2,3},{3,2},{4,5},{5,4},{6,7},{7,6},{8,9},{9,8},{10,11... | collective-permute-start | bytes 1179656 | tf_op jit(solution)/shard_map/ppermute | solution.py:820
  43.0 8.1 %collective-permute-start.16 = (bf16[128,768]{1,0:T(8,128)(2,1)}, bf16[128,768]{1,0:T(8,128)(2,1)}, u32[]{:S(2)}, u32[]{:S(2)}) collective-permute-start(bf16[128,768]{1,0:T(8,128)(2,1)} %get-tuple-element.47), channel_id=1, source_target_pairs={{0,2},{1,3},{2,0},{3,1},{4,6},{5,7},{6,4},{7,5},{8,10},{9,11},{10,... | collective-permute-start | bytes 589832 | tf_op jit(solution)/shard_map/ppermute | solution.py:823
  46.0 15.2 %collective-permute-start.8 = (bf16[3,192,384]{2,1,0:T(8,128)(2,1)S(1)}, bf16[3,192,384]{2,1,0:T(8,128)(2,1)}, u32[]{:S(2)}, u32[]{:S(2)}) collective-permute-start(bf16[3,192,384]{2,1,0:T(8,128)(2,1)S(1)} %get-tuple-element.189.refs_10_), channel_id=1, source_target_pairs={{0,1},{1,0},{2,3},{3,2},{4,5},{5,4},{6,7},{7,6},{8,9},{9,8},{10,11... | collective-permute-start | bytes 1327112 | tf_op jit(solution)/shard_map/ppermute | solution.py:820
  46.7 5.7 %collective-permute-start.17 = (bf16[128,768]{1,0:T(8,128)(2,1)S(1)}, bf16[128,768]{1,0:T(8,128)(2,1)S(1)}, u32[]{:S(2)}, u32[]{:S(2)}) collective-permute-start(bf16[128,768]{1,0:T(8,128)(2,1)S(1)} %bitcast.536), channel_id=1, source_target_pairs={{0,1},{1,0},{2,3},{3,2},{4,5},{5,4},{6,7},{7,6},{8,9},{9,8},{10,11... | collective-permute-start | bytes 589832 | tf_op jit(solution)/shard_map/ppermute | solution.py:820
  50.8 10.1 %collective-permute-start.4 = (bf16[192,768]{1,0:T(8,128)(2,1)}, bf16[192,768]{1,0:T(8,128)(2,1)S(1)}, u32[]{:S(2)}, u32[]{:S(2)}) collective-permute-start(bf16[192,768]{1,0:T(8,128)(2,1)} %param.19), channel_id=1, source_target_pairs={{0,2},{1,3},{2,0},{3,1},{4,6},{5,7},{6,4},{7,5},{8,10},{9,11},{10,... | collective-permute-start | bytes 884744 | tf_op jit(solution)/shard_map/ppermute | solution.py:823
  51.1 1.8 collective-permute-start.18
  52.4 22.2 %collective-permute-start.5 = (bf16[192,768]{1,0:T(8,128)(2,1)}, bf16[192,768]{1,0:T(8,128)(2,1)S(1)}, u32[]{:S(2)}, u32[]{:S(2)}) collective-permute-start(bf16[192,768]{1,0:T(8,128)(2,1)} %param.19), channel_id=1, source_target_pairs={{0,1},{1,0},{2,3},{3,2},{4,5},{5,4},{6,7},{7,6},{8,9},{9,8},{10,11... | collective-permute-start | bytes 884744 | tf_op jit(solution)/shard_map/ppermute | solution.py:820
  52.9 49.3 %collective-permute-start.13 = (bf16[3,192,768]{2,1,0:T(8,128)(2,1)}, bf16[3,192,768]{2,1,0:T(8,128)(2,1)}, u32[]{:S(2)}, u32[]{:S(2)}) collective-permute-start(bf16[3,192,768]{2,1,0:T(8,128)(2,1)} %param.20), channel_id=1, source_target_pairs={{0,2},{1,3},{2,0},{3,1},{4,6},{5,7},{6,4},{7,5},{8,10},{9,11},{10,... | collective-permute-start | bytes 2654216 | tf_op jit(solution)/shard_map/ppermute | solution.py:823
  55.7 30.6 %collective-permute-start.10 = (bf16[192,768]{1,0:T(8,128)(2,1)}, bf16[192,768]{1,0:T(8,128)(2,1)}, u32[]{:S(2)}, u32[]{:S(2)}) collective-permute-start(bf16[192,768]{1,0:T(8,128)(2,1)} %param.21), channel_id=1, source_target_pairs={{0,2},{1,3},{2,0},{3,1},{4,6},{5,7},{6,4},{7,5},{8,10},{9,11},{10,... | collective-permute-start | bytes 884744 | tf_op jit(solution)/shard_map/ppermute | solution.py:823
  60.9 41.3 %collective-permute-start.21 = (bf16[2,192,1024]{2,1,0:T(8,128)(2,1)}, bf16[2,192,1024]{2,1,0:T(8,128)(2,1)}, u32[]{:S(2)}, u32[]{:S(2)}) collective-permute-start(bf16[2,192,1024]{2,1,0:T(8,128)(2,1)} %fusion.51), channel_id=1, source_target_pairs={{0,2},{1,3},{2,0},{3,1},{4,6},{5,7},{6,4},{7,5},{8,10},{9,11},{10,... | collective-permute-start | bytes 2359304 | tf_op jit(solution)/shard_map/ppermute | solution.py:823
  61.2 25.1 %collective-permute-start.6 = (bf16[192,768]{1,0:T(8,128)(2,1)S(1)}, bf16[192,768]{1,0:T(8,128)(2,1)S(1)}, u32[]{:S(2)}, u32[]{:S(2)}) collective-permute-start(bf16[192,768]{1,0:T(8,128)(2,1)S(1)} %collective-permute-done.4), channel_id=1, source_target_pairs={{0,1},{1,0},{2,3},{3,2},{4,5},{5,4},{6,7},{7,6},{8,9},{9,8},{10,11... | collective-permute-start | bytes 884744 | tf_op jit(solution)/shard_map/ppermute | solution.py:820
  74.7 28.0 %collective-permute-start.9 = (bf16[384,1024]{1,0:T(8,128)(2,1)S(1)}, bf16[384,1024]{1,0:T(8,128)(2,1)}, u32[]{:S(2)}, u32[]{:S(2)}) collective-permute-start(bf16[384,1024]{1,0:T(8,128)(2,1)S(1)} %get-tuple-element.44.refs_6_), channel_id=1, source_target_pairs={{0,1},{1,0},{2,3},{3,2},{4,5},{5,4},{6,7},{7,6},{8,9},{9,8},{10,11... | collective-permute-start | bytes 2359304 | tf_op jit(solution)/shard_map/ppermute | solution.py:820
  86.3 3.5 collective-permute-start.11
  86.3 5.4 %collective-permute-start.12 = (bf16[192,768]{1,0:T(8,128)(2,1)}, bf16[192,768]{1,0:T(8,128)(2,1)}, u32[]{:S(2)}, u32[]{:S(2)}) collective-permute-start(bf16[192,768]{1,0:T(8,128)(2,1)} %collective-permute-done.10), channel_id=1, source_target_pairs={{0,1},{1,0},{2,3},{3,2},{4,5},{5,4},{6,7},{7,6},{8,9},{9,8},{10,11... | collective-permute-start | bytes 884744 | tf_op jit(solution)/shard_map/ppermute | solution.py:820
  91.2 18.7 %collective-permute-start.14 = (bf16[3,192,768]{2,1,0:T(8,128)(2,1)S(1)}, bf16[3,192,768]{2,1,0:T(8,128)(2,1)S(1)}, u32[]{:S(2)}, u32[]{:S(2)}) collective-permute-start(bf16[3,192,768]{2,1,0:T(8,128)(2,1)S(1)} %copy-done.86), channel_id=1, source_target_pairs={{0,1},{1,0},{2,3},{3,2},{4,5},{5,4},{6,7},{7,6},{8,9},{9,8},{10,11... | collective-permute-start | bytes 2654216 | tf_op jit(solution)/shard_map/ppermute | solution.py:820
  91.7 15.3 %collective-permute-start.22 = (bf16[2,192,1024]{2,1,0:T(8,128)(2,1)}, bf16[2,192,1024]{2,1,0:T(8,128)(2,1)S(1)}, u32[]{:S(2)}, u32[]{:S(2)}) collective-permute-start(bf16[2,192,1024]{2,1,0:T(8,128)(2,1)} %fusion.51), channel_id=1, source_target_pairs={{0,1},{1,0},{2,3},{3,2},{4,5},{5,4},{6,7},{7,6},{8,9},{9,8},{10,11... | collective-permute-start | bytes 2359304 | tf_op jit(solution)/shard_map/ppermute | solution.py:820
  93.2 32.4 %copy-start.65 = (bf16[192,768]{1,0:T(8,128)(2,1)}, bf16[192,768]{1,0:T(8,128)(2,1)S(1)}, u32[]{:S(2)}) copy-start(bf16[192,768]{1,0:T(8,128)(2,1)S(1)} %get-tuple-element.181) | copy-start | bytes 884740
  102.2 4.8 %collective-permute-start.23 = (bf16[2,192,1024]{2,1,0:T(8,128)(2,1)}, bf16[2,192,1024]{2,1,0:T(8,128)(2,1)S(1)}, u32[]{:S(2)}, u32[]{:S(2)}) collective-permute-start(bf16[2,192,1024]{2,1,0:T(8,128)(2,1)} %collective-permute-done.21), channel_id=1, source_target_pairs={{0,1},{1,0},{2,3},{3,2},{4,5},{5,4},{6,7},{7,6},{8,9},{9,8},{10,11... | collective-permute-start | bytes 2359304 | tf_op jit(solution)/shard_map/ppermute | solution.py:820
  102.2 7.7 %collective-permute-start.15 = (bf16[3,192,768]{2,1,0:T(8,128)(2,1)}, bf16[3,192,768]{2,1,0:T(8,128)(2,1)S(1)}, u32[]{:S(2)}, u32[]{:S(2)}) collective-permute-start(bf16[3,192,768]{2,1,0:T(8,128)(2,1)} %collective-permute-done.13), channel_id=1, source_target_pairs={{0,1},{1,0},{2,3},{3,2},{4,5},{5,4},{6,7},{7,6},{8,9},{9,8},{10,11... | collective-permute-start | bytes 2654216 | tf_op jit(solution)/shard_map/ppermute | solution.py:820
  122.4 2.5 collective-permute-start.19
  123.4 50.6 %copy-start.43 = (bf16[2,768,1024]{2,1,0:T(8,128)(2,1)}, bf16[2,768,1024]{2,1,0:T(8,128)(2,1)S(1)}, u32[]{:S(2)}) copy-start(bf16[2,768,1024]{2,1,0:T(8,128)(2,1)S(1)} %pad_maximum_fusion.4) | copy-start | bytes 9437188
  133.2 20.0 %collective-permute-start.24 = (bf16[384,1024]{1,0:T(8,128)(2,1)S(1)}, bf16[384,1024]{1,0:T(8,128)(2,1)S(1)}, u32[]{:S(2)}, u32[]{:S(2)}) collective-permute-start(bf16[384,1024]{1,0:T(8,128)(2,1)S(1)} %constant_dynamic-slice_fusion.4), channel_id=1, source_target_pairs={{0,2},{1,3},{2,0},{3,1},{4,6},{5,7},{6,4},{7,5},{8,10},{9,11},{10,... | collective-permute-start | bytes 2359304 | tf_op jit(solution)/shard_map/ppermute | solution.py:823
  139.4 15.2 %collective-permute-start.20 = (bf16[2,192,1024]{2,1,0:T(8,128)(2,1)S(1)}, bf16[2,192,1024]{2,1,0:T(8,128)(2,1)S(1)}, u32[]{:S(2)}, u32[]{:S(2)}) collective-permute-start(bf16[2,192,1024]{2,1,0:T(8,128)(2,1)S(1)} %fusion.107), channel_id=1, source_target_pairs={{0,1},{1,0},{2,3},{3,2},{4,5},{5,4},{6,7},{7,6},{8,9},{9,8},{10,11... | collective-permute-start | bytes 2359304 | tf_op jit(solution)/shard_map/ppermute | solution.py:820
  145.2 48.8 %collective-permute-start.30 = (bf16[2,192,1024]{2,1,0:T(8,128)(2,1)}, bf16[2,192,1024]{2,1,0:T(8,128)(2,1)}, u32[]{:S(2)}, u32[]{:S(2)}) collective-permute-start(bf16[2,192,1024]{2,1,0:T(8,128)(2,1)} %fusion.106), channel_id=1, source_target_pairs={{0,1},{1,0},{2,3},{3,2},{4,5},{5,4},{6,7},{7,6},{8,9},{9,8},{10,11... | collective-permute-start | bytes 2359304 | tf_op jit(solution)/shard_map/ppermute | solution.py:820
  153.2 3.8 collective-permute-start.25
  166.1 11.4 %collective-permute-start.28 = (bf16[2,192,1024]{2,1,0:T(8,128)(2,1)}, bf16[2,192,1024]{2,1,0:T(8,128)(2,1)}, u32[]{:S(2)}, u32[]{:S(2)}) collective-permute-start(bf16[2,192,1024]{2,1,0:T(8,128)(2,1)} %fusion.109), channel_id=1, source_target_pairs={{0,1},{1,0},{2,3},{3,2},{4,5},{5,4},{6,7},{7,6},{8,9},{9,8},{10,11... | collective-permute-start | bytes 2359304 | tf_op jit(solution)/shard_map/ppermute | solution.py:820
  169.6 2.9 collective-permute-start.26
  173.7 20.3 %collective-permute-start.27 = (bf16[2,192,1024]{2,1,0:T(8,128)(2,1)}, bf16[2,192,1024]{2,1,0:T(8,128)(2,1)}, u32[]{:S(2)}, u32[]{:S(2)}) collective-permute-start(bf16[2,192,1024]{2,1,0:T(8,128)(2,1)} %fusion.72), channel_id=1, source_target_pairs={{0,2},{1,3},{2,0},{3,1},{4,6},{5,7},{6,4},{7,5},{8,10},{9,11},{10,... | collective-permute-start | bytes 2359304 | tf_op jit(solution)/shard_map/ppermute | solution.py:823
  197.2 6.8 %collective-permute-start.31 = (bf16[2,192,1024]{2,1,0:T(8,128)(2,1)}, bf16[2,192,1024]{2,1,0:T(8,128)(2,1)}, u32[]{:S(2)}, u32[]{:S(2)}) collective-permute-start(bf16[2,192,1024]{2,1,0:T(8,128)(2,1)} %get-tuple-element.149), channel_id=1, source_target_pairs={{0,1},{1,0},{2,3},{3,2},{4,5},{5,4},{6,7},{7,6},{8,9},{9,8},{10,11... | collective-permute-start | bytes 2359304 | tf_op jit(solution)/shard_map/ppermute | solution.py:820
  203.6 20.1 %collective-permute-start.29 = (bf16[2,192,1024]{2,1,0:T(8,128)(2,1)}, bf16[2,192,1024]{2,1,0:T(8,128)(2,1)S(1)}, u32[]{:S(2)}, u32[]{:S(2)}) collective-permute-start(bf16[2,192,1024]{2,1,0:T(8,128)(2,1)} %pad_maximum_fusion.17), channel_id=1, source_target_pairs={{0,2},{1,3},{2,0},{3,1},{4,6},{5,7},{6,4},{7,5},{8,10},{9,11},{10,... | collective-permute-start | bytes 2359304 | tf_op jit(solution)/shard_map/ppermute | solution.py:823
  223.1 7.9 %collective-permute-start.39 = (bf16[384,512]{1,0:T(8,128)(2,1)S(1)}, bf16[384,512]{1,0:T(8,128)(2,1)S(1)}, u32[]{:S(2)}, u32[]{:S(2)}) collective-permute-start(bf16[384,512]{1,0:T(8,128)(2,1)S(1)} %get-tuple-element.62), channel_id=1, source_target_pairs={{0,1},{1,0},{2,3},{3,2},{4,5},{5,4},{6,7},{7,6},{8,9},{9,8},{10,11... | collective-permute-start | bytes 1179656 | tf_op jit(solution)/shard_map/ppermute | solution.py:820
  230.5 6.5 %collective-permute-start.32 = (bf16[384,1024]{1,0:T(8,128)(2,1)S(1)}, bf16[384,1024]{1,0:T(8,128)(2,1)S(1)}, u32[]{:S(2)}, u32[]{:S(2)}) collective-permute-start(bf16[384,1024]{1,0:T(8,128)(2,1)S(1)} %get-tuple-element.54), channel_id=1, source_target_pairs={{0,1},{1,0},{2,3},{3,2},{4,5},{5,4},{6,7},{7,6},{8,9},{9,8},{10,11... | collective-permute-start | bytes 2359304 | tf_op jit(solution)/shard_map/ppermute | solution.py:820
  230.6 2.7 collective-permute-start.38
  234.2 27.0 %collective-permute-start.40 = (bf16[128,768]{1,0:T(8,128)(2,1)S(1)}, bf16[128,768]{1,0:T(8,128)(2,1)S(1)}, u32[]{:S(2)}, u32[]{:S(2)}) collective-permute-start(bf16[128,768]{1,0:T(8,128)(2,1)S(1)} %fusion.101), channel_id=1, source_target_pairs={{0,2},{1,3},{2,0},{3,1},{4,6},{5,7},{6,4},{7,5},{8,10},{9,11},{10,... | collective-permute-start | bytes 589832 | tf_op jit(solution)/shard_map/ppermute | solution.py:823
  260.5 10.2 %collective-permute-start.33 = (bf16[384,1024]{1,0:T(8,128)(2,1)}, bf16[384,1024]{1,0:T(8,128)(2,1)}, u32[]{:S(2)}, u32[]{:S(2)}) collective-permute-start(bf16[384,1024]{1,0:T(8,128)(2,1)} %get-tuple-element.57.refs_0_), channel_id=1, source_target_pairs={{0,1},{1,0},{2,3},{3,2},{4,5},{5,4},{6,7},{7,6},{8,9},{9,8},{10,11... | collective-permute-start | bytes 2359304 | tf_op jit(solution)/shard_map/ppermute | solution.py:820
  260.6 10.1 %collective-permute-start.34 = (bf16[384,1024]{1,0:T(8,128)(2,1)}, bf16[384,1024]{1,0:T(8,128)(2,1)}, u32[]{:S(2)}, u32[]{:S(2)}) collective-permute-start(bf16[384,1024]{1,0:T(8,128)(2,1)} %get-tuple-element.58.refs_1_), channel_id=1, source_target_pairs={{0,1},{1,0},{2,3},{3,2},{4,5},{5,4},{6,7},{7,6},{8,9},{9,8},{10,11... | collective-permute-start | bytes 2359304 | tf_op jit(solution)/shard_map/ppermute | solution.py:820
  261.1 9.6 %collective-permute-start.35 = (bf16[384,1024]{1,0:T(8,128)(2,1)}, bf16[384,1024]{1,0:T(8,128)(2,1)}, u32[]{:S(2)}, u32[]{:S(2)}) collective-permute-start(bf16[384,1024]{1,0:T(8,128)(2,1)} %get-tuple-element.59.refs_2_), channel_id=1, source_target_pairs={{0,1},{1,0},{2,3},{3,2},{4,5},{5,4},{6,7},{7,6},{8,9},{9,8},{10,11... | collective-permute-start | bytes 2359304 | tf_op jit(solution)/shard_map/ppermute | solution.py:820
  267.5 29.2 %collective-permute-start.41 = (bf16[3072,192]{0,1:T(8,128)(2,1)}, bf16[3072,192]{0,1:T(8,128)(2,1)}, u32[]{:S(2)}, u32[]{:S(2)}) collective-permute-start(bf16[3072,192]{0,1:T(8,128)(2,1)} %copy.82), channel_id=1, source_target_pairs={{0,2},{1,3},{2,0},{3,1},{4,6},{5,7},{6,4},{7,5},{8,10},{9,11},{10,... | collective-permute-start | bytes 3538952 | tf_op jit(solution)/shard_map/ppermute | solution.py:823
  284.4 1.2 collective-permute-start.36
  288.5 61.5 %collective-permute-start.37 = (bf16[192,1024]{1,0:T(8,128)(2,1)}, bf16[192,1024]{1,0:T(8,128)(2,1)}, u32[]{:S(2)}, u32[]{:S(2)}) collective-permute-start(bf16[192,1024]{1,0:T(8,128)(2,1)} %get-tuple-element.192), channel_id=1, source_target_pairs={{0,2},{1,3},{2,0},{3,1},{4,6},{5,7},{6,4},{7,5},{8,10},{9,11},{10,... | collective-permute-start | bytes 1179656 | tf_op jit(solution)/shard_map/ppermute | solution.py:823
  (104 other events, 531.8 us)
Sparse Core Ops, SparseCore 0:
  204.1 80.9 reduce-scatter.1

commit v2 on v1

--- a/solution.py
+++ b/solution.py
@@ -11,6 +11,7 @@
 HEAD = 64
 
 
+DP, MP = "dp", "mp"
 EPSILON = 1e-06
 MASKED_SCORE = -1e30
 
@@ -120,7 +121,7 @@
 ):
     length = segments.shape[1]
     local_len = length // lax.axis_size("mp")
-    offset = lax.axis_index("mp") * local_len
+    offset = lax.axis_index(MP) * local_len
     state_f = jnp.transpose(wide_state.astype(jnp.float32), (0, 3, 1, 2))
     block_a = state_f[:, :, 0]
     block_b = state_f[:, :, 1]
@@ -485,7 +486,7 @@
 
 def all_sum_kernel(dp_size, mp_size, part_ref, out_ref, mp_slots, row_sum, dp_slots, *sems):
     mp_send, mp_recv, dp_send, dp_recv = sems
-    dp, mp = lax.axis_index("dp"), lax.axis_index("mp")
+    dp, mp = lax.axis_index(DP), lax.axis_index(MP)
     mp_peers = [lax.rem(mp + s, mp_size) for s in range(1, mp_size)]
     dp_peers = [lax.rem(dp + s, dp_size) for s in range(1, dp_size)]
     barrier = pltpu.get_barrier_semaphore()
@@ -549,15 +550,16 @@
     )(part)
 
 
-def row_scatter_kernel(dp_size, keep_ref, send_ref, side_ref, out_ref, side_out_ref, *scratch):
-    landed, mine, step_send, step_land, far_send, far_land = scratch[:6]
-    cross_sems, step_sems, far_sems = scratch[6:8], scratch[8:10], scratch[10:12]
+def finish_kernel(dp_size, keep_ref, got_ref, *refs):
+    side_refs, ffn_refs = refs[:4], refs[4:8]
+    qkv_out, out_out, cross_out, cross_out_out, in_out, down_out = refs[8:14]
+    step_send, step_land, far_send, far_land = refs[14:18]
+    step_sems, far_sems = refs[18:20], refs[20:22]
     bf16, f32 = jnp.bfloat16, jnp.float32
-    dp, mp = lax.axis_index("dp"), lax.axis_index("mp")
-    chip, core = mp // 2, lax.rem(mp, 2)
+    dp, mp = lax.axis_index(DP), lax.axis_index(MP)
+    core = lax.rem(mp, 2)
     outer, inner = dp // 2, lax.rem(dp, 2)
     count = dp_size // 2
-    peer = ((dp, (1 - chip) * 2 + core))
     mate = (outer * 2 + 1 - inner, mp)
     offsets = [(count // 2 + i) % count for i in range(count)]
     offsets = [o for o in offsets if o] + [0]
@@ -566,9 +568,9 @@
     last = count - 1
 
     barrier = pltpu.get_barrier_semaphore()
-    for device in [peer, mate] + targets[:last]:
+    for device in [mate] + targets[:last]:
         pl.semaphore_signal(barrier, inc=1, device_id=device, device_id_type=MESH)
-    pl.semaphore_wait(barrier, count + 1)
+    pl.semaphore_wait(barrier, count)
 
     def remote(source, target, sems, index, device):
         return pltpu.make_async_remote_copy(
@@ -580,93 +582,78 @@
             device_id_type=MESH,
         )
 
-    def half_block(dp_index):
-        return lax.rem(dp_index // count + core, 2), lax.rem(dp_index, count)
-
-    crossing = []
+    def summed(place, own):
+        index = place * 2 + (inner if own else 1 - inner)
+        part, block = lax.rem(index // count + core, 2), lax.rem(index, count)
+        return keep_ref[part, :, block].astype(f32) + got_ref[part, :, block].astype(f32)
+
+    stepping = []
     for k, place in enumerate(places):
-        for own in range(2):
-            part, block = half_block(place * 2 + (inner if own else 1 - inner))
-            copy = remote(
-                send_ref.at[part, :, block], landed.at[2 * k + own], cross_sems, 2 * k + own, peer
-            )
-            copy.start()
-            crossing.append(copy)
-    stepping = {}
+        step_send[k] = summed(place, False).astype(bf16)
+        stepping.append(remote(step_send.at[k], step_land.at[k], step_sems, k, mate))
+        stepping[k].start()
+
+    def turned(pairs, first, second):
+        depth = first.shape[1]
+        for pair in range(2):
+            flipped = pairs[pair].T
+            for side in range(2):
+                mat = 2 * pair + side
+                piece = flipped[side * depth : (side + 1) * depth]
+                if mat < 3:
+                    first[mat] = piece
+                else:
+                    second[...] = piece
+
+    turned(sum(ref[...].astype(f32) for ref in side_refs), cross_out, cross_out_out)
+    for mat in range(2):
+        in_out[mat] = sum(ref[mat].astype(f32) for ref in ffn_refs)
+    down_out[...] = sum(ref[2].astype(f32) for ref in ffn_refs).T
+
+    going = []
     for k, place in enumerate(places):
-        stepping[0, k] = remote(
-            side_ref.at[:, place * 2 + 1 - inner], step_land.at[0, k], step_sems, k, mate
-        )
-        stepping[0, k].start()
-    going = []
-
-    def pass_on(group, k, value, final_ref):
-        stepping[group, k].wait()
-        total = value.astype(f32) + step_land[group, k].astype(f32)
+        stepping[k].wait()
+        total = summed(place, True) + step_land[k].astype(f32)
         if k == last:
-            final_ref[...] = total
-            return
-        far_send[group, k] = total.astype(bf16)
-        copy = remote(
-            far_send.at[group, k], far_land.at[group, k], far_sems, group * last + k, targets[k]
-        )
-        copy.start()
-        going.append((copy, final_ref, group, k))
-
-    for k, place in enumerate(places):
-        pass_on(0, k, side_ref[:, place * 2 + inner], side_out_ref)
-    for k, place in enumerate(places):
-        for own in range(2):
-            part, block = half_block(place * 2 + (inner if own else 1 - inner))
-            crossing[2 * k + own].wait()
-            total = keep_ref[part, :, block].astype(f32) + landed[2 * k + own].astype(f32)
-            if own:
-                mine[k] = total.astype(bf16)
-            else:
-                step_send[k] = total.astype(bf16)
-                stepping[1, k] = remote(
-                    step_send.at[k], step_land.at[1, k], step_sems, count + k, mate
-                )
-                stepping[1, k].start()
-        if k:
-            pass_on(1, k - 1, mine[k - 1], out_ref)
-    pass_on(1, last, mine[last], out_ref)
-    for copy, final_ref, group, k in going:
+            continue
+        far_send[k] = total.astype(bf16)
+        going.append(remote(far_send.at[k], far_land.at[k], far_sems, k, targets[k]))
+        going[k].start()
+    for k, copy in enumerate(going):
         copy.wait()
-        final_ref[...] += far_land[group, k].astype(f32)
-
-
-def row_scatter(keep, send, side, dp_size):
-    _, mats, _, rows, columns = keep.shape
-    block = (mats, rows, columns)
+        total += far_land[k].astype(f32)
+    turned(total, qkv_out, out_out)
+
+
+def finish(keep, got, side_terms, ffn_terms, dp_size):
+    pairs, _, rows, columns = keep.shape[1:]
+    depth, width = columns // 2, ffn_terms[0].shape[2]
+    block = (pairs, rows, columns)
     count = dp_size // 2
     whole = pl.BlockSpec(memory_space=pltpu.VMEM)
-    shape = jax.ShapeDtypeStruct(block, jnp.float32)
     dma = pltpu.SemaphoreType.DMA
+    three, one = (3, depth, rows), (depth, rows)
+    shapes = [three, one, three, one, (2, rows, width), (width, rows)]
     return pl.pallas_call(
-        functools.partial(row_scatter_kernel, dp_size),
-        out_shape=[shape, shape],
-        in_specs=[whole] * 3,
-        out_specs=[whole] * 2,
+        functools.partial(finish_kernel, dp_size),
+        out_shape=[jax.ShapeDtypeStruct(shape, jnp.float32) for shape in shapes],
+        in_specs=[whole] * 10,
+        out_specs=[whole] * 6,
         scratch_shapes=[
-            pltpu.VMEM((dp_size, *block), jnp.bfloat16),
             pltpu.VMEM((count, *block), jnp.bfloat16),
             pltpu.VMEM((count, *block), jnp.bfloat16),
-            pltpu.VMEM((2, count, *block), jnp.bfloat16),
-            pltpu.VMEM((2, count - 1, *block), jnp.bfloat16),
-            pltpu.VMEM((2, count - 1, *block), jnp.bfloat16),
-            dma((dp_size,)),
-            dma((dp_size,)),
-            dma((2 * count,)),
-            dma((2 * count,)),
-            dma((2 * (count - 1),)),
-            dma((2 * (count - 1),)),
+            pltpu.VMEM((count - 1, *block), jnp.bfloat16),
+            pltpu.VMEM((count - 1, *block), jnp.bfloat16),
+            dma((count,)),
+            dma((count,)),
+            dma((count - 1,)),
+            dma((count - 1,)),
         ],
         compiler_params=pltpu.CompilerParams(
             collective_id=1, has_side_effects=True, vmem_limit_bytes=40 << 20
         ),
-        name="row_scatter",
-    )(keep, send, side)
+        name="finish",
+    )(keep, got, *side_terms, *ffn_terms)
 
 
 def join_norm_kernel(place_ref, gain_ref, *refs):
@@ -709,29 +696,30 @@
 
 def outer_kernel(sizes, *refs):
     keep_ref, send_ref = refs[-2:]
-    at, row = 0, 0
+    depth = refs[0].shape[0]
+    at, mat = 0, 0
     for size in sizes:
         near, far = refs[at][...], refs[at + 1][...]
         for ref in refs[at + 2 : at + 2 + size]:
+            columns = slice(mat % 2 * depth, (mat % 2 + 1) * depth)
             for low in range(0, ref.shape[0], 384):
                 block = ref[low : low + 384, :]
-                rows = slice(row, row + block.shape[0])
-                keep_ref[rows, :] = dot_nt(block, near).astype(jnp.bfloat16)
-                send_ref[rows, :] = dot_nt(block, far).astype(jnp.bfloat16)
-                row += block.shape[0]
+                rows = slice(low, low + block.shape[0])
+                keep_ref[mat // 2, rows, columns] = dot_nt(block, near).astype(jnp.bfloat16)
+                send_ref[mat // 2, rows, columns] = dot_nt(block, far).astype(jnp.bfloat16)
+            mat += 1
         at += 2 + size
 
 
 def outer_products(groups):
-    operands, sizes, rows, flops = [], [], 0, 0
+    operands, sizes, flops = [], [], 0
     for outer, inner in groups:
         operands += [*inner, *outer]
         sizes.append(len(outer))
-        rows += sum(o.shape[0] for o in outer)
         flops += sum(4 * o.size * inner[0].shape[0] for o in outer)
-    columns = operands[0].shape[0]
+    rows, columns = groups[0][0][0].shape[0], 2 * operands[0].shape[0]
     whole = pl.BlockSpec(memory_space=pltpu.VMEM)
-    shape = jax.ShapeDtypeStruct((rows, columns), jnp.bfloat16)
+    shape = jax.ShapeDtypeStruct((sum(sizes) // 2, rows, columns), jnp.bfloat16)
     return pl.pallas_call(
         functools.partial(outer_kernel, tuple(sizes)),
         out_shape=[shape, shape],
@@ -740,7 +728,7 @@
         compiler_params=pltpu.CompilerParams(vmem_limit_bytes=32 << 20),
         cost_estimate=pl.CostEstimate(
             flops=flops,
-            bytes_accessed=sum(2 * o.size for o in operands) + 4 * rows * columns,
+            bytes_accessed=sum(2 * o.size for o in operands) + 4 * shape.size,
             transcendentals=0,
         ),
         name="outer_products",
@@ -748,19 +736,42 @@
 
 
 def self_products_kernel(core_ref, *refs):
-    grads, (norm_ref, near_own, near_mate, far_own, far_mate) = refs[:6], refs[6:11]
-    attn_ref, mix_near, mix_far, keep_ref, send_ref, into_ref = refs[11:]
+    grads, (norm_ref, attn_ref, mix_ref, out_ref) = refs[:6], refs[6:]
     core = core_ref[0]
-    for i, ref in enumerate(grads):
-        side, mat = i // 3, i % 3
-        grad = ref[...]
-        send_ref[side, mat] = dot_nt(grad, norm_ref[1]).astype(jnp.bfloat16)
-        keep_ref[side, mat] = dot_nt(grad, norm_ref[0]).astype(jnp.bfloat16)
+    depth = norm_ref.shape[0]
+    norm, mix = norm_ref[...], mix_ref[...]
     for side in range(2):
-        place = core if side == 0 else 1 - core
-        grad = attn_ref[place]
-        send_ref[side, 3] = dot_nt(grad, mix_far[...]).astype(jnp.bfloat16)
-        keep_ref[side, 3] = dot_nt(grad, mix_near[...]).astype(jnp.bfloat16)
+        grad_rows = [ref[...] for ref in grads[3 * side : 3 * side + 3]]
+        grad_rows.append(attn_ref[core if side == 0 else 1 - core])
+        for mat, grad in enumerate(grad_rows):
+            columns = slice(mat % 2 * depth, (mat % 2 + 1) * depth)
+            value = dot_nt(grad, mix if mat == 3 else norm)
+            out_ref[side, mat // 2, :, columns] = value.astype(jnp.bfloat16)
+
+
+def self_products(grads, normed, grad_attn, mix, core):
+    half, length = grads[0].shape
+    depth = normed.shape[0]
+    whole = pl.BlockSpec(memory_space=pltpu.VMEM)
+    operands = [*grads, normed, grad_attn, mix]
+    shape = jax.ShapeDtypeStruct((2, 2, half, 2 * depth), jnp.bfloat16)
+    return pl.pallas_call(
+        self_products_kernel,
+        out_shape=shape,
+        in_specs=[pl.BlockSpec(memory_space=pltpu.SMEM)] + [whole] * len(operands),
+        out_specs=whole,
+        compiler_params=pltpu.CompilerParams(vmem_limit_bytes=32 << 20),
+        cost_estimate=pl.CostEstimate(
+            flops=16 * half * length * depth,
+            bytes_accessed=sum(2 * o.size for o in operands) + 2 * shape.size,
+            transcendentals=0,
+        ),
+        name="self_products",
+    )(core, *operands)
+
+
+def into_kernel(*refs):
+    grads, (near_own, near_mate, far_own, far_mate, into_ref) = refs[:6], refs[6:]
     for mat in range(3):
         joined = jnp.concatenate([grads[mat][...], grads[3 + mat][...]], axis=0)
         for out, (own, mate) in enumerate(((near_own, near_mate), (far_own, far_mate))):
@@ -771,25 +782,58 @@
                 into_ref[out] += term
 
 
-def self_products(grads, normed, weights, grad_attn, mixes, core):
+def into_active(grads, weights):
     half, length = grads[0].shape
-    depth = normed.shape[1]
+    depth = weights[0].shape[1]
     whole = pl.BlockSpec(memory_space=pltpu.VMEM)
-    shape = jax.ShapeDtypeStruct((2, 4, half, depth), jnp.bfloat16)
-    operands = [*grads, normed, *weights, grad_attn, *mixes]
+    operands = [*grads, *weights]
     return pl.pallas_call(
-        self_products_kernel,
-        out_shape=[shape, shape, jax.ShapeDtypeStruct((2, depth, length), jnp.float32)],
-        in_specs=[pl.BlockSpec(memory_space=pltpu.SMEM)] + [whole] * len(operands),
-        out_specs=[whole] * 3,
-        compiler_params=pltpu.CompilerParams(vmem_limit_bytes=40 << 20),
+        into_kernel,
+        out_shape=jax.ShapeDtypeStruct((2, depth, length), jnp.float32),
+        in_specs=[whole] * len(operands),
+        out_specs=whole,
+        compiler_params=pltpu.CompilerParams(vmem_limit_bytes=32 << 20),
         cost_estimate=pl.CostEstimate(
-            flops=2 * 28 * half * length * depth,
+            flops=24 * half * length * depth,
             bytes_accessed=sum(2 * o.size for o in operands) + 8 * depth * length,
             transcendentals=0,
         ),
-        name="self_products",
-    )(core, *operands)
+        name="into_active",
+    )(*operands)
+
+
+def state_grads_kernel(predict_ref, chip_ref, state_ref, cot_ref, own_ref, far_ref, out_ref, sum_ref):
+    row = pl.program_id(0)
+    own_row = row == chip_ref[0]
+    grad = jnp.where(own_row, own_ref[...], far_ref[...]).astype(jnp.float32)
+    for j in range(2):
+        sum_ref[row, j] = jnp.sum(grad * state_ref[0, j].astype(jnp.float32))
+    guess_a = cot_ref[0, 0].astype(jnp.float32) + grad
+    guess_b = cot_ref[0, 1].astype(jnp.float32)
+    for j in range(2):
+        out_ref[0, j] = predict_ref[0, j] * guess_a + predict_ref[1, j] * guess_b
+
+
+def state_grads(predict, chip, wide_state, cotangent, own, far):
+    rows, blocks, depth, length = wide_state.shape
+    smem = pl.BlockSpec(memory_space=pltpu.SMEM)
+    one_row = pl.BlockSpec((1, blocks, depth, length), lambda row: (row, 0, 0, 0))
+    whole = pl.BlockSpec((depth, length), lambda row: (0, 0))
+    return pl.pallas_call(
+        state_grads_kernel,
+        grid=(rows,),
+        out_shape=[
+            jax.ShapeDtypeStruct(wide_state.shape, jnp.float32),
+            jax.ShapeDtypeStruct((rows, blocks), jnp.float32),
+        ],
+        in_specs=[smem, smem, one_row, one_row, whole, whole],
+        out_specs=[one_row, smem],
+        compiler_params=pltpu.CompilerParams(vmem_limit_bytes=32 << 20),
+        cost_estimate=pl.CostEstimate(
+            flops=12 * wide_state.size, bytes_accessed=9 * wide_state.size, transcendentals=0
+        ),
+        name="state_grads",
+    )(predict, chip, wide_state, cotangent, own, far)
 
 
 def paired_shards(
@@ -810,17 +854,17 @@
     cotangent,
 ):
     bf16, f32 = jnp.bfloat16, jnp.float32
-    me = lax.axis_index("mp")
+    me = lax.axis_index(MP)
     chip, core = me // 2, me % 2
     far = me ^ 2
     mates = [(i, i ^ 1) for i in range(4)]
     peers = [(i, i ^ 2) for i in range(4)]
 
     def to_mate(array):
-        return lax.ppermute(array, "mp", mates)
+        return lax.ppermute(array, MP, mates)
 
     def to_peer(array):
-        return lax.ppermute(array, "mp", peers)
+        return lax.ppermute(array, MP, peers)
 
     def quarters(own, across, axis=0):
         pieces = [own, across, to_mate(own), to_mate(across)]
@@ -857,6 +901,16 @@
     act_own = pick(active_rows, chip)
     act_far = to_peer(pick(active_rows, 1 - chip))
     qkv_far = to_peer(self_qkv)
+    cot_a = cotangent[:, 0].astype(f32)
+    cot_b = cotangent[:, 1].astype(f32)
+    grad_branch = (correct[0] * cot_a + correct[1] * cot_b).astype(bf16)
+    early_sums = [jnp.sum(c * b) for c in (cot_a, cot_b) for b in (block_a, block_b)]
+    seg_row = pick(segments, chip)
+    code = jnp.where(pick(key_valid, chip) > 0, seg_row, -1)
+    mask = (seg_row[None], jnp.broadcast_to(code[:, None], (wide_state.shape[3], 128)))
+    act_far, grad_branch, early_sums, mask = lax.optimization_barrier(
+        (act_far, grad_branch, early_sums, mask)
+    )
     act_pieces = [act_own, act_far, to_mate(act_own), to_mate(act_far)]
     places = jnp.stack([me, far, me ^ 1, me ^ 3]).astype(jnp.int32)
     active, normed_pieces, scale_a = join_norm(
@@ -864,15 +918,11 @@
     )
     active = active.reshape(width, length)
     normed_a = normed_pieces.reshape(width, length)
-    self_out = after(self_out, qkv_far, act_far)
     self_out_far = to_peer(self_out)
-    enc_far = to_peer(after(pick(encoder, 1 - chip), qkv_far, act_far))
-    cross_qkv_far = to_peer(after(cross_qkv, qkv_far, act_far))
-    cross_out_far = to_peer(after(cross_out, qkv_far, act_far))
-    cot_a = cotangent[:, 0].astype(f32)
-    cot_b = cotangent[:, 1].astype(f32)
-    grad_branch = (correct[0] * cot_a + correct[1] * cot_b).astype(bf16)
-    grad_far = to_peer(after(grad_branch, qkv_far, act_far))
+    enc_far = to_peer(pick(encoder, 1 - chip))
+    cross_qkv_far = to_peer(cross_qkv)
+    cross_out_far = to_peer(cross_out)
+    grad_far = to_peer(grad_branch)
 
     def columns(array, which):
         return lax.dynamic_slice_in_dim(array, which * half, half, array.ndim - 1)
@@ -890,9 +940,6 @@
 
     resid_a = active.astype(f32)
     qkv = jnp.concatenate([project(w_qkv[i], normed_a).astype(bf16) for i in range(3)], axis=0)
-    seg_row = pick(segments, chip)
-    code = jnp.where(pick(key_valid, chip) > 0, seg_row, -1)
-    mask = (seg_row[None], jnp.broadcast_to(code[:, None], (length, 128)))
     self_args = ((qkv, 0), (qkv, heads), (qkv, 2 * heads), heads, mask)
     mix_own, self_log = attention_call(*self_args, None, 512)
     self_mix = halves(mix_own)
@@ -942,34 +989,53 @@
         got = to_mate(pick(split, 1 - core, 1).astype(bf16))
         return pick(split, core, 1) + got.astype(f32)
 
+    block = width // dp_size
+
+    place = lax.axis_index(DP)
+    outer, inner = place // 2, place % 2
+    count = dp_size // 2
+
+    def dp_start(mats):
+        split = mats.reshape(mats.shape[0], count, 2, *mats.shape[2:])
+        swap = [(i, i ^ 1) for i in range(dp_size)]
+        sent = pick(split, 1 - inner, 2)
+        got = lax.ppermute(sent, DP, swap)
+        return pick(split, inner, 2), sent, got
+
+    def dp_terms(started):
+        mine = (started[0].astype(f32) + started[2].astype(f32)).astype(bf16)
+        terms = [pick(mine, outer, 1)]
+        for o in [(count // 2 + i) % count for i in range(count)]:
+            if o:
+                turn = [(i, (i + 2 * o) % dp_size) for i in range(dp_size)]
+                terms.append(lax.ppermute(pick(mine, (outer + o) % count, 1), DP, turn))
+        return terms
+
+    def near_far(inner):
+        split = inner.reshape(4, depth, inner.shape[1])
+        return pick(split, me), pick(split, far)
+
     gate_o, up_o, hid_o, res_o = forward(normed_own)
     gg_o, gu_o, back_o = backward(gate_o, up_o, grad_own)
     normed_other = after(normed_other, gg_o, gu_o, back_o)
     gate_t, up_t, hid_t, res_t = forward(normed_other)
     gg_t, gu_t, back_t = backward(gate_t, up_t, grad_other)
 
-    block = width // dp_size
-
-    def joined(mats):
-        return jnp.concatenate([m.reshape(dp_size, block, m.shape[1]) for m in mats], axis=1)
-
-    def scatter(rows):
-        out = lax.psum_scatter(rows, "dp", scatter_dimension=0, tiled=True)
-        return out.reshape(-1, block, out.shape[2]).astype(f32)
-
     grad_in = [
         (dot_nt(normed_own, own) + dot_nt(normed_other, other)).astype(bf16)
         for own, other in ((gg_o, gg_t), (gu_o, gu_t))
     ]
     grad_out = (dot_nt(grad_own, hid_o) + dot_nt(grad_other, hid_t)).astype(bf16)
-    ffn_joined = joined(grad_in + [grad_out])
+    ffn_joined = jnp.stack(grad_in + [grad_out]).reshape(3, dp_size, block, width)
     back_sent = my_half(back_t).astype(bf16)
     back_far = to_peer(back_sent)
     sum_o = my_half(res_o) + pick(branch.reshape(2, 2, depth, length), core, 1).astype(f32)
     sum_t = my_half(res_t)
     sum_sent = jnp.stack([pick(sum_o, 1 - chip), pick(sum_t, 1 - chip)]).astype(bf16)
-    back_far, ffn_joined, sum_sent = lax.optimization_barrier(
-        (back_far, ffn_joined, sum_sent)
+    ffn_started = dp_start(ffn_joined)
+    enc_near_far = near_far(enc.T)
+    back_far, sum_sent, enc_near_far, _ = lax.optimization_barrier(
+        (back_far, sum_sent, enc_near_far, ffn_started[1])
     )
     back_half = my_half(back_o) + back_far.astype(f32)
     back_mate = to_mate(back_half.astype(bf16)).astype(f32)
@@ -978,16 +1044,9 @@
         width, length
     )
 
-    ffn_parts = scatter(ffn_joined)
+    ffn_terms = dp_terms(ffn_started)
 
     sum_far = to_peer(sum_sent)
-    branch_sum = by_row(
-        pick(sum_o, chip) + sum_far[1].astype(f32), pick(sum_t, chip) + sum_far[0].astype(f32)
-    )
-    new_state = jnp.stack(
-        [guess_a + correct[0] * branch_sum, guess_b + correct[1] * branch_sum], axis=1
-    ).astype(bf16)
-    grad_correct = jnp.stack([jnp.sum(cot_a * branch_sum), jnp.sum(cot_b * branch_sum)])
 
 
     def rms_back(values, scale, gain, incoming):
@@ -996,10 +1055,6 @@
             scale * gain * incoming - values * (scale * scale * scale) * inner,
             jnp.sum(incoming * values * scale, axis=1),
         )
-
-    def near_far(inner):
-        split = inner.reshape(4, depth, inner.shape[1])
-        return pick(split, me), pick(split, far)
 
     grad_rows = grad_own.astype(f32)
     grad_resid_c, gain_grad_c = rms_back(resid_c, scale_c, gains[2], grad_normed_c)
@@ -1012,11 +1067,11 @@
     side_keep, side_send = outer_products(
         (
             ((gcq_all,), near_far(normed_b)),
-            ((gck_all, gcv_all), near_far(enc.T)),
+            ((gck_all, gcv_all), enc_near_far),
             ((grad_cross_b,), near_far(cross_mix)),
         )
     )
-    side_sum = (side_keep.astype(f32) + to_peer(side_send).astype(f32)).astype(bf16)
+    side_got = to_peer(side_send)
     enc_rows = encoder.shape[1]
 
     def encoder_grad(which):
@@ -1024,8 +1079,7 @@
         values = lax.dynamic_slice_in_dim(gcv_all, which * enc_rows, enc_rows, 1)
         return dot_tt(keys, w_cross[1]) + dot_tt(values, w_cross[2])
 
-    enc_got = to_peer(encoder_grad(far).astype(bf16)).astype(f32)
-    grad_encoder = by_row(encoder_grad(me), enc_got)
+    enc_got = to_peer(encoder_grad(far).astype(bf16))
 
     resid_b_part, gain_grad_b = rms_back(resid_b, scale_b, gains[1], grad_normed_b)
     grad_resid_b = grad_resid_c + resid_b_part
@@ -1034,21 +1088,28 @@
     grad_mix = dot_nn(self_out_rows, grad_attn_b).astype(bf16)
     g_own = attention_call(*self_args, (self_log, mix_own, grad_mix), 256)
     g_mate = [to_mate(g) for g in g_own]
-    keep, send, both_in = self_products(
-        (*g_own, *g_mate),
-        normed_pieces,
-        (own_near, mate_near, own_far, mate_far),
-        grad_attn_b.reshape(2, half, length),
-        near_far(self_mix),
-        core.astype(jnp.int32).reshape(1),
-    )
-    blocks = (2, 4, dp_size // 2, half // (dp_size // 2), depth)
-    self_parts, side_parts = row_scatter(
-        keep.reshape(blocks),
-        send.reshape(blocks),
-        side_sum.reshape(4, dp_size, block, depth),
-        dp_size,
-    )
+    mix_near, mix_far = near_far(self_mix)
+    attn_halves = grad_attn_b.reshape(2, half, length)
+    where = core.astype(jnp.int32).reshape(1)
+    grads = (*g_own, *g_mate)
+    send = self_products(grads, normed_pieces[1], attn_halves, mix_far, where)
+    sum_far, enc_got, send = lax.optimization_barrier((sum_far, enc_got, send))
+    side_sum = (side_keep.astype(f32) + side_got.astype(f32)).astype(bf16)
+    side_started = dp_start(side_sum.reshape(2, dp_size, block, 2 * depth))
+    branch_sum = by_row(
+        pick(sum_o, chip) + sum_far[1].astype(f32), pick(sum_t, chip) + sum_far[0].astype(f32)
+    )
+    new_state = jnp.stack(
+        [guess_a + correct[0] * branch_sum, guess_b + correct[1] * branch_sum], axis=1
+    ).astype(bf16)
+    grad_correct = (jnp.sum(cot_a * branch_sum), jnp.sum(cot_b * branch_sum))
+    grad_encoder = by_row(encoder_grad(me), enc_got.astype(f32))
+    got = to_peer(send)
+    keep = self_products(grads, normed_pieces[0], attn_halves, mix_near, where)
+    both_in = into_active(grads, (own_near, mate_near, own_far, mate_far))
+    blocks = (2, 2, count, block, 2 * depth)
+    side_terms = dp_terms(side_started)
+    finished = finish(keep.reshape(blocks), got.reshape(blocks), side_terms, ffn_terms, dp_size)
     both_act = jnp.stack([act_own, act_far]).astype(f32)
     gain_a = norm_gains[0].reshape(4, depth)
     both_gain = jnp.stack([pick(gain_a, me), pick(gain_a, far)])[:, :, None]
@@ -1065,41 +1126,30 @@
         + jnp.where(slot == far, gain_sums[1][None], 0.0)
     ).reshape(width)
 
-    grad_cols = by_row(grad_active[0], to_peer(grad_active[1])).astype(f32)
-    grad_guess_a = cot_a + grad_cols
-    grad_predict = jnp.stack(
-        [
-            jnp.sum(grad_guess_a * block_a),
-            jnp.sum(grad_guess_a * block_b),
-            jnp.sum(cot_b * block_a),
-            jnp.sum(cot_b * block_b),
-        ]
-    )
-    grad_state = jnp.stack(
-        [
-            predict[0, 0] * grad_guess_a + predict[1, 0] * cot_b,
-            predict[0, 1] * grad_guess_a + predict[1, 1] * cot_b,
-        ],
-        axis=1,
-    )
-    scalars = jnp.concatenate([grad_predict, grad_correct, jnp.zeros((width - 6,), f32)])
+    active_got = to_peer(grad_active[1])
+    grad_state, late_sums = state_grads(
+        predict, chip.astype(jnp.int32).reshape(1), wide_state, cotangent, grad_active[0], active_got
+    )
+    grad_predict = (
+        early_sums[0] + late_sums[0, 0] + late_sums[1, 0],
+        early_sums[1] + late_sums[0, 1] + late_sums[1, 1],
+        early_sums[2],
+        early_sums[3],
+    )
+    lane = jnp.arange(width, dtype=jnp.int32)
+    scalars = sum(
+        jnp.where(lane == i, value, 0.0)
+        for i, value in enumerate((*grad_predict, grad_correct[0], grad_correct[1]))
+    )
     total = all_sum(
         jnp.stack([gain_grad_a, 0.5 * gain_grad_b, 0.5 * gain_grad_c, scalars]), dp_size, 4
     )
-
-    def columns_out(part):
-        return jnp.swapaxes(part, -1, -2)
 
     return (
         new_state,
         grad_state,
         grad_encoder,
-        columns_out(self_parts[:3]),
-        columns_out(self_parts[3]),
-        columns_out(side_parts[:3]),
-        columns_out(side_parts[3]),
-        ffn_parts[:2],
-        columns_out(ffn_parts[2]),
+        *finished,
         total[:3],
         total[3, :4].reshape(2, 2),
         total[3, 4:6],

time: 395 us -> 420 us (1.063)
  waiting for transfers between devices: 66.9 us -> 103 us
  matrix products: 44.6 us -> 69.6 us
  Pallas kernels: 110 us -> 87.8 us
  starting transfers between devices: 19 us -> 34 us
  other arithmetic: 68.8 us -> 56.6 us
  between operations: 16.3 us -> 6.59 us
  local copies, waits for them, and re-layouts: 63.4 us -> 54.5 us
    ppermute x42 -> x51, waiting for transfers between devices: 66.9 us -> 103 us  [the longest x14 67.3 us: to_peer(): return lax.ppermute(array, MP, peers)]
    pallas_call x2 -> x5, Pallas kernels: 53 us -> 30.6 us  [the longest x1 21 us: finish(): pl.pallas_call(functools.partial(finish_kernel, dp_size), out_shape=[jax....]
    ppermute x42 -> x51, starting transfers between devices: 18.9 us -> 34 us  [the longest x14 16.1 us: to_peer(): return lax.ppermute(array, MP, peers)]
    convert_element_type x5 -> x3, other arithmetic: 13.9 us -> 3.82 us  [the longest x2 3.53 us: dp_terms(): mine = (started[0].astype(f32) + started[2].astype(f32)).astype(bf16)]
    dot_general x6, matrix products: 8.34 us -> 17.6 us  [dot_nt(): lax.dot_general(left, right, (((1,), (1,)), ((), ())), preferred_element_...]
    dot_general x12, matrix products: 18.4 us -> 27 us  [dot_tn(): lax.dot_general(left, right, (((0,), (0,)), ((), ())), preferred_element_...]
    dot_general x9, matrix products: 14.6 us -> 20.4 us  [dot_nn(): lax.dot_general(left, right, (((1,), (0,)), ((), ())), preferred_element_...]
    reduce_sum x1 -> x2, other arithmetic: 2.79 us -> 7.98 us  [the longest x1 6.87 us: paired_shards(): jnp.sum(c * b)]
  transfers between devices with their start and end apart: 43 -> 51, of which waited for: 10 -> 10; matrix products, arithmetic and copies ran while one was open for 34% -> 34% of each run, Pallas kernels for 26% -> 14%
where the time goes in v2:
time: 420 us; the launch traced here: 412 us
  waiting for transfers between devices  103 us (25%)
  Pallas kernels  87.8 us (21%)
  matrix products  69.6 us (17%)
  other arithmetic  56.6 us (13%)
  local copies, waits for them, and re-layouts  54.5 us (13%)
  starting transfers between devices  34 us (8%)
  between operations  6.59 us (2%)
    ppermute x14, waiting for transfers between devices, to_peer(): return lax.ppermute(array, MP, peers)  67.3 us
    pallas_call x4, Pallas kernels, attention_call(): pl.pallas_call(functools.partial(kernel, mask is not None, size), grid=(h...  39.6 us
    unnamed x211, local copies, waits for them, and re-layouts  29.1 us
    dot_general x12, matrix products, dot_tn(): lax.dot_general(left, right, (((0,), (0,)), ((), ())), preferred_element_...  27 us
    ppermute x2, waiting for transfers between devices, dp_start(): got = lax.ppermute(sent, DP, swap)  24.3 us
    pallas_call x1, Pallas kernels, finish(): pl.pallas_call(functools.partial(finish_kernel, dp_size), out_shape=[jax....  21 us
    dot_general x9, matrix products, dot_nn(): lax.dot_general(left, right, (((1,), (0,)), ((), ())), preferred_element_...  20.4 us
    dot_general x6, matrix products, dot_nt(): lax.dot_general(left, right, (((1,), (1,)), ((), ())), preferred_element_...  17.6 us
  transfers between devices with their start and end apart: 51, of which 10 were waited for; matrix products, arithmetic and copies ran while one was open for 34% of the time, Pallas kernels for 14%

profile of v2, /device:TPU:0, one launch (start us, length us, event | category | flops | bytes accessed | tf_op | source)
XLA Modules:
  0.0 412.3 jit_solution(2622426446059009066)
XLA Ops:
  1.2 2.6 collective-permute-start.3
  10.9 6.9 %fusion.53 = (f32[]{:T(128)}, f32[]{:T(128)}, f32[]{:T(128)}, f32[]{:T(128)}, bf16[2,192,1024]{2,1,0:T(8,128)(2,1)S(1)}, /*index=5*/bf16[2,192,1024]{2,1,0:T(8,128)(2,1)}) fusion(bf16[2,2,192,1024]{3,2,1,0:T(8,128)(2,1)} %cot_ref.1, bf16[2,2,192,1024]{3,2,1,0:T(8,128)(2,1)} %state_ref.1, f32[]{:T(128)} %bitcast.1, f32[]{:T(128)} %bitcast, f32[]{:T(128)} %bitcast.12, ...), kind=kLoop, calls=%fused_computation.119 | loop fusion | flops 7864316 | bytes 4718624 | tf_op jit(solution)/shard_map/reduce_sum | solution.py:907
  27.6 13.8 %collective-permute-done.10 = bf16[192,768]{1,0:T(8,128)(2,1)} collective-permute-done((bf16[192,768]{1,0:T(8,128)(2,1)}, bf16[192,768]{1,0:T(8,128)(2,1)}, u32[]{:S(2)}, u32[]{:S(2)}) %collective-permute-start.10) | collective-permute-done | bytes 294944 | tf_op jit(solution)/shard_map/ppermute | solution.py:867
  41.4 2.0 collective-permute-start.13
  43.5 6.3 %collective-permute-done.refs_1_ = bf16[192,1024]{1,0:T(8,128)(2,1)S(1)} collective-permute-done((bf16[192,1024]{1,0:T(8,128)(2,1)}, bf16[192,1024]{1,0:T(8,128)(2,1)S(1)}, u32[]{:S(2)}, u32[]{:S(2)}) %collective-permute-start) | collective-permute-done | bytes 393248 | tf_op jit(solution)/shard_map/ppermute | solution.py:867
  49.8 1.9 dynamic-slice_bitcast_fusion.33
  52.4 2.0 collective-permute-start.21
  62.7 3.5 join_norm.1
  66.4 2.5 collective-permute-done.13
  68.8 16.6 %collective-permute-done.21 = bf16[2,192,1024]{2,1,0:T(8,128)(2,1)} collective-permute-done((bf16[2,192,1024]{2,1,0:T(8,128)(2,1)}, bf16[2,192,1024]{2,1,0:T(8,128)(2,1)}, u32[]{:S(2)}, u32[]{:S(2)}) %collective-permute-start.21) | collective-permute-done | bytes 786464 | tf_op jit(solution)/shard_map/ppermute | solution.py:867
  89.7 9.1 %attend.2 = (bf16[384,1024]{1,0:T(8,128)(2,1)S(1)}, f32[6,1,1024]{2,1,0:T(1,128)S(1)}) custom-call(bf16[1152,1024]{1,0:T(8,128)(2,1)S(1)} %pad_maximum_fusion.6.refs_0_.refs_1_.refs_2_, bf16[1152,1024]{1,0:T(8,128)(2,1)S(1)} %pad_maximum_fusion.6.refs_0_.refs_1_.refs_2_, bf16[1152,1024]{1,0:T(8,128)(2,1)S(1)} %pad_maximum_fusion.6.refs_0_.refs_1_.refs_2_, ...), custom_call_target="tpu_custom_call" | custom-call | flops 3865470464 | bytes 3145728 | tf_op jit(solution)/shard_map/attend/pallas_call | solution.py:455
  99.4 1.9 pad_maximum_fusion
  108.4 3.3 multiply_reduce_fusion.3
  113.2 7.3 %attend.3 = (bf16[384,1024]{1,0:T(8,128)(2,1)S(1)}, f32[6,1,1024]{2,1,0:T(1,128)S(1)}) custom-call(bf16[384,1024]{1,0:T(8,128)(2,1)S(1)} %convolution_convert_fusion.2.refs_0_, bf16[768,512]{1,0:T(8,128)(2,1)S(1)} %pad_maximum_fusion.15.refs_1_.refs_2_, bf16[768,512]{1,0:T(8,128)(2,1)S(1)} %pad_maximum_fusion.15.refs_1_.refs_2_), custom_call_target="tpu_custom_call" | custom-call | flops 3221225472 | bytes 2359296 | tf_op jit(solution)/shard_map/attend/pallas_call | solution.py:455
  121.5 3.1 fusion.67
  129.8 3.1 fusion.80
  132.9 3.1 fusion.88
  137.8 6.8 %fusion.25 = (bf16[768,1024]{0,1:T(8,128)(2,1)S(1)}, bf16[768,1024]{0,1:T(8,128)(2,1)}, bf16[768,1024]{0,1:T(8,128)(2,1)}) fusion(f32[1024,768]{1,0:T(8,128)} %fusion.88, f32[1024,768]{1,0:T(8,128)} %fusion.80, bf16[768,768]{1,0:T(8,128)(2,1)S(1)} %copy-done, bf16[2,768,1024]{2,1,0:T(8,128)(2,1)S(1)} %pad_maximum_fusion.4, s32[]{:T(128)S(6)} %select_n.343), kind=kOutput, calls=%fused_computation.52 | convolution fusion | flops 1228406784 | bytes 13762564 | tf_op jit(solution)/shard_map/dot_general | solution.py:334
  144.6 3.0 fusion.140
  151.9 4.2 %fusion.61 = f32[768,768]{1,0:T(8,128)} fusion(bf16[768,1024]{0,1:T(8,128)(2,1)} %get-tuple-element.154, bf16[2,768,1024]{2,1,0:T(8,128)(2,1)S(1)} %pad_maximum_fusion.4, s32[]{:T(128)S(6)} %select_n.343), kind=kOutput, calls=%fused_computation.141 | convolution fusion | flops 1207959552 | bytes 5505028 | tf_op jit(solution)/shard_map/dot_general | solution.py:340
  157.4 2.8 fusion.143
  160.5 2.8 fusion.142
  166.5 6.8 %fusion.24 = (bf16[768,1024]{0,1:T(8,128)(2,1)S(1)}, bf16[768,1024]{0,1:T(8,128)(2,1)S(1)}, bf16[768,1024]{0,1:T(8,128)(2,1)}) fusion(f32[1024,768]{1,0:T(8,128)S(1)} %fusion.84, f32[1024,768]{1,0:T(8,128)} %fusion.67, bf16[768,1024]{1,0:T(8,128)(2,1)S(1)} %maximum_select_fusion.2, bf16[2,768,768]{2,1,0:T(8,128)(2,1)S(1)} %copy-done.91), kind=kOutput, calls=%fused_computation.49 | convolution fusion | flops 1228406784 | bytes 13762560 | tf_op jit(solution)/shard_map/dot_general | solution.py:328
  177.3 3.1 add_convert_fusion.3
  183.3 3.3 add_convert_fusion.4
  194.4 14.6 %collective-permute-done.27 = bf16[2,192,1024]{2,1,0:T(8,128)(2,1)S(1)} collective-permute-done((bf16[2,192,1024]{2,1,0:T(8,128)(2,1)}, bf16[2,192,1024]{2,1,0:T(8,128)(2,1)S(1)}, u32[]{:S(2)}, u32[]{:S(2)}) %collective-permute-start.27) | collective-permute-done | bytes 786464 | tf_op jit(solution)/shard_map/ppermute | solution.py:867
  220.3 10.2 %attend_back.2 = (bf16[384,1024]{1,0:T(8,128)(2,1)S(1)}, bf16[384,512]{1,0:T(8,128)(2,1)S(1)}, bf16[384,512]{1,0:T(8,128)(2,1)S(1)}) custom-call(bf16[384,1024]{1,0:T(8,128)(2,1)S(1)} %convolution_convert_fusion.2.refs_0_, bf16[768,512]{1,0:T(8,128)(2,1)S(1)} %pad_maximum_fusion.15.refs_1_.refs_2_, bf16[768,512]{1,0:T(8,128)(2,1)S(1)} %pad_maximum_fusion.15.refs_1_.refs_2_, ...), custom_call_target="tpu_custom_call" | custom-call | flops 8053063680 | bytes 5898240 | tf_op jit(solution)/shard_map/attend_back/pallas_call | solution.py:455
  230.6 24.2 %collective-permute-done.47 = bf16[3,4,96,768]{3,2,0,1:T(8,128)(2,1)} collective-permute-done((bf16[3,4,96,768]{3,2,0,1:T(8,128)(2,1)}, bf16[3,4,96,768]{3,2,0,1:T(8,128)(2,1)}, u32[]{:S(2)}, u32[]{:S(2)}) %collective-permute-start.47) | collective-permute-done | bytes 1769504 | tf_op jit(solution)/shard_map/ppermute | solution.py:1002
  254.8 2.1 fusion
  263.7 3.2 multiply_reduce_fusion
  266.9 4.8 %fusion.2 = (bf16[768,1024]{1,0:T(8,128)(2,1)S(1)}, f32[768,1024]{1,0:T(8,128)}) fusion(bf16[2,768,1024]{2,1,0:T(8,128)(2,1)S(1)} %copy-done.32, s32[]{:T(128)S(6)} %select_n.343, f32[1024]{0:T(1024)S(1)} %broadcast_multiply_fusion.2, f32[768,1024]{1,0:T(8,128)S(1)} %get-tuple-element.146, f32[1024]{0:T(1024)S(1)} %get-tuple-element.222, ...), kind=kLoop, calls=%fused_computation.16 | loop fusion | flops 11010048 | bytes 18905092 | tf_op jit(solution)/shard_map/convert_element_type | solution.py:1086
  273.1 13.1 %attend_back.3 = (bf16[384,1024]{1,0:T(8,128)(2,1)S(1)}, bf16[384,1024]{1,0:T(8,128)(2,1)S(1)}, bf16[384,1024]{1,0:T(8,128)(2,1)S(1)}) custom-call(bf16[1152,1024]{1,0:T(8,128)(2,1)S(1)} %pad_maximum_fusion.6.refs_0_.refs_1_.refs_2_, bf16[1152,1024]{1,0:T(8,128)(2,1)S(1)} %pad_maximum_fusion.6.refs_0_.refs_1_.refs_2_, ...), custom_call_target="tpu_custom_call" | custom-call | flops 9663676416 | bytes 7864320 | tf_op jit(solution)/shard_map/attend_back/pallas_call | solution.py:455
  287.1 1.9 fusion.90
  289.0 2.7 outer_products.1
  292.5 2.3 collective-permute-start.49
  296.9 1.9 self_products.2
  298.9 2.0 into_active.1
  304.4 4.5 %fusion.36 = (bf16[2,1,192,1024]{3,2,0,1:T(8,128)(2,1)S(1)}, bf16[2,1,192,1024]{3,2,0,1:T(8,128)(2,1)S(1)}) fusion(f32[1,1,192,1024]{3,2,0,1:T(8,128)S(1)} %bitcast.487, f32[1,1,192,1024]{3,2,0,1:T(8,128)S(1)} %bitcast.486, f32[]{:T(128)} %bitcast.2, f32[]{:T(128)} %bitcast.1, f32[]{:T(128)} %bitcast, pred[]{:T(512)S(6)} %eq.121, ...), kind=kLoop, calls=%fused_computation.102 | loop fusion | flops 6684672 | bytes 4718617 | tf_op jit(solution)/shard_map/convert.10
  314.4 13.5 %collective-permute-done.42 = bf16[2,768,384]{2,1,0:T(8,128)(2,1)S(1)} collective-permute-done((bf16[2,768,384]{2,1,0:T(8,128)(2,1)S(1)}, bf16[2,768,384]{2,1,0:T(8,128)(2,1)S(1)}, u32[]{:S(2)}, u32[]{:S(2)}) %collective-permute-start.42) | collective-permute-done | bytes 1179680 | tf_op jit(solution)/shard_map/ppermute | solution.py:867
  332.6 2.8 copy.73
  341.5 1.9 self_products.3
  344.2 3.8 state_grads.1
  352.5 2.5 fusion.132
  355.6 11.4 %all_sum.1 = f32[4,768]{1,0:T(4,128)} custom-call(f32[4,768]{1,0:T(4,128)} %pad_maximum_fusion.18.part_ref), custom_call_target="tpu_custom_call" | custom-call | tf_op jit(solution)/shard_map/all_sum/pallas_call | solution.py:534
  370.9 2.7 collective-permute-start.45
  374.3 4.1 collective-permute-done.46.refs_3_
  378.7 7.2 %collective-permute-done.44.refs_1_ = bf16[2,96,384]{2,1,0:T(8,128)(2,1)S(1)} collective-permute-done((bf16[2,96,384]{2,1,0:T(8,128)(2,1)S(1)}, bf16[2,96,384]{2,1,0:T(8,128)(2,1)S(1)}, u32[]{:S(2)}, u32[]{:S(2)}) %collective-permute-start.44) | collective-permute-done | bytes 147488 | tf_op jit(solution)/shard_map/ppermute | solution.py:1011
  385.9 21.0 %finish.1 = (f32[3,192,96]{2,1,0:T(8,128)S(1)}, f32[192,96]{1,0:T(8,128)S(1)}, f32[3,192,96]{2,1,0:T(8,128)S(1)}, f32[192,96]{1,0:T(8,128)S(1)}, f32[2,96,768]{2,1,0:T(8,128)S(1)}, /*index=5*/f32[768,96]{1,0:T(8,128)S(1)}) custom-call(bf16[2,2,4,96,384]{4,3,2,1,0:T(8,128)(2,1)S(1)} %bitcast.484, bf16[2,2,4,96,384]{4,3,2,1,0:T(8,128)(2,1)} %bitcast.138.got_ref, ...), custom_call_target="tpu_custom_call" | custom-call | tf_op jit(solution)/shard_map/finish/pallas_call | solution.py:637
  (413 shorter events, 125.5 us)
Async XLA Ops:
  0.7 26.5 %collective-permute-start.4 = (bf16[192,768]{1,0:T(8,128)(2,1)}, bf16[192,768]{1,0:T(8,128)(2,1)}, u32[]{:S(2)}, u32[]{:S(2)}) collective-permute-start(bf16[192,768]{1,0:T(8,128)(2,1)} %param.19), channel_id=1, source_target_pairs={{0,1},{1,0},{2,3},{3,2},{4,5},{5,4},{6,7},{7,6},{8,9},{9,8},{10,11... | collective-permute-start | bytes 884744 | tf_op jit(solution)/shard_map/ppermute | solution.py:864
  1.2 20.8 %collective-permute-start.3 = (bf16[192,768]{1,0:T(8,128)(2,1)}, bf16[192,768]{1,0:T(8,128)(2,1)}, u32[]{:S(2)}, u32[]{:S(2)}) collective-permute-start(bf16[192,768]{1,0:T(8,128)(2,1)} %param.19), channel_id=1, source_target_pairs={{0,2},{1,3},{2,0},{3,1},{4,6},{5,7},{6,4},{7,5},{8,10},{9,11},{10,... | collective-permute-start | bytes 884744 | tf_op jit(solution)/shard_map/ppermute | solution.py:867
  4.8 16.8 %collective-permute-start.17 = (bf16[128,768]{1,0:T(8,128)(2,1)S(1)}, bf16[128,768]{1,0:T(8,128)(2,1)S(1)}, u32[]{:S(2)}, u32[]{:S(2)}) collective-permute-start(bf16[128,768]{1,0:T(8,128)(2,1)S(1)} %bitcast.511), channel_id=1, source_target_pairs={{0,1},{1,0},{2,3},{3,2},{4,5},{5,4},{6,7},{7,6},{8,9},{9,8},{10,11... | collective-permute-start | bytes 589832 | tf_op jit(solution)/shard_map/ppermute | solution.py:864
  5.1 15.9 %collective-permute-start.16 = (bf16[128,768]{1,0:T(8,128)(2,1)S(1)}, bf16[128,768]{1,0:T(8,128)(2,1)}, u32[]{:S(2)}, u32[]{:S(2)}) collective-permute-start(bf16[128,768]{1,0:T(8,128)(2,1)S(1)} %get-tuple-element.219), channel_id=1, source_target_pairs={{0,2},{1,3},{2,0},{3,1},{4,6},{5,7},{6,4},{7,5},{8,10},{9,11},{10,... | collective-permute-start | bytes 589832 | tf_op jit(solution)/shard_map/ppermute | solution.py:867
  5.3 47.0 %collective-permute-start.6 = (bf16[3,192,768]{2,1,0:T(8,128)(2,1)}, bf16[3,192,768]{2,1,0:T(8,128)(2,1)}, u32[]{:S(2)}, u32[]{:S(2)}) collective-permute-start(bf16[3,192,768]{2,1,0:T(8,128)(2,1)} %param.18), channel_id=1, source_target_pairs={{0,2},{1,3},{2,0},{3,1},{4,6},{5,7},{6,4},{7,5},{8,10},{9,11},{10,... | collective-permute-start | bytes 2654216 | tf_op jit(solution)/shard_map/ppermute | solution.py:867
  21.7 19.8 %collective-permute-start.10 = (bf16[192,768]{1,0:T(8,128)(2,1)}, bf16[192,768]{1,0:T(8,128)(2,1)}, u32[]{:S(2)}, u32[]{:S(2)}) collective-permute-start(bf16[192,768]{1,0:T(8,128)(2,1)} %param.21), channel_id=1, source_target_pairs={{0,2},{1,3},{2,0},{3,1},{4,6},{5,7},{6,4},{7,5},{8,10},{9,11},{10,... | collective-permute-start | bytes 884744 | tf_op jit(solution)/shard_map/ppermute | solution.py:867
  22.3 27.4 %collective-permute-start = (bf16[192,1024]{1,0:T(8,128)(2,1)}, bf16[192,1024]{1,0:T(8,128)(2,1)S(1)}, u32[]{:S(2)}, u32[]{:S(2)}) collective-permute-start(bf16[192,1024]{1,0:T(8,128)(2,1)} %get-tuple-element.212), channel_id=1, source_target_pairs={{0,2},{1,3},{2,0},{3,1},{4,6},{5,7},{6,4},{7,5},{8,10},{9,11},{10,... | collective-permute-start | bytes 1179656 | tf_op jit(solution)/shard_map/ppermute | solution.py:867
  23.8 28.2 %collective-permute-start.5 = (bf16[192,768]{1,0:T(8,128)(2,1)}, bf16[192,768]{1,0:T(8,128)(2,1)}, u32[]{:S(2)}, u32[]{:S(2)}) collective-permute-start(bf16[192,768]{1,0:T(8,128)(2,1)} %collective-permute-done.3), channel_id=1, source_target_pairs={{0,1},{1,0},{2,3},{3,2},{4,5},{5,4},{6,7},{7,6},{8,9},{9,8},{10,11... | collective-permute-start | bytes 884744 | tf_op jit(solution)/shard_map/ppermute | solution.py:864
  27.1 29.9 %collective-permute-start.11 = (bf16[192,768]{1,0:T(8,128)(2,1)}, bf16[192,768]{1,0:T(8,128)(2,1)S(1)}, u32[]{:S(2)}, u32[]{:S(2)}) collective-permute-start(bf16[192,768]{1,0:T(8,128)(2,1)} %param.21), channel_id=1, source_target_pairs={{0,1},{1,0},{2,3},{3,2},{4,5},{5,4},{6,7},{7,6},{8,9},{9,8},{10,11... | collective-permute-start | bytes 884744 | tf_op jit(solution)/shard_map/ppermute | solution.py:864
  41.4 27.4 %collective-permute-start.13 = (bf16[3,192,768]{2,1,0:T(8,128)(2,1)}, bf16[3,192,768]{2,1,0:T(8,128)(2,1)}, u32[]{:S(2)}, u32[]{:S(2)}) collective-permute-start(bf16[3,192,768]{2,1,0:T(8,128)(2,1)} %param.20), channel_id=1, source_target_pairs={{0,2},{1,3},{2,0},{3,1},{4,6},{5,7},{6,4},{7,5},{8,10},{9,11},{10,... | collective-permute-start | bytes 2654216 | tf_op jit(solution)/shard_map/ppermute | solution.py:867
  49.8 7.4 %collective-permute-start.1 = (bf16[192,1024]{1,0:T(8,128)(2,1)}, bf16[192,1024]{1,0:T(8,128)(2,1)S(1)}, u32[]{:S(2)}, u32[]{:S(2)}) collective-permute-start(bf16[192,1024]{1,0:T(8,128)(2,1)} %bitcast.9.refs_0_), channel_id=1, source_target_pairs={{0,1},{1,0},{2,3},{3,2},{4,5},{5,4},{6,7},{7,6},{8,9},{9,8},{10,11... | collective-permute-start | bytes 1179656 | tf_op jit(solution)/shard_map/ppermute | solution.py:864
  51.9 6.8 %collective-permute-start.12 = (bf16[192,768]{1,0:T(8,128)(2,1)}, bf16[192,768]{1,0:T(8,128)(2,1)S(1)}, u32[]{:S(2)}, u32[]{:S(2)}) collective-permute-start(bf16[192,768]{1,0:T(8,128)(2,1)} %collective-permute-done.10), channel_id=1, source_target_pairs={{0,1},{1,0},{2,3},{3,2},{4,5},{5,4},{6,7},{7,6},{8,9},{9,8},{10,11... | collective-permute-start | bytes 884744 | tf_op jit(solution)/shard_map/ppermute | solution.py:864
  52.4 33.0 %collective-permute-start.21 = (bf16[2,192,1024]{2,1,0:T(8,128)(2,1)}, bf16[2,192,1024]{2,1,0:T(8,128)(2,1)}, u32[]{:S(2)}, u32[]{:S(2)}) collective-permute-start(bf16[2,192,1024]{2,1,0:T(8,128)(2,1)} %get-tuple-element.58), channel_id=1, source_target_pairs={{0,2},{1,3},{2,0},{3,1},{4,6},{5,7},{6,4},{7,5},{8,10},{9,11},{10,... | collective-permute-start | bytes 2359304 | tf_op jit(solution)/shard_map/ppermute | solution.py:867
  57.1 9.2 %collective-permute-start.7 = (bf16[3,192,384]{2,1,0:T(8,128)(2,1)S(1)}, bf16[3,192,384]{2,1,0:T(8,128)(2,1)}, u32[]{:S(2)}, u32[]{:S(2)}) collective-permute-start(bf16[3,192,384]{2,1,0:T(8,128)(2,1)S(1)} %get-tuple-element.199.refs_7_), channel_id=1, source_target_pairs={{0,1},{1,0},{2,3},{3,2},{4,5},{5,4},{6,7},{7,6},{8,9},{9,8},{10,11... | collective-permute-start | bytes 1327112 | tf_op jit(solution)/shard_map/ppermute | solution.py:864
  57.2 28.3 %collective-permute-start.8 = (bf16[3,192,384]{2,1,0:T(8,128)(2,1)S(1)}, bf16[3,192,384]{2,1,0:T(8,128)(2,1)}, u32[]{:S(2)}, u32[]{:S(2)}) collective-permute-start(bf16[3,192,384]{2,1,0:T(8,128)(2,1)S(1)} %get-tuple-element.201.refs_9_), channel_id=1, source_target_pairs={{0,1},{1,0},{2,3},{3,2},{4,5},{5,4},{6,7},{7,6},{8,9},{9,8},{10,11... | collective-permute-start | bytes 1327112 | tf_op jit(solution)/shard_map/ppermute | solution.py:864
  62.3 37.1 %collective-permute-start.14 = (bf16[3,192,768]{2,1,0:T(8,128)(2,1)}, bf16[3,192,768]{2,1,0:T(8,128)(2,1)}, u32[]{:S(2)}, u32[]{:S(2)}) collective-permute-start(bf16[3,192,768]{2,1,0:T(8,128)(2,1)} %param.20), channel_id=1, source_target_pairs={{0,1},{1,0},{2,3},{3,2},{4,5},{5,4},{6,7},{7,6},{8,9},{9,8},{10,11... | collective-permute-start | bytes 2654216 | tf_op jit(solution)/shard_map/ppermute | solution.py:864
  66.3 37.8 %collective-permute-start.22 = (bf16[2,192,1024]{2,1,0:T(8,128)(2,1)}, bf16[2,192,1024]{2,1,0:T(8,128)(2,1)S(1)}, u32[]{:S(2)}, u32[]{:S(2)}) collective-permute-start(bf16[2,192,1024]{2,1,0:T(8,128)(2,1)} %get-tuple-element.58), channel_id=1, source_target_pairs={{0,1},{1,0},{2,3},{3,2},{4,5},{5,4},{6,7},{7,6},{8,9},{9,8},{10,11... | collective-permute-start | bytes 2359304 | tf_op jit(solution)/shard_map/ppermute | solution.py:864
  68.8 30.6 %collective-permute-start.15 = (bf16[3,192,768]{2,1,0:T(8,128)(2,1)}, bf16[3,192,768]{2,1,0:T(8,128)(2,1)S(1)}, u32[]{:S(2)}, u32[]{:S(2)}) collective-permute-start(bf16[3,192,768]{2,1,0:T(8,128)(2,1)} %collective-permute-done.13), channel_id=1, source_target_pairs={{0,1},{1,0},{2,3},{3,2},{4,5},{5,4},{6,7},{7,6},{8,9},{9,8},{10,11... | collective-permute-start | bytes 2654216 | tf_op jit(solution)/shard_map/ppermute | solution.py:864
  85.4 18.6 %collective-permute-start.23 = (bf16[2,192,1024]{2,1,0:T(8,128)(2,1)}, bf16[2,192,1024]{2,1,0:T(8,128)(2,1)S(1)}, u32[]{:S(2)}, u32[]{:S(2)}) collective-permute-start(bf16[2,192,1024]{2,1,0:T(8,128)(2,1)} %collective-permute-done.21), channel_id=1, source_target_pairs={{0,1},{1,0},{2,3},{3,2},{4,5},{5,4},{6,7},{7,6},{8,9},{9,8},{10,11... | collective-permute-start | bytes 2359304 | tf_op jit(solution)/shard_map/ppermute | solution.py:864
  98.9 7.8 %collective-permute-start.9 = (bf16[384,1024]{1,0:T(8,128)(2,1)S(1)}, bf16[384,1024]{1,0:T(8,128)(2,1)S(1)}, u32[]{:S(2)}, u32[]{:S(2)}) collective-permute-start(bf16[384,1024]{1,0:T(8,128)(2,1)S(1)} %get-tuple-element.56.refs_6_), channel_id=1, source_target_pairs={{0,1},{1,0},{2,3},{3,2},{4,5},{5,4},{6,7},{7,6},{8,9},{9,8},{10,11... | collective-permute-start | bytes 2359304 | tf_op jit(solution)/shard_map/ppermute | solution.py:864
  120.5 4.0 collective-permute-start.19
  136.0 24.2 %collective-permute-start.24 = (bf16[384,1024]{1,0:T(8,128)(2,1)S(1)}, bf16[384,1024]{1,0:T(8,128)(2,1)S(1)}, u32[]{:S(2)}, u32[]{:S(2)}) collective-permute-start(bf16[384,1024]{1,0:T(8,128)(2,1)S(1)} %constant_dynamic-slice_fusion.8), channel_id=1, source_target_pairs={{0,2},{1,3},{2,0},{3,1},{4,6},{5,7},{6,4},{7,5},{8,10},{9,11},{10,... | collective-permute-start | bytes 2359304 | tf_op jit(solution)/shard_map/ppermute | solution.py:867
  147.7 15.5 %collective-permute-start.20 = (bf16[2,192,1024]{2,1,0:T(8,128)(2,1)S(1)}, bf16[2,192,1024]{2,1,0:T(8,128)(2,1)S(1)}, u32[]{:S(2)}, u32[]{:S(2)}) collective-permute-start(bf16[2,192,1024]{2,1,0:T(8,128)(2,1)S(1)} %fusion.97), channel_id=1, source_target_pairs={{0,1},{1,0},{2,3},{3,2},{4,5},{5,4},{6,7},{7,6},{8,9},{9,8},{10,11... | collective-permute-start | bytes 2359304 | tf_op jit(solution)/shard_map/ppermute | solution.py:864
  157.2 51.9 %collective-permute-start.30 = (bf16[2,192,1024]{2,1,0:T(8,128)(2,1)}, bf16[2,192,1024]{2,1,0:T(8,128)(2,1)}, u32[]{:S(2)}, u32[]{:S(2)}) collective-permute-start(bf16[2,192,1024]{2,1,0:T(8,128)(2,1)} %fusion.95), channel_id=1, source_target_pairs={{0,1},{1,0},{2,3},{3,2},{4,5},{5,4},{6,7},{7,6},{8,9},{9,8},{10,11... | collective-permute-start | bytes 2359304 | tf_op jit(solution)/shard_map/ppermute | solution.py:864
  160.2 3.6 collective-permute-start.25
  174.9 17.9 %collective-permute-start.28 = (bf16[2,192,1024]{2,1,0:T(8,128)(2,1)S(1)}, bf16[2,192,1024]{2,1,0:T(8,128)(2,1)S(1)}, u32[]{:S(2)}, u32[]{:S(2)}) collective-permute-start(bf16[2,192,1024]{2,1,0:T(8,128)(2,1)S(1)} %fusion.98), channel_id=1, source_target_pairs={{0,1},{1,0},{2,3},{3,2},{4,5},{5,4},{6,7},{7,6},{8,9},{9,8},{10,11... | collective-permute-start | bytes 2359304 | tf_op jit(solution)/shard_map/ppermute | solution.py:864
  182.0 6.0 %collective-permute-start.26 = (bf16[2,192,1024]{2,1,0:T(8,128)(2,1)S(1)}, bf16[2,192,1024]{2,1,0:T(8,128)(2,1)S(1)}, u32[]{:S(2)}, u32[]{:S(2)}) collective-permute-start(bf16[2,192,1024]{2,1,0:T(8,128)(2,1)S(1)} %fusion.96), channel_id=1, source_target_pairs={{0,1},{1,0},{2,3},{3,2},{4,5},{5,4},{6,7},{7,6},{8,9},{9,8},{10,11... | collective-permute-start | bytes 2359304 | tf_op jit(solution)/shard_map/ppermute | solution.py:864
  189.2 19.9 %collective-permute-start.27 = (bf16[2,192,1024]{2,1,0:T(8,128)(2,1)}, bf16[2,192,1024]{2,1,0:T(8,128)(2,1)S(1)}, u32[]{:S(2)}, u32[]{:S(2)}) collective-permute-start(bf16[2,192,1024]{2,1,0:T(8,128)(2,1)} %fusion.60), channel_id=1, source_target_pairs={{0,2},{1,3},{2,0},{3,1},{4,6},{5,7},{6,4},{7,5},{8,10},{9,11},{10,... | collective-permute-start | bytes 2359304 | tf_op jit(solution)/shard_map/ppermute | solution.py:867
  210.7 5.3 %collective-permute-start.31 = (bf16[2,192,1024]{2,1,0:T(8,128)(2,1)S(1)}, bf16[2,192,1024]{2,1,0:T(8,128)(2,1)S(1)}, u32[]{:S(2)}, u32[]{:S(2)}) collective-permute-start(bf16[2,192,1024]{2,1,0:T(8,128)(2,1)S(1)} %get-tuple-element.155), channel_id=1, source_target_pairs={{0,1},{1,0},{2,3},{3,2},{4,5},{5,4},{6,7},{7,6},{8,9},{9,8},{10,11... | collective-permute-start | bytes 2359304 | tf_op jit(solution)/shard_map/ppermute | solution.py:864
  213.9 40.9 %collective-permute-start.47 = (bf16[3,4,96,768]{3,2,0,1:T(8,128)(2,1)}, bf16[3,4,96,768]{3,2,0,1:T(8,128)(2,1)}, u32[]{:S(2)}, u32[]{:S(2)}) collective-permute-start(bf16[3,4,96,768]{3,2,0,1:T(8,128)(2,1)} %bitcast.479), channel_id=1, source_target_pairs={{0,4},{4,0},{8,12},{12,8},{16,20},{20,16},{24,28},{28,24},{1,5},{5... | collective-permute-start | bytes 5308424 | tf_op jit(solution)/shard_map/ppermute | solution.py:1002
  215.5 87.1 %collective-permute-start.29 = (bf16[2,192,1024]{2,1,0:T(8,128)(2,1)S(1)}, bf16[2,192,1024]{2,1,0:T(8,128)(2,1)}, u32[]{:S(2)}, u32[]{:S(2)}) collective-permute-start(bf16[2,192,1024]{2,1,0:T(8,128)(2,1)S(1)} %pad_maximum_fusion.16), channel_id=1, source_target_pairs={{0,2},{1,3},{2,0},{3,1},{4,6},{5,7},{6,4},{7,5},{8,10},{9,11},{10,... | collective-permute-start | bytes 2359304 | tf_op jit(solution)/shard_map/ppermute | solution.py:867
  230.5 30.2 %collective-permute-start.32 = (bf16[384,512]{1,0:T(8,128)(2,1)S(1)}, bf16[384,512]{1,0:T(8,128)(2,1)S(1)}, u32[]{:S(2)}, u32[]{:S(2)}) collective-permute-start(bf16[384,512]{1,0:T(8,128)(2,1)S(1)} %get-tuple-element.63), channel_id=1, source_target_pairs={{0,1},{1,0},{2,3},{3,2},{4,5},{5,4},{6,7},{7,6},{8,9},{9,8},{10,11... | collective-permute-start | bytes 1179656 | tf_op jit(solution)/shard_map/ppermute | solution.py:864
  257.0 4.1 collective-permute-start.33
  258.4 112.6 %collective-permute-start.50 = (bf16[3,96,768]{2,1,0:T(8,128)(2,1)}, bf16[3,96,768]{2,1,0:T(8,128)(2,1)}, u32[]{:S(2)}, u32[]{:S(2)}) collective-permute-start(bf16[3,96,768]{2,1,0:T(8,128)(2,1)} %get-tuple-element.174), channel_id=1, source_target_pairs={{0,8},{4,12},{8,16},{12,20},{16,24},{20,28},{24,0},{28,4},{1,9},{5... | collective-permute-start | bytes 1327112 | tf_op jit(solution)/shard_map/ppermute | solution.py:1011
  286.2 6.3 %collective-permute-start.36 = (bf16[384,1024]{1,0:T(8,128)(2,1)S(1)}, bf16[384,1024]{1,0:T(8,128)(2,1)S(1)}, u32[]{:S(2)}, u32[]{:S(2)}) collective-permute-start(bf16[384,1024]{1,0:T(8,128)(2,1)S(1)} %get-tuple-element.67.refs_0_), channel_id=1, source_target_pairs={{0,1},{1,0},{2,3},{3,2},{4,5},{5,4},{6,7},{7,6},{8,9},{9,8},{10,11... | collective-permute-start | bytes 2359304 | tf_op jit(solution)/shard_map/ppermute | solution.py:864
  286.6 8.3 %collective-permute-start.37 = (bf16[384,1024]{1,0:T(8,128)(2,1)S(1)}, bf16[384,1024]{1,0:T(8,128)(2,1)S(1)}, u32[]{:S(2)}, u32[]{:S(2)}) collective-permute-start(bf16[384,1024]{1,0:T(8,128)(2,1)S(1)} %get-tuple-element.68.refs_1_), channel_id=1, source_target_pairs={{0,1},{1,0},{2,3},{3,2},{4,5},{5,4},{6,7},{7,6},{8,9},{9,8},{10,11... | collective-permute-start | bytes 2359304 | tf_op jit(solution)/shard_map/ppermute | solution.py:864
  286.8 8.6 %collective-permute-start.38 = (bf16[384,1024]{1,0:T(8,128)(2,1)S(1)}, bf16[384,1024]{1,0:T(8,128)(2,1)S(1)}, u32[]{:S(2)}, u32[]{:S(2)}) collective-permute-start(bf16[384,1024]{1,0:T(8,128)(2,1)S(1)} %get-tuple-element.69.refs_2_), channel_id=1, source_target_pairs={{0,1},{1,0},{2,3},{3,2},{4,5},{5,4},{6,7},{7,6},{8,9},{9,8},{10,11... | collective-permute-start | bytes 2359304 | tf_op jit(solution)/shard_map/ppermute | solution.py:864
  292.5 81.1 %collective-permute-start.49 = (bf16[3,96,768]{2,1,0:T(8,128)(2,1)}, bf16[3,96,768]{2,1,0:T(8,128)(2,1)}, u32[]{:S(2)}, u32[]{:S(2)}) collective-permute-start(bf16[3,96,768]{2,1,0:T(8,128)(2,1)} %get-tuple-element.175), channel_id=1, source_target_pairs={{0,24},{4,28},{8,0},{12,4},{16,8},{20,12},{24,16},{28,20},{1,25},{... | collective-permute-start | bytes 1327112 | tf_op jit(solution)/shard_map/ppermute | solution.py:1011
  294.9 7.9 %collective-permute-start.34 = (bf16[128,768]{1,0:T(8,128)(2,1)S(1)}, bf16[128,768]{1,0:T(8,128)(2,1)S(1)}, u32[]{:S(2)}, u32[]{:S(2)}) collective-permute-start(bf16[128,768]{1,0:T(8,128)(2,1)S(1)} %fusion.90), channel_id=1, source_target_pairs={{0,2},{1,3},{2,0},{3,1},{4,6},{5,7},{6,4},{7,5},{8,10},{9,11},{10,... | collective-permute-start | bytes 589832 | tf_op jit(solution)/shard_map/ppermute | solution.py:867
  295.4 32.5 %collective-permute-start.42 = (bf16[2,768,384]{2,1,0:T(8,128)(2,1)S(1)}, bf16[2,768,384]{2,1,0:T(8,128)(2,1)S(1)}, u32[]{:S(2)}, u32[]{:S(2)}) collective-permute-start(bf16[2,768,384]{2,1,0:T(8,128)(2,1)S(1)} %get-tuple-element.78), channel_id=1, source_target_pairs={{0,2},{1,3},{2,0},{3,1},{4,6},{5,7},{6,4},{7,5},{8,10},{9,11},{10,... | collective-permute-start | bytes 3538952 | tf_op jit(solution)/shard_map/ppermute | solution.py:867
  302.7 8.7 %collective-permute-start.39 = (f32[1,1024]{1,0:T(1,128)S(1)}, f32[1,1024]{1,0:T(1,128)S(1)}, u32[]{:S(2)}, u32[]{:S(2)}) collective-permute-start(f32[1,1024]{1,0:T(1,128)S(1)} %bitcast.524), channel_id=1, source_target_pairs={{0,1},{1,0},{2,3},{3,2},{4,5},{5,4},{6,7},{7,6},{8,9},{9,8},{10,11... | collective-permute-start | bytes 12296 | tf_op jit(solution)/shard_map/ppermute | solution.py:864
  313.8 29.6 %collective-permute-start.40 = (bf16[192,1024]{1,0:T(8,128)(2,1)}, bf16[192,1024]{1,0:T(8,128)(2,1)}, u32[]{:S(2)}, u32[]{:S(2)}) collective-permute-start(bf16[192,1024]{1,0:T(8,128)(2,1)} %get-tuple-element.202), channel_id=1, source_target_pairs={{0,2},{1,3},{2,0},{3,1},{4,6},{5,7},{6,4},{7,5},{8,10},{9,11},{10,... | collective-permute-start | bytes 1179656 | tf_op jit(solution)/shard_map/ppermute | solution.py:867
  330.1 38.3 %collective-permute-start.43 = (bf16[2,4,96,384]{3,2,0,1:T(8,128)(2,1)}, bf16[2,4,96,384]{3,2,0,1:T(8,128)(2,1)}, u32[]{:S(2)}, u32[]{:S(2)}) collective-permute-start(bf16[2,4,96,384]{3,2,0,1:T(8,128)(2,1)} %bitcast.480), channel_id=1, source_target_pairs={{0,4},{4,0},{8,12},{12,8},{16,20},{20,16},{24,28},{28,24},{1,5},{5... | collective-permute-start | bytes 1769480 | tf_op jit(solution)/shard_map/ppermute | solution.py:1002
  335.4 50.5 %collective-permute-start.41 = (bf16[2,2,384,384]{3,2,1,0:T(8,128)(2,1)}, bf16[2,2,384,384]{3,2,1,0:T(8,128)(2,1)}, u32[]{:S(2)}, u32[]{:S(2)}) collective-permute-start(bf16[2,2,384,384]{3,2,1,0:T(8,128)(2,1)} %copy-done.23), channel_id=1, source_target_pairs={{0,2},{1,3},{2,0},{3,1},{4,6},{5,7},{6,4},{7,5},{8,10},{9,11},{10,... | collective-permute-start | bytes 3538952 | tf_op jit(solution)/shard_map/ppermute | solution.py:867
  343.4 30.9 %collective-permute-start.48 = (bf16[3,96,768]{2,1,0:T(8,128)(2,1)}, bf16[3,96,768]{2,1,0:T(8,128)(2,1)}, u32[]{:S(2)}, u32[]{:S(2)}) collective-permute-start(bf16[3,96,768]{2,1,0:T(8,128)(2,1)} %get-tuple-element.176), channel_id=1, source_target_pairs={{0,16},{4,20},{8,24},{12,28},{16,0},{20,4},{24,8},{28,12},{1,17},{... | collective-permute-start | bytes 1327112 | tf_op jit(solution)/shard_map/ppermute | solution.py:1011
  369.8 8.6 %collective-permute-start.46 = (bf16[2,96,384]{2,1,0:T(8,128)(2,1)S(1)}, bf16[2,96,384]{2,1,0:T(8,128)(2,1)S(1)}, u32[]{:S(2)}, u32[]{:S(2)}) collective-permute-start(bf16[2,96,384]{2,1,0:T(8,128)(2,1)S(1)} %get-tuple-element.214), channel_id=1, source_target_pairs={{0,8},{4,12},{8,16},{12,20},{16,24},{20,28},{24,0},{28,4},{1,9},{5... | collective-permute-start | bytes 442376 | tf_op jit(solution)/shard_map/ppermute | solution.py:1011
  370.9 7.8 %collective-permute-start.45 = (bf16[2,96,384]{2,1,0:T(8,128)(2,1)S(1)}, bf16[2,96,384]{2,1,0:T(8,128)(2,1)S(1)}, u32[]{:S(2)}, u32[]{:S(2)}) collective-permute-start(bf16[2,96,384]{2,1,0:T(8,128)(2,1)S(1)} %get-tuple-element.215), channel_id=1, source_target_pairs={{0,24},{4,28},{8,0},{12,4},{16,8},{20,12},{24,16},{28,20},{1,25},{... | collective-permute-start | bytes 442376 | tf_op jit(solution)/shard_map/ppermute | solution.py:1011
  373.7 12.2 %collective-permute-start.44 = (bf16[2,96,384]{2,1,0:T(8,128)(2,1)S(1)}, bf16[2,96,384]{2,1,0:T(8,128)(2,1)S(1)}, u32[]{:S(2)}, u32[]{:S(2)}) collective-permute-start(bf16[2,96,384]{2,1,0:T(8,128)(2,1)S(1)} %get-tuple-element.216), channel_id=1, source_target_pairs={{0,16},{4,20},{8,24},{12,28},{16,0},{20,4},{24,8},{28,12},{1,17},{... | collective-permute-start | bytes 442376 | tf_op jit(solution)/shard_map/ppermute | solution.py:1011
  (104 other events, 693.9 us)

commit v3 on v2

--- a/solution.py
+++ b/solution.py
@@ -484,8 +484,14 @@
     return lax.dynamic_index_in_dim(array, index, axis, keepdims=False)
 
 
-def all_sum_kernel(dp_size, mp_size, part_ref, out_ref, mp_slots, row_sum, dp_slots, *sems):
-    mp_send, mp_recv, dp_send, dp_recv = sems
+def all_sum_kernel(dp_size, mp_size, *refs):
+    early_refs, (late_ref, gains_ref, out_ref) = refs[:6], refs[6:9]
+    part_ref, mp_slots, row_sum, dp_slots, mp_send, mp_recv, dp_send, dp_recv = refs[9:]
+    late = [late_ref[0, j] + late_ref[1, j] for j in range(2)]
+    scalars = [ref[0, 0] + (late[i] if i < 2 else 0.0) for i, ref in enumerate(early_refs)]
+    lane = lax.broadcasted_iota(jnp.int32, (1, part_ref.shape[1]), 1)
+    part_ref[:3, :] = gains_ref[...]
+    part_ref[3:, :] = sum(jnp.where(lane == i, value, 0.0) for i, value in enumerate(scalars))
     dp, mp = lax.axis_index(DP), lax.axis_index(MP)
     mp_peers = [lax.rem(mp + s, mp_size) for s in range(1, mp_size)]
     dp_peers = [lax.rem(dp + s, dp_size) for s in range(1, dp_size)]
@@ -530,16 +536,20 @@
     return total
 
 
-def all_sum(part, dp_size, mp_size):
+def all_sum(early, late, gains, dp_size, mp_size):
+    whole = pl.BlockSpec(memory_space=pltpu.VMEM)
+    smem = pl.BlockSpec(memory_space=pltpu.SMEM)
+    shape = (4, gains.shape[1])
     return pl.pallas_call(
         functools.partial(all_sum_kernel, dp_size, mp_size),
-        out_shape=jax.ShapeDtypeStruct(part.shape, part.dtype),
-        in_specs=[pl.BlockSpec(memory_space=pltpu.VMEM)],
-        out_specs=pl.BlockSpec(memory_space=pltpu.VMEM),
+        out_shape=jax.ShapeDtypeStruct(shape, gains.dtype),
+        in_specs=[smem] * 7 + [whole],
+        out_specs=whole,
         scratch_shapes=[
-            pltpu.VMEM((mp_size - 1, *part.shape), part.dtype),
-            pltpu.VMEM(part.shape, part.dtype),
-            pltpu.VMEM((dp_size - 1, *part.shape), part.dtype),
+            pltpu.VMEM(shape, gains.dtype),
+            pltpu.VMEM((mp_size - 1, *shape), gains.dtype),
+            pltpu.VMEM(shape, gains.dtype),
+            pltpu.VMEM((dp_size - 1, *shape), gains.dtype),
             pltpu.SemaphoreType.DMA((mp_size - 1,)),
             pltpu.SemaphoreType.DMA((mp_size - 1,)),
             pltpu.SemaphoreType.DMA((dp_size - 1,)),
@@ -547,14 +557,20 @@
         ],
         compiler_params=pltpu.CompilerParams(collective_id=0, has_side_effects=True),
         name="all_sum",
-    )(part)
+    )(*[value.reshape(1, 1) for value in early], late, gains)
 
 
 def finish_kernel(dp_size, keep_ref, got_ref, *refs):
-    side_refs, ffn_refs = refs[:4], refs[4:8]
+    terms = refs[:8]
     qkv_out, out_out, cross_out, cross_out_out, in_out, down_out = refs[8:14]
     step_send, step_land, far_send, far_land = refs[14:18]
     step_sems, far_sems = refs[18:20], refs[20:22]
+    side_terms, ffn_terms, load_sem = refs[22:]
+    loads = []
+    for i, ref in enumerate(terms):
+        place = side_terms.at[i] if i < 4 else ffn_terms.at[i - 4]
+        loads.append(pltpu.make_async_copy(ref, place, load_sem.at[i]))
+        loads[i].start()
     bf16, f32 = jnp.bfloat16, jnp.float32
     dp, mp = lax.axis_index(DP), lax.axis_index(MP)
     core = lax.rem(mp, 2)
@@ -605,10 +621,12 @@
                 else:
                     second[...] = piece
 
-    turned(sum(ref[...].astype(f32) for ref in side_refs), cross_out, cross_out_out)
+    for load in loads:
+        load.wait()
+    turned(sum(side_terms[i].astype(f32) for i in range(4)), cross_out, cross_out_out)
     for mat in range(2):
-        in_out[mat] = sum(ref[mat].astype(f32) for ref in ffn_refs)
-    down_out[...] = sum(ref[2].astype(f32) for ref in ffn_refs).T
+        in_out[mat] = sum(ffn_terms[i, mat].astype(f32) for i in range(4))
+    down_out[...] = sum(ffn_terms[i, 2].astype(f32) for i in range(4)).T
 
     going = []
     for k, place in enumerate(places):
@@ -637,7 +655,7 @@
     return pl.pallas_call(
         functools.partial(finish_kernel, dp_size),
         out_shape=[jax.ShapeDtypeStruct(shape, jnp.float32) for shape in shapes],
-        in_specs=[whole] * 10,
+        in_specs=[whole] * 2 + [pl.BlockSpec(memory_space=pl.ANY)] * 8,
         out_specs=[whole] * 6,
         scratch_shapes=[
             pltpu.VMEM((count, *block), jnp.bfloat16),
@@ -648,6 +666,9 @@
             dma((count,)),
             dma((count - 1,)),
             dma((count - 1,)),
+            pltpu.VMEM((4, *side_terms[0].shape), jnp.bfloat16),
+            pltpu.VMEM((4, *ffn_terms[0].shape), jnp.bfloat16),
+            dma((8,)),
         ],
         compiler_params=pltpu.CompilerParams(
             collective_id=1, has_side_effects=True, vmem_limit_bytes=40 << 20
@@ -1130,20 +1151,9 @@
     grad_state, late_sums = state_grads(
         predict, chip.astype(jnp.int32).reshape(1), wide_state, cotangent, grad_active[0], active_got
     )
-    grad_predict = (
-        early_sums[0] + late_sums[0, 0] + late_sums[1, 0],
-        early_sums[1] + late_sums[0, 1] + late_sums[1, 1],
-        early_sums[2],
-        early_sums[3],
-    )
-    lane = jnp.arange(width, dtype=jnp.int32)
-    scalars = sum(
-        jnp.where(lane == i, value, 0.0)
-        for i, value in enumerate((*grad_predict, grad_correct[0], grad_correct[1]))
-    )
-    total = all_sum(
-        jnp.stack([gain_grad_a, 0.5 * gain_grad_b, 0.5 * gain_grad_c, scalars]), dp_size, 4
-    )
+    early = (*early_sums, *grad_correct)
+    gain_sums = jnp.stack([gain_grad_a, 0.5 * gain_grad_b, 0.5 * gain_grad_c])
+    total = all_sum(early, late_sums, gain_sums, dp_size, 4)
 
     return (
         new_state,

time: 420 us -> 436 us (1.038)
  waiting for transfers between devices: 103 us -> 121 us
  Pallas kernels: 87.8 us -> 97.2 us
  matrix products: 69.6 us -> 61.8 us
    ppermute x14, waiting for transfers between devices: 67.3 us -> 84.7 us  [to_peer(): return lax.ppermute(array, MP, peers)]
    pallas_call x1, Pallas kernels: 11.4 us -> 19.6 us  [all_sum(): pl.pallas_call(functools.partial(all_sum_kernel, dp_size, mp_size), out_s...]
    unnamed x211 -> x247, local copies, waits for them, and re-layouts: 29.1 us -> 27 us
  transfers between devices with their start and end apart: 51 -> 51, of which waited for: 10 -> 11; matrix products, arithmetic and copies ran while one was open for 34% -> 31% of each run, Pallas kernels for 14% -> 16%
where the time goes in v3:
time: 436 us; the launch traced here: 429 us
  waiting for transfers between devices  121 us (28%)
  Pallas kernels  97.2 us (22%)
  matrix products  61.8 us (14%)
  other arithmetic  58.2 us (13%)
  local copies, waits for them, and re-layouts  52.4 us (12%)
  starting transfers between devices  36.1 us (8%)
    ppermute x14, waiting for transfers between devices, to_peer(): return lax.ppermute(array, MP, peers)  84.7 us
    pallas_call x4, Pallas kernels, attention_call(): pl.pallas_call(functools.partial(kernel, mask is not None, size), grid=(h...  39.6 us
    unnamed x247, local copies, waits for them, and re-layouts  27 us
    dot_general x12, matrix products, dot_tn(): lax.dot_general(left, right, (((0,), (0,)), ((), ())), preferred_element_...  24 us
    ppermute x2, waiting for transfers between devices, dp_start(): got = lax.ppermute(sent, DP, swap)  23.6 us
    pallas_call x1, Pallas kernels, finish(): pl.pallas_call(functools.partial(finish_kernel, dp_size), out_shape=[jax....  21.5 us
    dot_general x9, matrix products, dot_nn(): lax.dot_general(left, right, (((1,), (0,)), ((), ())), preferred_element_...  20 us
    pallas_call x1, Pallas kernels, all_sum(): pl.pallas_call(functools.partial(all_sum_kernel, dp_size, mp_size), out_s...  19.6 us
  transfers between devices with their start and end apart: 51, of which 11 were waited for; matrix products, arithmetic and copies ran while one was open for 31% of the time, Pallas kernels for 16%

profile of v3, /device:TPU:0, one launch (start us, length us, event | category | flops | bytes accessed | tf_op | source)
XLA Modules:
  0.0 429.1 jit_solution(12048171958784945478)
XLA Ops:
  1.2 2.6 collective-permute-start.3
  5.3 1.7 collective-permute-start.6
  10.8 6.8 %fusion.53 = (f32[]{:T(128)}, f32[]{:T(128)}, f32[]{:T(128)}, f32[]{:T(128)}, bf16[2,192,1024]{2,1,0:T(8,128)(2,1)S(1)}, /*index=5*/bf16[2,192,1024]{2,1,0:T(8,128)(2,1)}) fusion(bf16[2,2,192,1024]{3,2,1,0:T(8,128)(2,1)} %cot_ref.1, bf16[2,2,192,1024]{3,2,1,0:T(8,128)(2,1)} %state_ref.1, f32[]{:T(128)} %bitcast.1, f32[]{:T(128)} %bitcast, f32[]{:T(128)} %bitcast.12, ...), kind=kLoop, calls=%fused_computation.119 | loop fusion | flops 7864316 | bytes 4718624 | tf_op jit(solution)/shard_map/reduce_sum | solution.py:928
  27.5 14.0 %collective-permute-done.10 = bf16[192,768]{1,0:T(8,128)(2,1)} collective-permute-done((bf16[192,768]{1,0:T(8,128)(2,1)}, bf16[192,768]{1,0:T(8,128)(2,1)}, u32[]{:S(2)}, u32[]{:S(2)}) %collective-permute-start.10) | collective-permute-done | bytes 294944 | tf_op jit(solution)/shard_map/ppermute | solution.py:888
  41.4 2.0 collective-permute-start.13
  43.5 6.3 %collective-permute-done.refs_1_ = bf16[192,1024]{1,0:T(8,128)(2,1)S(1)} collective-permute-done((bf16[192,1024]{1,0:T(8,128)(2,1)}, bf16[192,1024]{1,0:T(8,128)(2,1)S(1)}, u32[]{:S(2)}, u32[]{:S(2)}) %collective-permute-start) | collective-permute-done | bytes 393248 | tf_op jit(solution)/shard_map/ppermute | solution.py:888
  49.8 1.9 dynamic-slice_bitcast_fusion.33
  52.4 2.0 collective-permute-start.21
  62.7 3.6 join_norm.1
  66.3 2.5 collective-permute-done.13
  68.8 16.6 %collective-permute-done.21 = bf16[2,192,1024]{2,1,0:T(8,128)(2,1)} collective-permute-done((bf16[2,192,1024]{2,1,0:T(8,128)(2,1)}, bf16[2,192,1024]{2,1,0:T(8,128)(2,1)}, u32[]{:S(2)}, u32[]{:S(2)}) %collective-permute-start.21) | collective-permute-done | bytes 786464 | tf_op jit(solution)/shard_map/ppermute | solution.py:888
  89.8 9.1 %attend.2 = (bf16[384,1024]{1,0:T(8,128)(2,1)S(1)}, f32[6,1,1024]{2,1,0:T(1,128)S(1)}) custom-call(bf16[1152,1024]{1,0:T(8,128)(2,1)S(1)} %pad_maximum_fusion.6.refs_0_.refs_1_.refs_2_, bf16[1152,1024]{1,0:T(8,128)(2,1)S(1)} %pad_maximum_fusion.6.refs_0_.refs_1_.refs_2_, bf16[1152,1024]{1,0:T(8,128)(2,1)S(1)} %pad_maximum_fusion.6.refs_0_.refs_1_.refs_2_, ...), custom_call_target="tpu_custom_call" | custom-call | flops 3865470464 | bytes 3145728 | tf_op jit(solution)/shard_map/attend/pallas_call | solution.py:455
  99.5 1.9 pad_maximum_fusion
  108.6 3.3 multiply_reduce_fusion.3
  114.2 7.3 %attend.3 = (bf16[384,1024]{1,0:T(8,128)(2,1)S(1)}, f32[6,1,1024]{2,1,0:T(1,128)S(1)}) custom-call(bf16[384,1024]{1,0:T(8,128)(2,1)S(1)} %convolution_convert_fusion.2.refs_0_, bf16[768,512]{1,0:T(8,128)(2,1)S(1)} %pad_maximum_fusion.15.refs_1_.refs_2_, bf16[768,512]{1,0:T(8,128)(2,1)S(1)} %pad_maximum_fusion.15.refs_1_.refs_2_), custom_call_target="tpu_custom_call" | custom-call | flops 3221225472 | bytes 2359296 | tf_op jit(solution)/shard_map/attend/pallas_call | solution.py:455
  122.5 3.1 fusion.67
  127.5 1.8 multiply_reduce_fusion.2
  132.4 3.1 fusion.88
  135.6 1.7 collective-permute-start.24
  137.3 6.5 %fusion.25 = (bf16[768,1024]{0,1:T(8,128)(2,1)}, bf16[768,1024]{0,1:T(8,128)(2,1)}, bf16[768,1024]{0,1:T(8,128)(2,1)S(1)}) fusion(f32[1024,768]{1,0:T(8,128)} %fusion.88, f32[1024,768]{1,0:T(8,128)S(1)} %fusion.80, bf16[768,768]{1,0:T(8,128)(2,1)S(1)} %copy-done, bf16[2,768,1024]{2,1,0:T(8,128)(2,1)S(1)} %pad_maximum_fusion.4, s32[]{:T(128)S(6)} %select_n.282), kind=kOutput, calls=%fused_computation.52 | convolution fusion | flops 1228406784 | bytes 13762564 | tf_op jit(solution)/shard_map/dot_general | solution.py:334
  150.3 2.8 fusion.61
  153.5 2.8 fusion.137
  156.6 2.8 fusion.136
  159.9 2.5 maximum_select_fusion.2
  163.9 6.7 %fusion.24 = (bf16[768,1024]{0,1:T(8,128)(2,1)S(1)}, bf16[768,1024]{0,1:T(8,128)(2,1)}, bf16[768,1024]{0,1:T(8,128)(2,1)S(1)}) fusion(f32[1024,768]{1,0:T(8,128)S(1)} %fusion.84, f32[1024,768]{1,0:T(8,128)} %fusion.67, bf16[768,1024]{1,0:T(8,128)(2,1)S(1)} %maximum_select_fusion.2, bf16[2,768,768]{2,1,0:T(8,128)(2,1)S(1)} %copy-done.106), kind=kOutput, calls=%fused_computation.49 | convolution fusion | flops 1228406784 | bytes 13762560 | tf_op jit(solution)/shard_map/dot_general | solution.py:328
  179.7 3.3 add_convert_fusion.4
  190.5 14.0 %collective-permute-done.27 = bf16[2,192,1024]{2,1,0:T(8,128)(2,1)S(1)} collective-permute-done((bf16[2,192,1024]{2,1,0:T(8,128)(2,1)S(1)}, bf16[2,192,1024]{2,1,0:T(8,128)(2,1)S(1)}, u32[]{:S(2)}, u32[]{:S(2)}) %collective-permute-start.27) | collective-permute-done | bytes 786464 | tf_op jit(solution)/shard_map/ppermute | solution.py:888
  215.3 10.2 %attend_back.2 = (bf16[384,1024]{1,0:T(8,128)(2,1)S(1)}, bf16[384,512]{1,0:T(8,128)(2,1)S(1)}, bf16[384,512]{1,0:T(8,128)(2,1)S(1)}) custom-call(bf16[384,1024]{1,0:T(8,128)(2,1)S(1)} %convolution_convert_fusion.2.refs_0_, bf16[768,512]{1,0:T(8,128)(2,1)S(1)} %pad_maximum_fusion.15.refs_1_.refs_2_, bf16[768,512]{1,0:T(8,128)(2,1)S(1)} %pad_maximum_fusion.15.refs_1_.refs_2_, ...), custom_call_target="tpu_custom_call" | custom-call | flops 8053063680 | bytes 5898240 | tf_op jit(solution)/shard_map/attend_back/pallas_call | solution.py:455
  225.6 23.6 %collective-permute-done.47 = bf16[3,4,96,768]{3,2,0,1:T(8,128)(2,1)} collective-permute-done((bf16[3,4,96,768]{3,2,0,1:T(8,128)(2,1)}, bf16[3,4,96,768]{3,2,0,1:T(8,128)(2,1)}, u32[]{:S(2)}, u32[]{:S(2)}) %collective-permute-start.47) | collective-permute-done | bytes 1769504 | tf_op jit(solution)/shard_map/ppermute | solution.py:1023
  249.2 2.1 fusion
  258.0 3.2 multiply_reduce_fusion
  261.1 4.8 %fusion.2 = (bf16[768,1024]{1,0:T(8,128)(2,1)S(1)}, f32[768,1024]{1,0:T(8,128)}) fusion(bf16[2,768,1024]{2,1,0:T(8,128)(2,1)S(1)} %copy-done.43, s32[]{:T(128)S(6)} %select_n.282, f32[1024]{0:T(1024)S(1)} %broadcast_multiply_fusion.2, f32[768,1024]{1,0:T(8,128)S(1)} %get-tuple-element.146, f32[1024]{0:T(1024)S(1)} %get-tuple-element.222, ...), kind=kLoop, calls=%fused_computation.16 | loop fusion | flops 11010048 | bytes 18905092 | tf_op jit(solution)/shard_map/convert_element_type | solution.py:1107
  267.3 13.1 %attend_back.3 = (bf16[384,1024]{1,0:T(8,128)(2,1)S(1)}, bf16[384,1024]{1,0:T(8,128)(2,1)S(1)}, bf16[384,1024]{1,0:T(8,128)(2,1)S(1)}) custom-call(bf16[1152,1024]{1,0:T(8,128)(2,1)S(1)} %pad_maximum_fusion.6.refs_0_.refs_1_.refs_2_, bf16[1152,1024]{1,0:T(8,128)(2,1)S(1)} %pad_maximum_fusion.6.refs_0_.refs_1_.refs_2_, ...), custom_call_target="tpu_custom_call" | custom-call | flops 9663676416 | bytes 7864320 | tf_op jit(solution)/shard_map/attend_back/pallas_call | solution.py:455
  281.9 3.7 outer_products.1
  287.7 2.3 collective-permute-start.49
  292.1 1.9 self_products.2
  294.1 2.0 into_active.1
  300.4 4.3 %fusion.36 = (bf16[2,1,192,1024]{3,2,0,1:T(8,128)(2,1)S(1)}, bf16[2,1,192,1024]{3,2,0,1:T(8,128)(2,1)S(1)}) fusion(f32[1,1,192,1024]{3,2,0,1:T(8,128)S(1)} %bitcast.489, f32[1,1,192,1024]{3,2,0,1:T(8,128)S(1)} %bitcast.488, f32[]{:T(128)} %bitcast.2, f32[]{:T(128)} %bitcast.1, f32[]{:T(128)} %bitcast, pred[]{:T(512)S(6)} %eq.43, ...), kind=kLoop, calls=%fused_computation.102 | loop fusion | flops 6684672 | bytes 4718617 | tf_op jit(solution)/shard_map/convert.10
  310.1 2.0 fusion.43
  313.2 10.0 %collective-permute-done.42 = bf16[2,768,384]{2,1,0:T(8,128)(2,1)} collective-permute-done((bf16[2,768,384]{2,1,0:T(8,128)(2,1)}, bf16[2,768,384]{2,1,0:T(8,128)(2,1)}, u32[]{:S(2)}, u32[]{:S(2)}) %collective-permute-start.42) | collective-permute-done | bytes 1179680 | tf_op jit(solution)/shard_map/ppermute | solution.py:888
  331.4 1.9 self_products.3
  334.5 21.3 %collective-permute-done.40.far_ref = bf16[192,1024]{1,0:T(8,128)(2,1)S(1)} collective-permute-done((bf16[192,1024]{1,0:T(8,128)(2,1)S(1)}, bf16[192,1024]{1,0:T(8,128)(2,1)S(1)}, u32[]{:S(2)}, u32[]{:S(2)}) %collective-permute-start.40) | collective-permute-done | bytes 393248 | tf_op jit(solution)/shard_map/ppermute | solution.py:888
  356.6 3.3 state_grads.1
  360.5 19.6 %all_sum.1 = f32[4,768]{1,0:T(4,128)} custom-call(f32[1,1]{1,0:T(1,128)} %bitcast.157.refs_0_, f32[1,1]{1,0:T(1,128)} %bitcast.158.refs_1_, f32[1,1]{1,0:T(1,128)} %bitcast.159.refs_2_, f32[1,1]{1,0:T(1,128)} %bitcast.160.refs_3_, f32[1,1]{1,0:T(1,128)} %bitcast.161.refs_4_, f32[1,1]{1,0:T(1,128)} %bitcast.162.refs_5_, f32[2,2]{1,0:T(2,128)} %copy-done.39, ...), custom_call_target="tpu_custom_call" | custom-call | tf_op jit(solution)/shard_map/all_sum/pallas_call | solution.py:543
  384.2 2.7 collective-permute-start.45
  387.5 4.1 collective-permute-done.46.refs_3_
  392.7 7.1 %collective-permute-done.44.refs_1_ = bf16[2,96,384]{2,1,0:T(8,128)(2,1)S(1)} collective-permute-done((bf16[2,96,384]{2,1,0:T(8,128)(2,1)S(1)}, bf16[2,96,384]{2,1,0:T(8,128)(2,1)S(1)}, u32[]{:S(2)}, u32[]{:S(2)}) %collective-permute-start.44) | collective-permute-done | bytes 147488 | tf_op jit(solution)/shard_map/ppermute | solution.py:1032
  399.8 21.5 %finish.1 = (f32[3,192,96]{2,1,0:T(8,128)S(1)}, f32[192,96]{1,0:T(8,128)S(1)}, f32[3,192,96]{2,1,0:T(8,128)S(1)}, f32[192,96]{1,0:T(8,128)S(1)}, f32[2,96,768]{2,1,0:T(8,128)S(1)}, /*index=5*/f32[768,96]{1,0:T(8,128)S(1)}) custom-call(bf16[2,2,4,96,384]{4,3,2,1,0:T(8,128)(2,1)S(1)} %bitcast.486, bf16[2,2,4,96,384]{4,3,2,1,0:T(8,128)(2,1)} %bitcast.138.got_ref, ...), custom_call_target="tpu_custom_call" | custom-call | tf_op jit(solution)/shard_map/finish/pallas_call | solution.py:655
  (447 shorter events, 128.7 us)
Async XLA Ops:
  0.7 26.3 %collective-permute-start.4 = (bf16[192,768]{1,0:T(8,128)(2,1)}, bf16[192,768]{1,0:T(8,128)(2,1)}, u32[]{:S(2)}, u32[]{:S(2)}) collective-permute-start(bf16[192,768]{1,0:T(8,128)(2,1)} %param.19), channel_id=1, source_target_pairs={{0,1},{1,0},{2,3},{3,2},{4,5},{5,4},{6,7},{7,6},{8,9},{9,8},{10,11... | collective-permute-start | bytes 884744 | tf_op jit(solution)/shard_map/ppermute | solution.py:885
  1.2 20.7 %collective-permute-start.3 = (bf16[192,768]{1,0:T(8,128)(2,1)}, bf16[192,768]{1,0:T(8,128)(2,1)}, u32[]{:S(2)}, u32[]{:S(2)}) collective-permute-start(bf16[192,768]{1,0:T(8,128)(2,1)} %param.19), channel_id=1, source_target_pairs={{0,2},{1,3},{2,0},{3,1},{4,6},{5,7},{6,4},{7,5},{8,10},{9,11},{10,... | collective-permute-start | bytes 884744 | tf_op jit(solution)/shard_map/ppermute | solution.py:888
  4.8 16.7 %collective-permute-start.17 = (bf16[128,768]{1,0:T(8,128)(2,1)S(1)}, bf16[128,768]{1,0:T(8,128)(2,1)S(1)}, u32[]{:S(2)}, u32[]{:S(2)}) collective-permute-start(bf16[128,768]{1,0:T(8,128)(2,1)S(1)} %bitcast.513), channel_id=1, source_target_pairs={{0,1},{1,0},{2,3},{3,2},{4,5},{5,4},{6,7},{7,6},{8,9},{9,8},{10,11... | collective-permute-start | bytes 589832 | tf_op jit(solution)/shard_map/ppermute | solution.py:885
  5.1 15.7 %collective-permute-start.16 = (bf16[128,768]{1,0:T(8,128)(2,1)S(1)}, bf16[128,768]{1,0:T(8,128)(2,1)}, u32[]{:S(2)}, u32[]{:S(2)}) collective-permute-start(bf16[128,768]{1,0:T(8,128)(2,1)S(1)} %get-tuple-element.219), channel_id=1, source_target_pairs={{0,2},{1,3},{2,0},{3,1},{4,6},{5,7},{6,4},{7,5},{8,10},{9,11},{10,... | collective-permute-start | bytes 589832 | tf_op jit(solution)/shard_map/ppermute | solution.py:888
  5.3 47.0 %collective-permute-start.6 = (bf16[3,192,768]{2,1,0:T(8,128)(2,1)}, bf16[3,192,768]{2,1,0:T(8,128)(2,1)}, u32[]{:S(2)}, u32[]{:S(2)}) collective-permute-start(bf16[3,192,768]{2,1,0:T(8,128)(2,1)} %param.18), channel_id=1, source_target_pairs={{0,2},{1,3},{2,0},{3,1},{4,6},{5,7},{6,4},{7,5},{8,10},{9,11},{10,... | collective-permute-start | bytes 2654216 | tf_op jit(solution)/shard_map/ppermute | solution.py:888
  21.5 19.9 %collective-permute-start.10 = (bf16[192,768]{1,0:T(8,128)(2,1)}, bf16[192,768]{1,0:T(8,128)(2,1)}, u32[]{:S(2)}, u32[]{:S(2)}) collective-permute-start(bf16[192,768]{1,0:T(8,128)(2,1)} %param.21), channel_id=1, source_target_pairs={{0,2},{1,3},{2,0},{3,1},{4,6},{5,7},{6,4},{7,5},{8,10},{9,11},{10,... | collective-permute-start | bytes 884744 | tf_op jit(solution)/shard_map/ppermute | solution.py:888
  22.2 27.5 %collective-permute-start = (bf16[192,1024]{1,0:T(8,128)(2,1)}, bf16[192,1024]{1,0:T(8,128)(2,1)S(1)}, u32[]{:S(2)}, u32[]{:S(2)}) collective-permute-start(bf16[192,1024]{1,0:T(8,128)(2,1)} %get-tuple-element.212), channel_id=1, source_target_pairs={{0,2},{1,3},{2,0},{3,1},{4,6},{5,7},{6,4},{7,5},{8,10},{9,11},{10,... | collective-permute-start | bytes 1179656 | tf_op jit(solution)/shard_map/ppermute | solution.py:888
  23.6 28.3 %collective-permute-start.5 = (bf16[192,768]{1,0:T(8,128)(2,1)}, bf16[192,768]{1,0:T(8,128)(2,1)}, u32[]{:S(2)}, u32[]{:S(2)}) collective-permute-start(bf16[192,768]{1,0:T(8,128)(2,1)} %collective-permute-done.3), channel_id=1, source_target_pairs={{0,1},{1,0},{2,3},{3,2},{4,5},{5,4},{6,7},{7,6},{8,9},{9,8},{10,11... | collective-permute-start | bytes 884744 | tf_op jit(solution)/shard_map/ppermute | solution.py:885
  27.0 30.1 %collective-permute-start.11 = (bf16[192,768]{1,0:T(8,128)(2,1)}, bf16[192,768]{1,0:T(8,128)(2,1)S(1)}, u32[]{:S(2)}, u32[]{:S(2)}) collective-permute-start(bf16[192,768]{1,0:T(8,128)(2,1)} %param.21), channel_id=1, source_target_pairs={{0,1},{1,0},{2,3},{3,2},{4,5},{5,4},{6,7},{7,6},{8,9},{9,8},{10,11... | collective-permute-start | bytes 884744 | tf_op jit(solution)/shard_map/ppermute | solution.py:885
  41.4 27.4 %collective-permute-start.13 = (bf16[3,192,768]{2,1,0:T(8,128)(2,1)}, bf16[3,192,768]{2,1,0:T(8,128)(2,1)}, u32[]{:S(2)}, u32[]{:S(2)}) collective-permute-start(bf16[3,192,768]{2,1,0:T(8,128)(2,1)} %param.20), channel_id=1, source_target_pairs={{0,2},{1,3},{2,0},{3,1},{4,6},{5,7},{6,4},{7,5},{8,10},{9,11},{10,... | collective-permute-start | bytes 2654216 | tf_op jit(solution)/shard_map/ppermute | solution.py:888
  49.8 7.4 %collective-permute-start.1 = (bf16[192,1024]{1,0:T(8,128)(2,1)}, bf16[192,1024]{1,0:T(8,128)(2,1)S(1)}, u32[]{:S(2)}, u32[]{:S(2)}) collective-permute-start(bf16[192,1024]{1,0:T(8,128)(2,1)} %bitcast.9.refs_0_), channel_id=1, source_target_pairs={{0,1},{1,0},{2,3},{3,2},{4,5},{5,4},{6,7},{7,6},{8,9},{9,8},{10,11... | collective-permute-start | bytes 1179656 | tf_op jit(solution)/shard_map/ppermute | solution.py:885
  51.9 6.8 %collective-permute-start.12 = (bf16[192,768]{1,0:T(8,128)(2,1)}, bf16[192,768]{1,0:T(8,128)(2,1)S(1)}, u32[]{:S(2)}, u32[]{:S(2)}) collective-permute-start(bf16[192,768]{1,0:T(8,128)(2,1)} %collective-permute-done.10), channel_id=1, source_target_pairs={{0,1},{1,0},{2,3},{3,2},{4,5},{5,4},{6,7},{7,6},{8,9},{9,8},{10,11... | collective-permute-start | bytes 884744 | tf_op jit(solution)/shard_map/ppermute | solution.py:885
  52.4 33.1 %collective-permute-start.21 = (bf16[2,192,1024]{2,1,0:T(8,128)(2,1)}, bf16[2,192,1024]{2,1,0:T(8,128)(2,1)}, u32[]{:S(2)}, u32[]{:S(2)}) collective-permute-start(bf16[2,192,1024]{2,1,0:T(8,128)(2,1)} %get-tuple-element.58), channel_id=1, source_target_pairs={{0,2},{1,3},{2,0},{3,1},{4,6},{5,7},{6,4},{7,5},{8,10},{9,11},{10,... | collective-permute-start | bytes 2359304 | tf_op jit(solution)/shard_map/ppermute | solution.py:888
  57.1 9.2 %collective-permute-start.7 = (bf16[3,192,384]{2,1,0:T(8,128)(2,1)S(1)}, bf16[3,192,384]{2,1,0:T(8,128)(2,1)}, u32[]{:S(2)}, u32[]{:S(2)}) collective-permute-start(bf16[3,192,384]{2,1,0:T(8,128)(2,1)S(1)} %get-tuple-element.199.refs_7_), channel_id=1, source_target_pairs={{0,1},{1,0},{2,3},{3,2},{4,5},{5,4},{6,7},{7,6},{8,9},{9,8},{10,11... | collective-permute-start | bytes 1327112 | tf_op jit(solution)/shard_map/ppermute | solution.py:885
  57.2 28.3 %collective-permute-start.8 = (bf16[3,192,384]{2,1,0:T(8,128)(2,1)S(1)}, bf16[3,192,384]{2,1,0:T(8,128)(2,1)}, u32[]{:S(2)}, u32[]{:S(2)}) collective-permute-start(bf16[3,192,384]{2,1,0:T(8,128)(2,1)S(1)} %get-tuple-element.201.refs_9_), channel_id=1, source_target_pairs={{0,1},{1,0},{2,3},{3,2},{4,5},{5,4},{6,7},{7,6},{8,9},{9,8},{10,11... | collective-permute-start | bytes 1327112 | tf_op jit(solution)/shard_map/ppermute | solution.py:885
  62.3 37.2 %collective-permute-start.14 = (bf16[3,192,768]{2,1,0:T(8,128)(2,1)}, bf16[3,192,768]{2,1,0:T(8,128)(2,1)}, u32[]{:S(2)}, u32[]{:S(2)}) collective-permute-start(bf16[3,192,768]{2,1,0:T(8,128)(2,1)} %param.20), channel_id=1, source_target_pairs={{0,1},{1,0},{2,3},{3,2},{4,5},{5,4},{6,7},{7,6},{8,9},{9,8},{10,11... | collective-permute-start | bytes 2654216 | tf_op jit(solution)/shard_map/ppermute | solution.py:885
  66.2 37.8 %collective-permute-start.22 = (bf16[2,192,1024]{2,1,0:T(8,128)(2,1)}, bf16[2,192,1024]{2,1,0:T(8,128)(2,1)S(1)}, u32[]{:S(2)}, u32[]{:S(2)}) collective-permute-start(bf16[2,192,1024]{2,1,0:T(8,128)(2,1)} %get-tuple-element.58), channel_id=1, source_target_pairs={{0,1},{1,0},{2,3},{3,2},{4,5},{5,4},{6,7},{7,6},{8,9},{9,8},{10,11... | collective-permute-start | bytes 2359304 | tf_op jit(solution)/shard_map/ppermute | solution.py:885
  68.8 30.6 %collective-permute-start.15 = (bf16[3,192,768]{2,1,0:T(8,128)(2,1)}, bf16[3,192,768]{2,1,0:T(8,128)(2,1)S(1)}, u32[]{:S(2)}, u32[]{:S(2)}) collective-permute-start(bf16[3,192,768]{2,1,0:T(8,128)(2,1)} %collective-permute-done.13), channel_id=1, source_target_pairs={{0,1},{1,0},{2,3},{3,2},{4,5},{5,4},{6,7},{7,6},{8,9},{9,8},{10,11... | collective-permute-start | bytes 2654216 | tf_op jit(solution)/shard_map/ppermute | solution.py:885
  85.4 18.6 %collective-permute-start.23 = (bf16[2,192,1024]{2,1,0:T(8,128)(2,1)}, bf16[2,192,1024]{2,1,0:T(8,128)(2,1)S(1)}, u32[]{:S(2)}, u32[]{:S(2)}) collective-permute-start(bf16[2,192,1024]{2,1,0:T(8,128)(2,1)} %collective-permute-done.21), channel_id=1, source_target_pairs={{0,1},{1,0},{2,3},{3,2},{4,5},{5,4},{6,7},{7,6},{8,9},{9,8},{10,11... | collective-permute-start | bytes 2359304 | tf_op jit(solution)/shard_map/ppermute | solution.py:885
  98.9 7.8 %collective-permute-start.9 = (bf16[384,1024]{1,0:T(8,128)(2,1)S(1)}, bf16[384,1024]{1,0:T(8,128)(2,1)S(1)}, u32[]{:S(2)}, u32[]{:S(2)}) collective-permute-start(bf16[384,1024]{1,0:T(8,128)(2,1)S(1)} %get-tuple-element.56.refs_6_), channel_id=1, source_target_pairs={{0,1},{1,0},{2,3},{3,2},{4,5},{5,4},{6,7},{7,6},{8,9},{9,8},{10,11... | collective-permute-start | bytes 2359304 | tf_op jit(solution)/shard_map/ppermute | solution.py:885
  121.5 4.1 collective-permute-start.19
  135.6 20.7 %collective-permute-start.24 = (bf16[384,1024]{1,0:T(8,128)(2,1)S(1)}, bf16[384,1024]{1,0:T(8,128)(2,1)}, u32[]{:S(2)}, u32[]{:S(2)}) collective-permute-start(bf16[384,1024]{1,0:T(8,128)(2,1)S(1)} %constant_dynamic-slice_fusion.8), channel_id=1, source_target_pairs={{0,2},{1,3},{2,0},{3,1},{4,6},{5,7},{6,4},{7,5},{8,10},{9,11},{10,... | collective-permute-start | bytes 2359304 | tf_op jit(solution)/shard_map/ppermute | solution.py:888
  145.4 14.0 %collective-permute-start.20 = (bf16[2,192,1024]{2,1,0:T(8,128)(2,1)S(1)}, bf16[2,192,1024]{2,1,0:T(8,128)(2,1)S(1)}, u32[]{:S(2)}, u32[]{:S(2)}) collective-permute-start(bf16[2,192,1024]{2,1,0:T(8,128)(2,1)S(1)} %fusion.97), channel_id=1, source_target_pairs={{0,1},{1,0},{2,3},{3,2},{4,5},{5,4},{6,7},{7,6},{8,9},{9,8},{10,11... | collective-permute-start | bytes 2359304 | tf_op jit(solution)/shard_map/ppermute | solution.py:885
  153.2 51.3 %collective-permute-start.30 = (bf16[2,192,1024]{2,1,0:T(8,128)(2,1)S(1)}, bf16[2,192,1024]{2,1,0:T(8,128)(2,1)S(1)}, u32[]{:S(2)}, u32[]{:S(2)}) collective-permute-start(bf16[2,192,1024]{2,1,0:T(8,128)(2,1)S(1)} %fusion.95), channel_id=1, source_target_pairs={{0,1},{1,0},{2,3},{3,2},{4,5},{5,4},{6,7},{7,6},{8,9},{9,8},{10,11... | collective-permute-start | bytes 2359304 | tf_op jit(solution)/shard_map/ppermute | solution.py:885
  156.3 3.6 collective-permute-start.25
  172.3 16.6 %collective-permute-start.28 = (bf16[2,192,1024]{2,1,0:T(8,128)(2,1)S(1)}, bf16[2,192,1024]{2,1,0:T(8,128)(2,1)S(1)}, u32[]{:S(2)}, u32[]{:S(2)}) collective-permute-start(bf16[2,192,1024]{2,1,0:T(8,128)(2,1)S(1)} %fusion.98), channel_id=1, source_target_pairs={{0,1},{1,0},{2,3},{3,2},{4,5},{5,4},{6,7},{7,6},{8,9},{9,8},{10,11... | collective-permute-start | bytes 2359304 | tf_op jit(solution)/shard_map/ppermute | solution.py:885
  178.4 6.0 %collective-permute-start.26 = (bf16[2,192,1024]{2,1,0:T(8,128)(2,1)S(1)}, bf16[2,192,1024]{2,1,0:T(8,128)(2,1)S(1)}, u32[]{:S(2)}, u32[]{:S(2)}) collective-permute-start(bf16[2,192,1024]{2,1,0:T(8,128)(2,1)S(1)} %fusion.96), channel_id=1, source_target_pairs={{0,1},{1,0},{2,3},{3,2},{4,5},{5,4},{6,7},{7,6},{8,9},{9,8},{10,11... | collective-permute-start | bytes 2359304 | tf_op jit(solution)/shard_map/ppermute | solution.py:885
  184.8 19.7 %collective-permute-start.27 = (bf16[2,192,1024]{2,1,0:T(8,128)(2,1)S(1)}, bf16[2,192,1024]{2,1,0:T(8,128)(2,1)S(1)}, u32[]{:S(2)}, u32[]{:S(2)}) collective-permute-start(bf16[2,192,1024]{2,1,0:T(8,128)(2,1)S(1)} %fusion.60), channel_id=1, source_target_pairs={{0,2},{1,3},{2,0},{3,1},{4,6},{5,7},{6,4},{7,5},{8,10},{9,11},{10,... | collective-permute-start | bytes 2359304 | tf_op jit(solution)/shard_map/ppermute | solution.py:888
  204.9 6.1 %collective-permute-start.31 = (bf16[2,192,1024]{2,1,0:T(8,128)(2,1)S(1)}, bf16[2,192,1024]{2,1,0:T(8,128)(2,1)S(1)}, u32[]{:S(2)}, u32[]{:S(2)}) collective-permute-start(bf16[2,192,1024]{2,1,0:T(8,128)(2,1)S(1)} %get-tuple-element.155), channel_id=1, source_target_pairs={{0,1},{1,0},{2,3},{3,2},{4,5},{5,4},{6,7},{7,6},{8,9},{9,8},{10,11... | collective-permute-start | bytes 2359304 | tf_op jit(solution)/shard_map/ppermute | solution.py:885
  208.3 40.8 %collective-permute-start.47 = (bf16[3,4,96,768]{3,2,0,1:T(8,128)(2,1)}, bf16[3,4,96,768]{3,2,0,1:T(8,128)(2,1)}, u32[]{:S(2)}, u32[]{:S(2)}) collective-permute-start(bf16[3,4,96,768]{3,2,0,1:T(8,128)(2,1)} %bitcast.481), channel_id=1, source_target_pairs={{0,4},{4,0},{8,12},{12,8},{16,20},{20,16},{24,28},{28,24},{1,5},{5... | collective-permute-start | bytes 5308424 | tf_op jit(solution)/shard_map/ppermute | solution.py:1023
  209.9 88.0 %collective-permute-start.29 = (bf16[2,192,1024]{2,1,0:T(8,128)(2,1)}, bf16[2,192,1024]{2,1,0:T(8,128)(2,1)}, u32[]{:S(2)}, u32[]{:S(2)}) collective-permute-start(bf16[2,192,1024]{2,1,0:T(8,128)(2,1)} %pad_maximum_fusion.16), channel_id=1, source_target_pairs={{0,2},{1,3},{2,0},{3,1},{4,6},{5,7},{6,4},{7,5},{8,10},{9,11},{10,... | collective-permute-start | bytes 2359304 | tf_op jit(solution)/shard_map/ppermute | solution.py:888
  225.5 29.5 %collective-permute-start.32 = (bf16[384,512]{1,0:T(8,128)(2,1)S(1)}, bf16[384,512]{1,0:T(8,128)(2,1)S(1)}, u32[]{:S(2)}, u32[]{:S(2)}) collective-permute-start(bf16[384,512]{1,0:T(8,128)(2,1)S(1)} %get-tuple-element.63), channel_id=1, source_target_pairs={{0,1},{1,0},{2,3},{3,2},{4,5},{5,4},{6,7},{7,6},{8,9},{9,8},{10,11... | collective-permute-start | bytes 1179656 | tf_op jit(solution)/shard_map/ppermute | solution.py:885
  251.3 4.0 collective-permute-start.33
  252.6 131.5 %collective-permute-start.50 = (bf16[3,96,768]{2,1,0:T(8,128)(2,1)}, bf16[3,96,768]{2,1,0:T(8,128)(2,1)}, u32[]{:S(2)}, u32[]{:S(2)}) collective-permute-start(bf16[3,96,768]{2,1,0:T(8,128)(2,1)} %get-tuple-element.174), channel_id=1, source_target_pairs={{0,8},{4,12},{8,16},{12,20},{16,24},{20,28},{24,0},{28,4},{1,9},{5... | collective-permute-start | bytes 1327112 | tf_op jit(solution)/shard_map/ppermute | solution.py:1032
  280.4 7.3 %collective-permute-start.36 = (bf16[384,1024]{1,0:T(8,128)(2,1)S(1)}, bf16[384,1024]{1,0:T(8,128)(2,1)S(1)}, u32[]{:S(2)}, u32[]{:S(2)}) collective-permute-start(bf16[384,1024]{1,0:T(8,128)(2,1)S(1)} %get-tuple-element.67.refs_0_), channel_id=1, source_target_pairs={{0,1},{1,0},{2,3},{3,2},{4,5},{5,4},{6,7},{7,6},{8,9},{9,8},{10,11... | collective-permute-start | bytes 2359304 | tf_op jit(solution)/shard_map/ppermute | solution.py:885
  280.8 9.2 %collective-permute-start.37 = (bf16[384,1024]{1,0:T(8,128)(2,1)S(1)}, bf16[384,1024]{1,0:T(8,128)(2,1)S(1)}, u32[]{:S(2)}, u32[]{:S(2)}) collective-permute-start(bf16[384,1024]{1,0:T(8,128)(2,1)S(1)} %get-tuple-element.68.refs_1_), channel_id=1, source_target_pairs={{0,1},{1,0},{2,3},{3,2},{4,5},{5,4},{6,7},{7,6},{8,9},{9,8},{10,11... | collective-permute-start | bytes 2359304 | tf_op jit(solution)/shard_map/ppermute | solution.py:885
  281.0 10.1 %collective-permute-start.38 = (bf16[384,1024]{1,0:T(8,128)(2,1)S(1)}, bf16[384,1024]{1,0:T(8,128)(2,1)S(1)}, u32[]{:S(2)}, u32[]{:S(2)}) collective-permute-start(bf16[384,1024]{1,0:T(8,128)(2,1)S(1)} %get-tuple-element.69.refs_2_), channel_id=1, source_target_pairs={{0,1},{1,0},{2,3},{3,2},{4,5},{5,4},{6,7},{7,6},{8,9},{9,8},{10,11... | collective-permute-start | bytes 2359304 | tf_op jit(solution)/shard_map/ppermute | solution.py:885
  287.7 99.2 %collective-permute-start.49 = (bf16[3,96,768]{2,1,0:T(8,128)(2,1)}, bf16[3,96,768]{2,1,0:T(8,128)(2,1)}, u32[]{:S(2)}, u32[]{:S(2)}) collective-permute-start(bf16[3,96,768]{2,1,0:T(8,128)(2,1)} %get-tuple-element.175), channel_id=1, source_target_pairs={{0,24},{4,28},{8,0},{12,4},{16,8},{20,12},{24,16},{28,20},{1,25},{... | collective-permute-start | bytes 1327112 | tf_op jit(solution)/shard_map/ppermute | solution.py:1032
  290.0 8.0 %collective-permute-start.34 = (bf16[128,768]{1,0:T(8,128)(2,1)S(1)}, bf16[128,768]{1,0:T(8,128)(2,1)S(1)}, u32[]{:S(2)}, u32[]{:S(2)}) collective-permute-start(bf16[128,768]{1,0:T(8,128)(2,1)S(1)} %fusion.90), channel_id=1, source_target_pairs={{0,2},{1,3},{2,0},{3,1},{4,6},{5,7},{6,4},{7,5},{8,10},{9,11},{10,... | collective-permute-start | bytes 589832 | tf_op jit(solution)/shard_map/ppermute | solution.py:888
  291.1 32.1 %collective-permute-start.42 = (bf16[2,768,384]{2,1,0:T(8,128)(2,1)}, bf16[2,768,384]{2,1,0:T(8,128)(2,1)}, u32[]{:S(2)}, u32[]{:S(2)}) collective-permute-start(bf16[2,768,384]{2,1,0:T(8,128)(2,1)} %get-tuple-element.78), channel_id=1, source_target_pairs={{0,2},{1,3},{2,0},{3,1},{4,6},{5,7},{6,4},{7,5},{8,10},{9,11},{10,... | collective-permute-start | bytes 3538952 | tf_op jit(solution)/shard_map/ppermute | solution.py:888
  297.9 11.4 %collective-permute-start.39 = (f32[1,1024]{1,0:T(1,128)S(1)}, f32[1,1024]{1,0:T(1,128)}, u32[]{:S(2)}, u32[]{:S(2)}) collective-permute-start(f32[1,1024]{1,0:T(1,128)S(1)} %bitcast.526), channel_id=1, source_target_pairs={{0,1},{1,0},{2,3},{3,2},{4,5},{5,4},{6,7},{7,6},{8,9},{9,8},{10,11... | collective-permute-start | bytes 12296 | tf_op jit(solution)/shard_map/ppermute | solution.py:885
  308.3 91.5 %collective-permute-start.41 = (bf16[2,2,384,384]{3,2,1,0:T(8,128)(2,1)}, bf16[2,2,384,384]{3,2,1,0:T(8,128)(2,1)}, u32[]{:S(2)}, u32[]{:S(2)}) collective-permute-start(bf16[2,2,384,384]{3,2,1,0:T(8,128)(2,1)} %copy-done.30), channel_id=1, source_target_pairs={{0,2},{1,3},{2,0},{3,1},{4,6},{5,7},{6,4},{7,5},{8,10},{9,11},{10,... | collective-permute-start | bytes 3538952 | tf_op jit(solution)/shard_map/ppermute | solution.py:888
  312.2 43.7 %collective-permute-start.40 = (bf16[192,1024]{1,0:T(8,128)(2,1)S(1)}, bf16[192,1024]{1,0:T(8,128)(2,1)S(1)}, u32[]{:S(2)}, u32[]{:S(2)}) collective-permute-start(bf16[192,1024]{1,0:T(8,128)(2,1)S(1)} %get-tuple-element.202), channel_id=1, source_target_pairs={{0,2},{1,3},{2,0},{3,1},{4,6},{5,7},{6,4},{7,5},{8,10},{9,11},{10,... | collective-permute-start | bytes 1179656 | tf_op jit(solution)/shard_map/ppermute | solution.py:888
  326.8 54.7 %collective-permute-start.43 = (bf16[2,4,96,384]{3,2,0,1:T(8,128)(2,1)}, bf16[2,4,96,384]{3,2,0,1:T(8,128)(2,1)}, u32[]{:S(2)}, u32[]{:S(2)}) collective-permute-start(bf16[2,4,96,384]{3,2,0,1:T(8,128)(2,1)} %bitcast.482), channel_id=1, source_target_pairs={{0,4},{4,0},{8,12},{12,8},{16,20},{20,16},{24,28},{28,24},{1,5},{5... | collective-permute-start | bytes 1769480 | tf_op jit(solution)/shard_map/ppermute | solution.py:1023
  355.8 31.7 %collective-permute-start.48 = (bf16[3,96,768]{2,1,0:T(8,128)(2,1)}, bf16[3,96,768]{2,1,0:T(8,128)(2,1)}, u32[]{:S(2)}, u32[]{:S(2)}) collective-permute-start(bf16[3,96,768]{2,1,0:T(8,128)(2,1)} %get-tuple-element.176), channel_id=1, source_target_pairs={{0,16},{4,20},{8,24},{12,28},{16,0},{20,4},{24,8},{28,12},{1,17},{... | collective-permute-start | bytes 1327112 | tf_op jit(solution)/shard_map/ppermute | solution.py:1032
  383.0 8.6 %collective-permute-start.46 = (bf16[2,96,384]{2,1,0:T(8,128)(2,1)S(1)}, bf16[2,96,384]{2,1,0:T(8,128)(2,1)S(1)}, u32[]{:S(2)}, u32[]{:S(2)}) collective-permute-start(bf16[2,96,384]{2,1,0:T(8,128)(2,1)S(1)} %get-tuple-element.214), channel_id=1, source_target_pairs={{0,8},{4,12},{8,16},{12,20},{16,24},{20,28},{24,0},{28,4},{1,9},{5... | collective-permute-start | bytes 442376 | tf_op jit(solution)/shard_map/ppermute | solution.py:1032
  384.2 8.6 %collective-permute-start.45 = (bf16[2,96,384]{2,1,0:T(8,128)(2,1)S(1)}, bf16[2,96,384]{2,1,0:T(8,128)(2,1)S(1)}, u32[]{:S(2)}, u32[]{:S(2)}) collective-permute-start(bf16[2,96,384]{2,1,0:T(8,128)(2,1)S(1)} %get-tuple-element.215), channel_id=1, source_target_pairs={{0,24},{4,28},{8,0},{12,4},{16,8},{20,12},{24,16},{28,20},{1,25},{... | collective-permute-start | bytes 442376 | tf_op jit(solution)/shard_map/ppermute | solution.py:1032
  386.9 12.9 %collective-permute-start.44 = (bf16[2,96,384]{2,1,0:T(8,128)(2,1)S(1)}, bf16[2,96,384]{2,1,0:T(8,128)(2,1)S(1)}, u32[]{:S(2)}, u32[]{:S(2)}) collective-permute-start(bf16[2,96,384]{2,1,0:T(8,128)(2,1)S(1)} %get-tuple-element.216), channel_id=1, source_target_pairs={{0,16},{4,20},{8,24},{12,28},{16,0},{20,4},{24,8},{28,12},{1,17},{... | collective-permute-start | bytes 442376 | tf_op jit(solution)/shard_map/ppermute | solution.py:1032
  (122 other events, 854.8 us)
